TPU v7x, 512 devices: a 4x2x32 block of a 4x8x32 slice. The times are simulated.
512 devices in a mesh: parts: 2 (over y), slab: 32 (over z), orb: 4 (over x), pen: 2 (over core).
Axes of the slice: x: 4, y: 2, z: 32, core: 2. Of those that a mesh axis runs over, the one named last changes fastest.
The devices are a block of a 4x8x32 slice.
Arguments:
- orbitals: float32 [128, 128, 8, 256], P(('parts', 'orb'), 'slab', 'pen'), parts along dimension 0, may hold values from -7.6 to 7.6
- energies: float32 [128], P(('parts', 'orb')), parts along dimension 0, may hold values from -1 to 0.5
- frequency: float32 [2], P('parts'), parts along dimension 0, may hold values from 0.5 to 2
- local_potential: float32 [128, 8, 256], P('slab', 'pen'), may hold values from -1 to 1
- perturbation: float32 [128, 8, 256], P('slab', 'pen'), may hold values from 0.5 to 1.5
- projectors: float32 [128, 8, 256], P(None, 'pen'), may hold values from -0.0625 to 0.0625
- profiles: float32 [128, 5], replicated, may hold values from 0.5 to 2
- couplings: float32 [128], replicated, may hold values from 4 to 12
- atom_planes: int32 [128], replicated, may hold values from 0 to 127
Outputs:
- response_real: float32 [128, 128, 8, 256], P(('parts', 'orb'), 'slab', 'pen'), parts along dimension 0
- density: float32 [256, 8, 256], P(('parts', 'slab'), 'pen'), parts along dimension 0
There are 2 independent parts, one for each index of `parts`. A program takes and returns all parts, laid end to end along the dimension named above; an argument that names none is the same for every part. Nothing has to cross between parts.
Inputs may be any that keep to these rules, and one draw needn't show every extreme that they name: Projector a covers the planes (atom_planes[a] + d) mod 128 of the first dimension for d < 5.
All inputs are finite; a program needn't handle non-finite values.
Results may differ from a plain program's by a relative error of at most 0.0003.
Values sent between devices are 32-bit elements; how exact they have to be, the bound alone decides.
No kernel may reach another device: no remote copies, remote signals or barrier semaphores. Data moves between devices by JAX's collectives and lax.ppermute only.
A program may use at most 64 MiB of HBM per device.

v0:
```python
import functools

import jax
import jax.numpy as jnp
from jax import lax
from jax.sharding import PartitionSpec as P

NOCC = 64
ITERS = 2


kinetic_scale = 0.125
highest = lax.Precision.HIGHEST


def by_axis(array, axes):
    return functools.reduce(lax.psum, axes, array)


def copy_for_each(array, axis):
    copies = jnp.broadcast_to(array, (lax.axis_size(axis), *array.shape))
    return lax.all_to_all(copies, axis, split_axis=0, concat_axis=0, tiled=True)


def laid_out(blocks, dim):
    dims = list(blocks.shape[1:])
    dims[dim] *= blocks.shape[0]
    return jnp.moveaxis(blocks, 0, dim).reshape(dims)


def collect(array, axis, dim):
    blocks = copy_for_each(array, axis)
    return laid_out(blocks, dim)


def with_halo(array, sides, width):
    edges = {}
    for axis, dim in sides:
        peers, length = (lax.axis_size(axis), array.shape[dim])
        up = [(i, (i + 1) % peers) for i in range(peers)]
        last = lax.slice_in_dim(array, length - width, length, axis=dim)
        leading = lax.slice_in_dim(array, 0, width, axis=dim)
        edges[dim] = (
            lax.ppermute(last, axis, up),
            lax.ppermute(leading, axis, [(b, a) for a, b in up]),
        )
    done = []
    for _, dim in sides:
        low, high = edges[dim]
        around = [(width, width) if d in done else (0, 0) for d in range(array.ndim)]
        array = jnp.concatenate([jnp.pad(low, around), array, jnp.pad(high, around)], axis=dim)
        done.append(dim)
    return array


def taken_together(array, axis):
    return copy_for_each(array, axis).sum(axis=0)


def plane_weights(atom_planes, profiles, planes, depth_total):
    span_size = profiles.shape[1]
    covered = (atom_planes[:, None] + jnp.arange(span_size, dtype=jnp.int32)[None, :]) % depth_total
    matches = (covered[:, :, None] == planes[None, None, :]).astype(jnp.float32)
    return jnp.sum(profiles[:, :, None] * matches, axis=1)


def coefficients(values, projectors, weights, couplings):
    orb_count, plane_count, row_count, col_count = values.shape
    flat_values = values.reshape(orb_count * plane_count, row_count * col_count)
    flat_beta = projectors.reshape(projectors.shape[0], row_count * col_count)
    inner_sums = lax.dot_general(
        flat_beta, flat_values, (((1,), (1,)), ((), ())), precision=highest
    )
    inner_sums = inner_sums.reshape(projectors.shape[0], orb_count, plane_count)
    partial_sum = jnp.einsum("aiz,az->ai", inner_sums, weights, precision=highest)
    summed = by_axis(partial_sum, ("slab", "pen"))
    return couplings[:, None] * summed


def apply_section(padded, potential, beta_out, weights_out, expansion, energies):
    centre = padded[:, 1:-1, 1:-1]
    beside_all = (
        padded[:, 2:, 1:-1] + padded[:, :-2, 1:-1] + padded[:, 1:-1, 2:] + padded[:, 1:-1, :-2]
    )
    beside_all = beside_all + jnp.roll(centre, 1, 3) + jnp.roll(centre, -1, 3)
    orb_count, plane_count, row_count, col_count = centre.shape
    spread = weights_out[:, None, :] * expansion[:, :, None]
    flat_spread = spread.reshape(spread.shape[0], orb_count * plane_count)
    flat_beta = beta_out.reshape(beta_out.shape[0], row_count * col_count)
    nonlocal_term = lax.dot_general(
        flat_spread, flat_beta, (((0,), (0,)), ((), ())), precision=highest
    )
    nonlocal_term = nonlocal_term.reshape(orb_count, plane_count, row_count, col_count)
    return (
        kinetic_scale * (6.0 * centre - beside_all)
        + potential[None] * centre
        + nonlocal_term
        - energies[:, None, None, None] * centre
    )


def on_device(
    orbitals,
    energies,
    frequency,
    local_potential,
    perturbation,
    projectors,
    profiles,
    couplings,
    atom_planes,
):
    orb_count, plane_count, row_count, col_count = orbitals.shape
    depth_total = plane_count * lax.axis_size("slab")
    cell_total = float(depth_total * row_count * lax.axis_size("pen") * col_count)
    first_plane = lax.axis_index("slab") * plane_count
    planes = (first_plane + jnp.arange(plane_count, dtype=jnp.int32)) % depth_total
    weights = plane_weights(atom_planes, profiles, planes, depth_total)
    freq_square = frequency[0] * frequency[0]
    everyone = collect(orbitals, "orb", 0)
    every_flat = everyone.reshape(everyone.shape[0], -1)

    def correlation_terms(values):
        return lax.dot_general(
            every_flat, values.reshape(orb_count, -1), (((1,), (1,)), ((), ())), precision=highest
        )

    def removed(values, totals, factor):
        expansion = jax.scipy.linalg.cho_solve((factor, True), totals / cell_total)
        removed_part = lax.dot_general(
            expansion, every_flat, (((0,), (0,)), ((), ())), precision=highest
        )
        return values - removed_part.reshape(values.shape)

    def squares(values):
        return by_axis(jnp.sum(values * values, axis=(1, 2, 3)), ("slab", "pen"))

    def apply_shallow(values):
        padded = with_halo(values, (("slab", 1), ("pen", 2)), 1)
        expansion = coefficients(values, projectors, weights, couplings)
        return apply_section(padded, local_potential, projectors, weights, expansion, energies)

    source = perturbation[None] * orbitals
    gram_part = lax.dot_general(every_flat, every_flat, (((1,), (1,)), ((), ())), precision=highest)
    gram_total, source_total = (
        by_axis(gram_part, ("slab", "pen")),
        by_axis(correlation_terms(source), ("slab", "pen")),
    )
    factor = jnp.linalg.cholesky(gram_total / cell_total)
    residual = -removed(source, source_total, factor)
    direction = residual
    solution = jnp.zeros_like(residual)
    norm_now = squares(residual)
    for iteration in range(ITERS):
        direction_total = taken_together(correlation_terms(direction), ("slab", "pen"))
        inner_field = removed(direction, direction_total, factor)
        first_half = apply_shallow(inner_field)
        second = apply_shallow(first_half)
        first_half, second = (first_half, second)
        target = second + freq_square * inner_field
        curve_part = jnp.sum(first_half * first_half, axis=(1, 2, 3)) + freq_square * jnp.sum(
            inner_field * inner_field, axis=(1, 2, 3)
        )
        image_total, curvature = (
            by_axis(correlation_terms(target), ("slab", "pen")),
            by_axis(curve_part, ("slab", "pen")),
        )
        image_field = removed(target, image_total, factor)
        step_size = norm_now / curvature
        solution = solution + step_size[:, None, None, None] * direction
        residual = residual - step_size[:, None, None, None] * image_field
        norm_next = squares(residual)
        direction = residual + (norm_next / norm_now)[:, None, None, None] * direction
        norm_now = norm_next
    padded = with_halo(solution, (("slab", 1), ("pen", 2)), 1)
    final_expansion = coefficients(solution, projectors, weights, couplings)
    response_real = apply_section(
        padded, local_potential, projectors, weights, final_expansion, energies
    )
    density = taken_together(jnp.sum(orbitals * response_real, axis=0), "orb") * (4.0 / NOCC)
    return (response_real, density)


def solution(mesh):
    in_specs = (
        P(("parts", "orb"), "slab", "pen", None),
        P(("parts", "orb")),
        P("parts"),
        P("slab", "pen", None),
        P("slab", "pen", None),
        P(None, "pen", None),
        P(),
        P(),
        P(),
    )
    out_specs = (P(("parts", "orb"), "slab", "pen", None), P(("parts", "slab"), "pen", None))
    return jax.shard_map(
        on_device, mesh=mesh, in_specs=in_specs, out_specs=out_specs, check_vma=False
    )
```

profile of v0, /device:TPU:40, one launch (start us, length us, event | category | flops | bytes accessed | tf_op | source)
XLA Modules:
  0.0 781.0 jit_solution(7663754433908618940)
XLA Ops:
  0.6 2.2 broadcast_in_dim.10
  2.8 4.7 all-to-all-start
  8.0 14.7 %all-to-all-done = f32[4,16,4,4,256]{4,3,2,1,0:T(4,128)S(1)} async-done(((f32[4,16,4,4,256]{4,3,2,1,0:T(4,128)}), f32[4,16,4,4,256]{4,3,2,1,0:T(4,128)S(1)}, u32[]{:S(2)}, u32[]{:S(2)}) %all-to-all-start) | async-done | bytes 1048608 | tf_op jit(solution)/shard_map/all_to_all | solution.py:22
  23.3 1.0 fusion.104
  24.2 0.9 convolution_bitcast_fusion.7
  25.1 147.4 %all-reduce.9 = (f32[64,64]{0,1:T(8,128)S(1)}, f32[64,16]{0,1:T(8,128)S(1)}) all-reduce(f32[64,64]{0,1:T(8,128)S(1)} %fusion.104, f32[64,16]{0,1:T(8,128)S(1)} %convolution_bitcast_fusion.7), channel_id=1, replica_groups=mesh['parts'=2,'slab'=32,'orb'=4,'pen'=2] {'slab'}, use_global_device_ids=true, to_apply=%region_0.1 | all-reduce | flops 5120 | bytes 40960 | tf_op jit(solution)/shard_map/psum | solution.py:17
  172.5 3.5 all-reduce.11
  176.1 5.8 cholesky.18
  183.3 4.9 custom-call.11
  189.3 1.3 multiply_reduce_fusion.5
  190.9 0.9 convolution_bitcast_fusion.5
  191.9 1.0 reshape.188
  192.9 7.1 all-to-all-start.1
  200.6 1.1 copy.129
  201.8 1.0 copy.76
  203.5 38.0 %all-to-all-done.1 = f32[64,1,1024]{2,1,0:T(1,128)S(1)} async-done(((f32[64,1,1024]{2,1,0:T(1,128)}), f32[64,1,1024]{2,1,0:T(1,128)S(1)}, u32[]{:S(2)}, u32[]{:S(2)}) %all-to-all-start.1) | async-done | bytes 262176 | tf_op jit(solution)/shard_map/all_to_all | solution.py:22
  242.0 2.0 reduce.14
  244.0 1.1 reshape.189
  245.5 1.3 multiply_reduce_fusion.3
  247.8 0.9 fusion.100
  248.7 1.9 collective-permute-start.2
  250.6 2.4 collective-permute-start.3
  253.1 2.6 collective-permute-start.1
  255.7 4.5 collective-permute-start
  261.0 53.9 %psum.160 = f32[128,16]{0,1:T(8,128)S(1)} all-reduce(f32[128,16]{0,1:T(8,128)S(1)} %multiply_reduce_fusion.9), channel_id=1, replica_groups=mesh['parts'=2,'slab'=32,'orb'=4,'pen'=2] {'slab'}, use_global_device_ids=true, to_apply=%region_11.13 | all-reduce | flops 2048 | bytes 16384 | tf_op jit(solution)/shard_map/psum | solution.py:17
  314.9 2.6 psum.161
  318.2 2.1 multiply_reduce_fusion.4
  323.4 3.9 collective-permute-start.5
  327.3 3.2 collective-permute-start.4
  330.5 2.0 collective-permute-start.6
  332.4 2.4 collective-permute-start.7
  335.7 54.7 %psum.164 = f32[128,16]{0,1:T(8,128)S(1)} all-reduce(f32[128,16]{0,1:T(8,128)S(1)} %multiply_reduce_fusion.8), channel_id=1, replica_groups=mesh['parts'=2,'slab'=32,'orb'=4,'pen'=2] {'slab'}, use_global_device_ids=true, to_apply=%region_17.19 | all-reduce | flops 2048 | bytes 16384 | tf_op jit(solution)/shard_map/psum | solution.py:17
  390.3 2.6 psum.165
  393.6 2.0 fusion.7
  396.7 0.9 convolution_bitcast_fusion.3
  397.6 56.0 %all-reduce.8 = (f32[64,16]{0,1:T(8,128)S(1)}, f32[16]{0:T(128)S(1)}, f32[16]{0:T(128)S(1)}) all-reduce(f32[64,16]{0,1:T(8,128)S(1)} %convolution_bitcast_fusion.3, f32[16]{0:T(128)S(1)} %get-tuple-element.37, f32[16]{0:T(128)S(1)} %multiply_add_fusion.3), channel_id=1, replica_groups=mesh['parts'=2,'slab'=32,'orb'=4,'pen'=2] {'slab'}, use_global_device_ids=true, to_apply=%region_19.21 | all-reduce | flops 1056 | bytes 8448 | tf_op jit(solution)/shard_map/psum | solution.py:17
  453.6 2.6 all-reduce.10
  456.5 1.3 multiply_reduce_fusion.2
  457.8 53.7 %psum.168 = f32[16]{0:T(128)S(1)} all-reduce(f32[16]{0:T(128)S(1)} %get-tuple-element.60), channel_id=1, replica_groups=mesh['parts'=2,'slab'=32,'orb'=4,'pen'=2] {'slab'}, use_global_device_ids=true, to_apply=%region_22.24 | all-reduce | flops 16 | bytes 128 | tf_op jit(solution)/shard_map/psum | solution.py:17
  511.5 2.5 psum.169
  514.1 0.9 copy.82
  515.0 1.1 reshape.166
  516.1 0.9 convolution_bitcast_fusion.1
  517.4 51.2 %all_to_all.20 = f32[64,1,1024]{2,1,0:T(1,128)S(1)} all-to-all(f32[64,1,1024]{2,1,0:T(1,128)S(1)} %reshape.190), channel_id=1, replica_groups=mesh['parts'=2,'slab'=32,'orb'=4,'pen'=2] {'slab','pen'}, dimensions={0} | all-to-all | bytes 524288 | tf_op jit(solution)/shard_map/all_to_all | solution.py:22
  568.5 1.3 reduce.15
  570.3 1.3 multiply_reduce_fusion.1
  572.1 2.6 collective-permute-start.9
  574.7 4.5 collective-permute-start.8
  579.2 2.0 collective-permute-start.10
  581.2 2.4 collective-permute-start.11
  584.4 53.9 %psum.170 = f32[128,16]{0,1:T(8,128)S(1)} all-reduce(f32[128,16]{0,1:T(8,128)S(1)} %multiply_reduce_fusion.7), channel_id=1, replica_groups=mesh['parts'=2,'slab'=32,'orb'=4,'pen'=2] {'slab'}, use_global_device_ids=true, to_apply=%region_25.27 | all-reduce | flops 2048 | bytes 16384 | tf_op jit(solution)/shard_map/psum | solution.py:17
  638.3 2.6 psum.171
  641.5 1.7 fusion.8
  643.3 54.8 %psum.172 = f32[16]{0:T(128)S(1)} all-reduce(f32[16]{0:T(128)S(1)} %multiply_add_fusion.2), channel_id=1, replica_groups=mesh['parts'=2,'slab'=32,'orb'=4,'pen'=2] {'slab'}, use_global_device_ids=true, to_apply=%region_29.31 | all-reduce | flops 16 | bytes 128 | tf_op jit(solution)/shard_map/psum | solution.py:17
  698.0 2.5 psum.173
  701.1 2.0 collective-permute-start.13
  703.1 5.1 collective-permute-start.12
  708.3 2.0 collective-permute-start.14
  710.2 2.4 collective-permute-start.15
  713.4 53.9 %psum.174 = f32[128,16]{0,1:T(8,128)S(1)} all-reduce(f32[128,16]{0,1:T(8,128)S(1)} %multiply_reduce_fusion.6), channel_id=1, replica_groups=mesh['parts'=2,'slab'=32,'orb'=4,'pen'=2] {'slab'}, use_global_device_ids=true, to_apply=%region_31.33 | all-reduce | flops 2048 | bytes 16384 | tf_op jit(solution)/shard_map/psum | solution.py:17
  767.3 2.6 psum.175
  771.4 3.4 all-to-all-start.3
  774.8 0.9 copy.89
  775.7 4.7 all-to-all-done.3
  (125 shorter events, 20.0 us)
Async XLA Ops:
  2.8 4.7 copy-start
  2.8 4.7 copy-start.5
  2.8 19.9 %all-to-all-start = ((f32[4,16,4,4,256]{4,3,2,1,0:T(4,128)}), f32[4,16,4,4,256]{4,3,2,1,0:T(4,128)S(1)}, u32[]{:S(2)}, u32[]{:S(2)}) async-start(f32[4,16,4,4,256]{4,3,2,1,0:T(4,128)} %broadcast_in_dim.10), calls=%async_computation | async-start | bytes 2097152 | tf_op jit(solution)/shard_map/all_to_all | solution.py:22
  192.9 48.7 %all-to-all-start.1 = ((f32[64,1,1024]{2,1,0:T(1,128)}), f32[64,1,1024]{2,1,0:T(1,128)S(1)}, u32[]{:S(2)}, u32[]{:S(2)}) async-start(f32[64,1,1024]{2,1,0:T(1,128)} %reshape.188), calls=%async_computation.1 | async-start | bytes 524288 | tf_op jit(solution)/shard_map/all_to_all | solution.py:22
  201.8 1.0 copy-start.8
  202.8 0.7 copy-start.7
  248.7 68.8 %collective-permute-start.2 = (f32[16,4,1,256]{3,0,2,1:T(8,128)S(1)}, f32[16,4,1,256]{3,0,2,1:T(8,128)S(1)}, u32[]{:S(2)}, u32[]{:S(2)}) collective-permute-start(f32[16,4,1,256]{3,0,2,1:T(8,128)S(1)} %get-tuple-element.51), channel_id=1, source_target_pairs={{1,0},{0,1},{3,2},{2,3},{5,4},{4,5},{7,6},{6,7},{9,8},{8,9},{11,10... | collective-permute-start | bytes 196616 | tf_op jit(solution)/shard_map/ppermute | solution.py:45
  250.6 66.8 %collective-permute-start.3 = (f32[16,4,1,256]{3,0,2,1:T(8,128)S(1)}, f32[16,4,1,256]{3,0,2,1:T(8,128)}, u32[]{:S(2)}, u32[]{:S(2)}) collective-permute-start(f32[16,4,1,256]{3,0,2,1:T(8,128)S(1)} %get-tuple-element.52), channel_id=1, source_target_pairs={{0,1},{1,0},{2,3},{3,2},{4,5},{5,4},{6,7},{7,6},{8,9},{9,8},{10,11... | collective-permute-start | bytes 196616 | tf_op jit(solution)/shard_map/ppermute | solution.py:44
  253.1 64.4 %collective-permute-start.1 = (f32[16,1,4,256]{3,0,2,1:T(8,128)S(1)}, f32[16,1,4,256]{3,0,2,1:T(8,128)}, u32[]{:S(2)}, u32[]{:S(2)}) collective-permute-start(f32[16,1,4,256]{3,0,2,1:T(8,128)S(1)} %get-tuple-element.53), channel_id=1, source_target_pairs={{0,8},{8,16},{16,24},{24,32},{32,40},{40,48},{48,56},{56,64},{64,7... | collective-permute-start | bytes 196616 | tf_op jit(solution)/shard_map/ppermute | solution.py:44
  255.7 61.8 %collective-permute-start = (f32[16,1,4,256]{3,0,2,1:T(8,128)S(1)}, f32[16,1,4,256]{3,0,2,1:T(8,128)}, u32[]{:S(2)}, u32[]{:S(2)}) collective-permute-start(f32[16,1,4,256]{3,0,2,1:T(8,128)S(1)} %get-tuple-element.54), channel_id=1, source_target_pairs={{8,0},{16,8},{24,16},{32,24},{40,32},{48,40},{56,48},{64,56},{72,6... | collective-permute-start | bytes 196616 | tf_op jit(solution)/shard_map/ppermute | solution.py:45
  314.8 2.6 copy-start.6
  317.4 0.7 copy-start.9
  317.5 0.7 copy-start.12
  323.4 69.5 %collective-permute-start.5 = (f32[16,1,4,256]{3,0,2,1:T(8,128)}, f32[16,1,4,256]{3,0,2,1:T(8,128)}, u32[]{:S(2)}, u32[]{:S(2)}) collective-permute-start(f32[16,1,4,256]{3,0,2,1:T(8,128)} %get-tuple-element.45), channel_id=1, source_target_pairs={{0,8},{8,16},{16,24},{24,32},{32,40},{40,48},{48,56},{56,64},{64,7... | collective-permute-start | bytes 196616 | tf_op jit(solution)/shard_map/ppermute | solution.py:44
  327.3 65.7 %collective-permute-start.4 = (f32[16,1,4,256]{3,0,2,1:T(8,128)}, f32[16,1,4,256]{3,0,2,1:T(8,128)}, u32[]{:S(2)}, u32[]{:S(2)}) collective-permute-start(f32[16,1,4,256]{3,0,2,1:T(8,128)} %get-tuple-element.46), channel_id=1, source_target_pairs={{8,0},{16,8},{24,16},{32,24},{40,32},{48,40},{56,48},{64,56},{72,6... | collective-permute-start | bytes 196616 | tf_op jit(solution)/shard_map/ppermute | solution.py:45
  330.5 62.4 %collective-permute-start.6 = (f32[16,4,1,256]{3,0,2,1:T(8,128)}, f32[16,4,1,256]{3,0,2,1:T(8,128)}, u32[]{:S(2)}, u32[]{:S(2)}) collective-permute-start(f32[16,4,1,256]{3,0,2,1:T(8,128)} %get-tuple-element.43), channel_id=1, source_target_pairs={{1,0},{0,1},{3,2},{2,3},{5,4},{4,5},{7,6},{6,7},{9,8},{8,9},{11,10... | collective-permute-start | bytes 196616 | tf_op jit(solution)/shard_map/ppermute | solution.py:45
  332.4 60.5 %collective-permute-start.7 = (f32[16,4,1,256]{3,0,2,1:T(8,128)S(1)}, f32[16,4,1,256]{3,0,2,1:T(8,128)}, u32[]{:S(2)}, u32[]{:S(2)}) collective-permute-start(f32[16,4,1,256]{3,0,2,1:T(8,128)S(1)} %get-tuple-element.44), channel_id=1, source_target_pairs={{0,1},{1,0},{2,3},{3,2},{4,5},{5,4},{6,7},{7,6},{8,9},{9,8},{10,11... | collective-permute-start | bytes 196616 | tf_op jit(solution)/shard_map/ppermute | solution.py:44
  392.9 0.7 copy-start.10
  395.6 0.7 copy-start.2
  396.7 59.8 %copy-start.3 = (f32[16,4,4,256]{3,0,2,1:T(8,128)S(1)}, f32[16,4,4,256]{3,0,2,1:T(8,128)}, u32[]{:S(2)}) copy-start(f32[16,4,4,256]{3,0,2,1:T(8,128)} %copy-done.2) | copy-start | bytes 786436
  572.1 68.8 %collective-permute-start.9 = (f32[16,1,4,256]{3,0,2,1:T(8,128)S(1)}, f32[16,1,4,256]{3,0,2,1:T(8,128)S(1)}, u32[]{:S(2)}, u32[]{:S(2)}) collective-permute-start(f32[16,1,4,256]{3,0,2,1:T(8,128)S(1)} %get-tuple-element.35), channel_id=1, source_target_pairs={{0,8},{8,16},{16,24},{24,32},{32,40},{40,48},{48,56},{56,64},{64,7... | collective-permute-start | bytes 196616 | tf_op jit(solution)/shard_map/ppermute | solution.py:44
  574.7 66.1 %collective-permute-start.8 = (f32[16,1,4,256]{3,0,2,1:T(8,128)S(1)}, f32[16,1,4,256]{3,0,2,1:T(8,128)}, u32[]{:S(2)}, u32[]{:S(2)}) collective-permute-start(f32[16,1,4,256]{3,0,2,1:T(8,128)S(1)} %get-tuple-element.36), channel_id=1, source_target_pairs={{8,0},{16,8},{24,16},{32,24},{40,32},{48,40},{56,48},{64,56},{72,6... | collective-permute-start | bytes 196616 | tf_op jit(solution)/shard_map/ppermute | solution.py:45
  579.2 61.6 %collective-permute-start.10 = (f32[16,4,1,256]{3,0,2,1:T(8,128)S(1)}, f32[16,4,1,256]{3,0,2,1:T(8,128)}, u32[]{:S(2)}, u32[]{:S(2)}) collective-permute-start(f32[16,4,1,256]{3,0,2,1:T(8,128)S(1)} %get-tuple-element.33), channel_id=1, source_target_pairs={{1,0},{0,1},{3,2},{2,3},{5,4},{4,5},{7,6},{6,7},{9,8},{8,9},{11,10... | collective-permute-start | bytes 196616 | tf_op jit(solution)/shard_map/ppermute | solution.py:45
  581.2 59.7 %collective-permute-start.11 = (f32[16,4,1,256]{3,0,2,1:T(8,128)S(1)}, f32[16,4,1,256]{3,0,2,1:T(8,128)}, u32[]{:S(2)}, u32[]{:S(2)}) collective-permute-start(f32[16,4,1,256]{3,0,2,1:T(8,128)S(1)} %get-tuple-element.34), channel_id=1, source_target_pairs={{0,1},{1,0},{2,3},{3,2},{4,5},{5,4},{6,7},{7,6},{8,9},{9,8},{10,11... | collective-permute-start | bytes 196616 | tf_op jit(solution)/shard_map/ppermute | solution.py:44
  583.7 57.2 %copy-start.4 = (f32[1024,128]{1,0:T(8,128)S(1)}, f32[1024,128]{1,0:T(8,128)}, u32[]{:S(2)}) copy-start(f32[1024,128]{1,0:T(8,128)} %copy.76) | copy-start | bytes 1572868
  640.8 0.7 copy-start.11
  701.1 68.7 %collective-permute-start.13 = (f32[16,1,4,256]{3,0,2,1:T(8,128)S(1)}, f32[16,1,4,256]{3,0,2,1:T(8,128)S(1)}, u32[]{:S(2)}, u32[]{:S(2)}) collective-permute-start(f32[16,1,4,256]{3,0,2,1:T(8,128)S(1)} %get-tuple-element.27), channel_id=1, source_target_pairs={{0,8},{8,16},{16,24},{24,32},{32,40},{40,48},{48,56},{56,64},{64,7... | collective-permute-start | bytes 196616 | tf_op jit(solution)/shard_map/ppermute | solution.py:44
  703.1 66.8 %collective-permute-start.12 = (f32[16,1,4,256]{3,0,2,1:T(8,128)S(1)}, f32[16,1,4,256]{3,0,2,1:T(8,128)S(1)}, u32[]{:S(2)}, u32[]{:S(2)}) collective-permute-start(f32[16,1,4,256]{3,0,2,1:T(8,128)S(1)} %get-tuple-element.28), channel_id=1, source_target_pairs={{8,0},{16,8},{24,16},{32,24},{40,32},{48,40},{56,48},{64,56},{72,6... | collective-permute-start | bytes 196616 | tf_op jit(solution)/shard_map/ppermute | solution.py:45
  708.3 61.6 %collective-permute-start.14 = (f32[16,4,1,256]{3,0,2,1:T(8,128)S(1)}, f32[16,4,1,256]{3,0,2,1:T(8,128)S(1)}, u32[]{:S(2)}, u32[]{:S(2)}) collective-permute-start(f32[16,4,1,256]{3,0,2,1:T(8,128)S(1)} %get-tuple-element.25), channel_id=1, source_target_pairs={{1,0},{0,1},{3,2},{2,3},{5,4},{4,5},{7,6},{6,7},{9,8},{8,9},{11,10... | collective-permute-start | bytes 196616 | tf_op jit(solution)/shard_map/ppermute | solution.py:45
  710.2 59.7 %collective-permute-start.15 = (f32[16,4,1,256]{3,0,2,1:T(8,128)S(1)}, f32[16,4,1,256]{3,0,2,1:T(8,128)S(1)}, u32[]{:S(2)}, u32[]{:S(2)}) collective-permute-start(f32[16,4,1,256]{3,0,2,1:T(8,128)S(1)} %get-tuple-element.26), channel_id=1, source_target_pairs={{0,1},{1,0},{2,3},{3,2},{4,5},{5,4},{6,7},{7,6},{8,9},{9,8},{10,11... | collective-permute-start | bytes 196616 | tf_op jit(solution)/shard_map/ppermute | solution.py:44
  712.7 57.2 %copy-start.1 = (f32[16,4,4,256]{3,2,1,0:T(4,128)S(1)}, f32[16,4,4,256]{3,2,1,0:T(4,128)}, u32[]{:S(2)}) copy-start(f32[16,4,4,256]{3,2,1,0:T(4,128)} %param.11) | copy-start | bytes 786436
  771.4 8.9 %all-to-all-start.3 = ((f32[4,4,4,256]{3,2,1,0:T(4,128)}), f32[4,4,4,256]{3,2,1,0:T(4,128)S(1)}, u32[]{:S(2)}, u32[]{:S(2)}) async-start(f32[4,4,4,256]{3,2,1,0:T(4,128)} %broadcast_in_dim.13), calls=%async_computation.3 | async-start | bytes 131072 | tf_op jit(solution)/shard_map/all_to_all | solution.py:22
where the time goes:
time: 783 us; the launch traced here: 781 us
  blocking collectives  601 us (77%)
  starting transfers between devices  61.1 us (8%)
  waiting for transfers between devices  57.4 us (7%)
  local copies, waits for them, and re-layouts  22.5 us (3%)
  matrix products  20.4 us (3%)
  other arithmetic  16.8 us (2%)
    psum x16, blocking collectives, by_axis(): return functools.reduce(lax.psum, axes, array)  549 us
    all_to_all x3, waiting for transfers between devices, copy_for_each(): return lax.all_to_all(copies, axis, split_axis=0, concat_axis=0, tiled=True)  57.3 us
    all_to_all x1, blocking collectives, copy_for_each(): return lax.all_to_all(copies, axis, split_axis=0, concat_axis=0, tiled=True)  51.2 us
    ppermute x8, starting transfers between devices, with_halo(): lax.ppermute(leading, axis, [(b, a) for a, b in up])  25.1 us
    ppermute x8, starting transfers between devices, with_halo(): lax.ppermute(last, axis, up)  20.9 us
  transfers between devices with their start and end apart: 19, of which 3 were waited for; matrix products, arithmetic and copies ran while one was open for 1% of the time, Pallas kernels for 0%

commit v1 on v0

v1 whole, which is shorter than its diff:
```python
import functools

import jax
import jax.numpy as jnp
from jax import lax
from jax.experimental import pallas as pl
from jax.experimental.pallas import tpu as pltpu
from jax.sharding import PartitionSpec as P

NOCC = 64
NEAR = 4

kinetic_scale = 0.125
highest = lax.Precision.HIGHEST
f32 = jnp.float32
VMEM = pl.BlockSpec(memory_space=pltpu.VMEM)
SMEM = pl.BlockSpec(memory_space=pltpu.SMEM)


def dot_nn(a, b):
    return lax.dot_general(a, b, (((1,), (0,)), ((), ())), precision=highest, preferred_element_type=f32)


def dot_nt(a, b):
    return lax.dot_general(a, b, (((1,), (1,)), ((), ())), precision=highest, preferred_element_type=f32)


def call(body, args, kinds, outs, scratch=()):
    return pl.pallas_call(
        body,
        in_specs=[SMEM if k == "s" else VMEM for k in kinds],
        out_specs=[VMEM] * len(outs),
        out_shape=[jax.ShapeDtypeStruct(s, f32) for s in outs],
        scratch_shapes=list(scratch),
    )(*args)


def orbital_row_sums(products, own):
    total = functools.reduce(jnp.add, products)
    folded = functools.reduce(jnp.add, [total[i : i + own] for i in range(0, total.shape[0], own)])
    return jnp.sum(folded, axis=1, keepdims=True)


def lane_blocks(ref, cols):
    return [ref[:, i : i + cols] for i in range(0, ref.shape[1], cols)]


def inner_partials(v_ref, stat_refs, w_ref, own, natoms):
    half = stat_refs[0].shape[1]
    sums = sum(
        dot_nt(v_ref[:, h * half : (h + 1) * half], stat_refs[h][0:natoms, :]) for h in range(2)
    )
    planes = w_ref.shape[0]
    return sum(sums[z * own : (z + 1) * own] * w_ref[z : z + 1, :] for z in range(planes))


def pack_edges(v_ref, pc, up_ref, down_ref, own):
    width = v_ref.shape[1]
    up_ref[:, 0:width] = v_ref[v_ref.shape[0] - own :, :]
    up_ref[:, width:] = pc
    down_ref[:, 0:width] = v_ref[0:own, :]
    down_ref[:, width:] = pc


def apply_shift(emit, v_ref, pc_ref, lo_ref, hi_ref, stat_refs, w_ref, coup_ref, en_ref, cols):
    own = lo_ref.shape[0]
    planes = w_ref.shape[0]
    natoms = w_ref.shape[1]
    width = v_ref.shape[1]
    half = width // 2
    c = coup_ref[...] * (pc_ref[...] + lo_ref[:, width:] + hi_ref[:, width:])
    spread = jnp.concatenate([c * w_ref[z : z + 1, :] for z in range(planes)], axis=0)
    shift = jnp.concatenate([6.0 * kinetic_scale - en_ref[...]] * planes, axis=0)
    blocks = width // cols
    for k in range(blocks):
        at = slice(k * cols, (k + 1) * cols)
        stat = stat_refs[k * cols // half]
        inside = (k * cols) % half
        nonlocal_term = dot_nn(spread, stat[0:natoms, inside : inside + cols])
        v = v_ref[:, at]
        after, before = (k + 1) % blocks, (k - 1) % blocks
        beside = v_ref[:, after * cols : (after + 1) * cols] + v_ref[:, before * cols : (before + 1) * cols]
        beside = beside + jnp.concatenate([lo_ref[:, at], v_ref[0 : own * (planes - 1), at]], axis=0)
        beside = beside + jnp.concatenate([v_ref[own:, at], hi_ref[:, at]], axis=0)
        beside = beside + pltpu.roll(v, 1, 1) + pltpu.roll(v, cols - 1, 1)
        local = jnp.concatenate(
            [
                jnp.broadcast_to(stat[natoms + z : natoms + z + 1, inside : inside + cols], (own, cols))
                for z in range(planes)
            ],
            axis=0,
        )
        emit(at, (local + shift) * v - kinetic_scale * beside + nonlocal_term)


def gram_body(where_ref, mine_ref, other_ref, stat_m, stat_o, out_ref, *, own, planes, natoms):
    half = stat_m.shape[1]
    total = mine_ref.shape[0]
    span = total // 2
    rows = pl.ds(pl.multiple_of(where_ref[1] * span, span), span)
    start = pl.multiple_of(where_ref[0], own)
    gram = dot_nt(mine_ref[rows, :], mine_ref[...]) + dot_nt(other_ref[rows, :], other_ref[...])
    corr = jnp.zeros((own, total), f32)
    for orb_ref, stat in ((mine_ref, stat_m), (other_ref, stat_o)):
        for z in range(planes):
            at = slice(z * half, (z + 1) * half)
            source = stat[natoms + planes + z : natoms + planes + z + 1, :] * orb_ref[pl.ds(start, own), at]
            corr = corr + dot_nt(source, orb_ref[:, at])
    quarter = span // 2
    out_ref[0:quarter, :] = jnp.concatenate([gram[0:quarter], gram[quarter:]], axis=1)
    out_ref[quarter:, :] = jnp.concatenate([corr, jnp.zeros((own, total), f32)], axis=1)


def inverse_of(gram):
    n = gram.shape[0]
    eye = (lax.broadcasted_iota(jnp.int32, (n, n), 0) == lax.broadcasted_iota(jnp.int32, (n, n), 1)).astype(f32)
    work = jnp.concatenate([gram, eye], axis=1)
    tiles = [work[i : i + 8] for i in range(0, n, 8)]
    sub = lax.broadcasted_iota(jnp.int32, (8, 2 * n), 0)
    for k in range(n):
        t, r = divmod(k, 8)
        row = tiles[t][r : r + 1, :]
        scaled = row * (1.0 / row[:, k : k + 1])
        scale = lax.rsqrt(row[:, k : k + 1])
        for i in range(t, n // 8):
            step = tiles[i] - tiles[i][:, k : k + 1] * scaled
            if i == t:
                step = jnp.where(sub > r, step, jnp.where(sub == r, tiles[i] * scale, tiles[i]))
            tiles[i] = step
    lower_inverse = jnp.concatenate(tiles, axis=0)[:, n:]
    inv = lax.dot_general(
        lower_inverse, lower_inverse, (((0,), (0,)), ((), ())), precision=highest, preferred_element_type=f32
    )
    return 2.0 * inv - dot_nn(dot_nn(inv, gram), inv)


def source_body(
    where_ref, sums_ref, swapped_ref, mine_ref, other_ref, stat_m, stat_o, w_ref,
    r_ref, up_ref, down_ref, pc_ref, inv_ref, *, own, planes, natoms, cells,
):
    half = stat_m.shape[1]
    total = mine_ref.shape[0]
    quarter = total // 4
    ours, theirs = sums_ref[0:quarter, :], swapped_ref[...]
    first = where_ref[1] == 0
    low, high = jnp.where(first, ours, theirs), jnp.where(first, theirs, ours)
    gram = jnp.concatenate([low[:, :total], low[:, total:], high[:, :total], high[:, total:]], axis=0) / cells
    inv = inverse_of(gram)
    inv_ref[...] = inv
    g = dot_nn(sums_ref[quarter:, 0:total] / cells, inv)
    start = pl.multiple_of(where_ref[0], own)
    for h, (orb_ref, stat) in enumerate(((mine_ref, stat_m), (other_ref, stat_o))):
        for z in range(planes):
            at = slice(z * half, (z + 1) * half)
            source = stat[natoms + planes + z : natoms + planes + z + 1, :] * orb_ref[pl.ds(start, own), at]
            r_ref[z * own : (z + 1) * own, h * half : (h + 1) * half] = dot_nn(g, orb_ref[:, at]) - source
    pc = inner_partials(r_ref, (stat_m, stat_o), w_ref, own, natoms)
    pc_ref[...] = pc
    pack_edges(r_ref, pc, up_ref, down_ref, own)


def first_body(
    v_ref, pc_ref, lo_ref, hi_ref, stat_m, stat_o, w_ref, coup_ref, en_ref,
    f_ref, up_ref, down_ref, out_pc_ref, *, own, natoms, cols,
):
    def emit(at, block):
        f_ref[:, at] = block

    apply_shift(emit, v_ref, pc_ref, lo_ref, hi_ref, (stat_m, stat_o), w_ref, coup_ref, en_ref, cols)
    pc = inner_partials(f_ref, (stat_m, stat_o), w_ref, own, natoms)
    out_pc_ref[...] = pc
    pack_edges(f_ref, pc, up_ref, down_ref, own)


def target_body(
    freq_ref, v_ref, pc_ref, lo_ref, hi_ref, stat_m, stat_o, w_ref, coup_ref, en_ref, r_ref, mine_ref, other_ref,
    t_ref, out_ref, *, own, planes, cols,
):
    square = freq_ref[0] * freq_ref[0]

    def emit(at, block):
        t_ref[:, at] = block + square * r_ref[:, at]

    apply_shift(emit, v_ref, pc_ref, lo_ref, hi_ref, (stat_m, stat_o), w_ref, coup_ref, en_ref, cols)
    half = stat_m.shape[1]
    total = mine_ref.shape[0]
    corr = jnp.zeros((own, total), f32)
    for h, orb_ref in enumerate((mine_ref, other_ref)):
        for z in range(planes):
            block = t_ref[z * own : (z + 1) * own, h * half : (h + 1) * half]
            corr = corr + dot_nt(block, orb_ref[:, z * half : (z + 1) * half])
    rr = orbital_row_sums([b * b for b in lane_blocks(r_ref, cols)], own)
    ff = orbital_row_sums([b * b for b in lane_blocks(v_ref, cols)], own)
    lanes = out_ref.shape[1]
    lane = lax.broadcasted_iota(jnp.int32, (own, lanes), 1)
    spread = jnp.concatenate([corr, jnp.zeros((own, lanes - total), f32)], axis=1)
    out_ref[...] = jnp.where(lane == total, rr, jnp.where(lane == total + 1, ff, spread))


def residual_body(
    freq_ref, sums_ref, inv_ref, r_ref, t_ref, mine_ref, other_ref, stat_m, stat_o, w_ref,
    out_ref, up_ref, down_ref, pc_ref, *, own, planes, natoms, cells,
):
    half = stat_m.shape[1]
    total = mine_ref.shape[0]
    square = freq_ref[0] * freq_ref[0]
    g = dot_nn(sums_ref[:, 0:total] / cells, inv_ref[...])
    rr, ff = sums_ref[:, total : total + 1], sums_ref[:, total + 1 : total + 2]
    step = rr / (ff + square * rr)
    for h, orb_ref in enumerate((mine_ref, other_ref)):
        for z in range(planes):
            rows, at = slice(z * own, (z + 1) * own), slice(h * half, (h + 1) * half)
            image = t_ref[rows, at] - dot_nn(g, orb_ref[:, z * half : (z + 1) * half])
            out_ref[rows, at] = r_ref[rows, at] - step * image
    pc = inner_partials(out_ref, (stat_m, stat_o), w_ref, own, natoms)
    pc_ref[...] = pc
    pack_edges(out_ref, pc, up_ref, down_ref, own)


def last_body(
    v_ref, pc_ref, lo_ref, hi_ref, stat_m, stat_o, w_ref, coup_ref, en_ref, r_ref, f_ref, u_ref, out_ref, *, own, cols
):
    def emit(at, block):
        u_ref[:, at] = block

    apply_shift(emit, v_ref, pc_ref, lo_ref, hi_ref, (stat_m, stat_o), w_ref, coup_ref, en_ref, cols)
    r1, r0, u1, u0 = (lane_blocks(ref, cols) for ref in (v_ref, r_ref, u_ref, f_ref))
    values = [
        orbital_row_sums([a * b for a, b in zip(x, y)], own) for x, y in ((r1, r1), (u1, u1), (u1, u0), (r1, r0))
    ]
    lanes = out_ref.shape[2]
    lane = lax.broadcasted_iota(jnp.int32, (own, lanes), 1)
    row = lax.broadcasted_iota(jnp.int32, (own, lanes), 0)
    placed = sum(jnp.where(lane == own * s + row, value, 0.0) for s, value in enumerate(values))
    line = jnp.sum(placed, axis=0, keepdims=True)
    out_ref[...] = jnp.broadcast_to(line[None], out_ref.shape)


def response_body(
    where_ref, freq_ref, sums_ref, lines_ref, f_ref, u_ref, mine_ref, other_ref, out_ref, swap_ref, dens_ref, *, own, planes
):
    total = mine_ref.shape[0]
    half = f_ref.shape[1] // 2
    square = freq_ref[0] * freq_ref[0]
    rr0, ff = sums_ref[:, total : total + 1], sums_ref[:, total + 1 : total + 2]
    line = jnp.sum(lines_ref[...], axis=0)[0:1, :]
    lanes = line.shape[1]
    lane = lax.broadcasted_iota(jnp.int32, (own, lanes), 1)
    row = lax.broadcasted_iota(jnp.int32, (own, lanes), 0)
    rr1, uu, uf, rx = (
        jnp.sum(jnp.where(lane == own * s + row, line, 0.0), axis=1, keepdims=True) for s in range(4)
    )
    step0 = rr0 / (ff + square * rr0)
    beta = rr1 / rr0
    curvature = uu + 2.0 * beta * uf + beta * beta * ff + square * (rr1 + 2.0 * beta * rx + beta * beta * rr0)
    step1 = rr1 / curvature
    start = pl.multiple_of(where_ref[0], own)
    swap_ref[own:, :] = jnp.zeros((swap_ref.shape[0] - own, swap_ref.shape[1]), f32)
    for h, orb_ref in enumerate((mine_ref, other_ref)):
        for z in range(planes):
            rows, at = slice(z * own, (z + 1) * own), slice(h * half, (h + 1) * half)
            to = slice(z * half, (z + 1) * half)
            response = (step0 + step1 * beta) * f_ref[rows, at] + step1 * u_ref[rows, at]
            dens = jnp.sum(orb_ref[pl.ds(start, own), to] * response, axis=0, keepdims=True)
            if h == 0:
                out_ref[:, to] = response
                dens_ref[:, to] = dens
            else:
                swap_ref[0:own, to] = response
                swap_ref[own : own + 1, to] = dens


def copy_for_each(array, axis):
    copies = jnp.broadcast_to(array, (lax.axis_size(axis), *array.shape))
    return lax.all_to_all(copies, axis, split_axis=0, concat_axis=0, tiled=True)


def swap_cores(array):
    return lax.ppermute(array, "pen", [(0, 1), (1, 0)])


def summed(array):
    count = lax.axis_size("slab")
    runs = [[i + j for j in range(NEAR)] for i in range(0, count, NEAR)]
    across = [[i + j for i in range(0, count, NEAR)] for j in range(NEAR)]
    array = lax.psum(array, "slab", axis_index_groups=runs)
    return lax.psum(array, "slab", axis_index_groups=across)


def from_neighbours(up, down):
    count = lax.axis_size("slab")
    ring = [(i, (i + 1) % count) for i in range(count)]
    return lax.ppermute(up, "slab", ring), lax.ppermute(down, "slab", [(b, a) for a, b in ring])


def plane_weights(atom_planes, profiles, planes, depth_total):
    span_size = profiles.shape[1]
    covered = (atom_planes[:, None] + jnp.arange(span_size, dtype=jnp.int32)[None, :]) % depth_total
    matches = (covered[None, :, :] == planes[:, None, None]).astype(jnp.float32)
    return jnp.sum(profiles[None, :, :] * matches, axis=2)


def on_device(
    orbitals, energies, frequency, local_potential, perturbation, projectors, profiles, couplings, atom_planes
):
    chip_count, planes, row_count, cols = orbitals.shape
    natoms = projectors.shape[0]
    half = row_count * cols
    slabs = lax.axis_size("slab")
    assert lax.axis_size("pen") == 2 and slabs > 2
    assert profiles.shape[1] == planes + 1
    depth_total = planes * slabs
    cells = float(depth_total * 2 * half)
    own = chip_count // 2
    core = lax.axis_index("pen")
    first_plane = lax.axis_index("slab") * planes
    weights = plane_weights(atom_planes, profiles, first_plane + jnp.arange(planes, dtype=jnp.int32), depth_total)
    where = jnp.stack([lax.axis_index("orb") * chip_count + core * own, core]).astype(jnp.int32)
    own_energies = lax.dynamic_slice(energies, (core * own,), (own,)).reshape(own, 1)
    coup = couplings.reshape(1, natoms)

    stat_m = jnp.concatenate(
        [a.reshape(-1, half) for a in (projectors, local_potential, perturbation)], axis=0
    )
    stat_o = swap_cores(stat_m)
    mine = copy_for_each(orbitals.reshape(chip_count, planes * half), "orb").reshape(-1, planes * half)
    other = swap_cores(mine)
    total = mine.shape[0]
    stats = (stat_m, stat_o)
    field, edge, part = (planes * own, 2 * half), (own, 2 * half + natoms), (own, natoms)

    (gram_part,) = call(
        functools.partial(gram_body, own=own, planes=planes, natoms=natoms),
        (where, mine, other, *stats), "svvvv", [(total // 4 + own, 2 * total)],
    )
    gram_sum = summed(gram_part)
    gram_other = swap_cores(gram_sum[0 : total // 4])
    r0, up, down, pc, inv = call(
        functools.partial(source_body, own=own, planes=planes, natoms=natoms, cells=cells),
        (where, gram_sum, gram_other, mine, other, *stats, weights), "svvvvvvv",
        [field, edge, edge, part, (total, total)],
    )
    lo, hi = from_neighbours(up, down)
    first, up, down, first_pc = call(
        functools.partial(first_body, own=own, natoms=natoms, cols=cols),
        (r0, pc, lo, hi, *stats, weights, coup, own_energies), "v" * 9, [field, edge, edge, part],
    )
    lo, hi = from_neighbours(up, down)
    target, sums_part = call(
        functools.partial(target_body, own=own, planes=planes, cols=cols),
        (frequency, first, first_pc, lo, hi, *stats, weights, coup, own_energies, r0, mine, other), "s" + "v" * 12,
        [field, (own, 2 * total)],
    )
    sums = summed(sums_part)
    r1, up, down, pc = call(
        functools.partial(residual_body, own=own, planes=planes, natoms=natoms, cells=cells),
        (frequency, sums, inv, r0, target, mine, other, *stats, weights), "s" + "v" * 9, [field, edge, edge, part],
    )
    lo, hi = from_neighbours(up, down)
    last, lines = call(
        functools.partial(last_body, own=own, cols=cols),
        (r1, pc, lo, hi, *stats, weights, coup, own_energies, r0, first), "v" * 11,
        [field, (slabs, 2, 2 * total)],
    )
    lines = lax.all_to_all(lines, "slab", split_axis=0, concat_axis=0, tiled=True)
    response, to_other, dens = call(
        functools.partial(response_body, own=own, planes=planes),
        (where, frequency, sums, lines, first, last, mine, other), "ss" + "v" * 6,
        [(own, planes * half), (2 * own, planes * half), (1, planes * half)],
    )
    got = swap_cores(to_other)
    theirs = got[0:own]
    low, high = jnp.where(core == 0, response, theirs), jnp.where(core == 0, theirs, response)
    response_real = jnp.concatenate([low, high], axis=0).reshape(orbitals.shape)
    dens = (dens + got[own : own + 1]).reshape(planes, half)
    density = copy_for_each(dens, "orb").sum(axis=0) * (4.0 / NOCC)
    return response_real, density.reshape(planes, row_count, cols)


def solution(mesh):
    in_specs = (
        P(("parts", "orb"), "slab", "pen", None),
        P(("parts", "orb")),
        P("parts"),
        P("slab", "pen", None),
        P("slab", "pen", None),
        P(None, "pen", None),
        P(),
        P(),
        P(),
    )
    out_specs = (P(("parts", "orb"), "slab", "pen", None), P(("parts", "slab"), "pen", None))
    return jax.shard_map(on_device, mesh=mesh, in_specs=in_specs, out_specs=out_specs, check_vma=False)
```

time: 783 us -> 290 us (0.37)
  blocking collectives: 601 us -> 191 us
  waiting for transfers between devices: 57.4 us -> 12.9 us
  Pallas kernels: 0 us -> 38.2 us
  starting transfers between devices: 61.1 us -> 33.3 us
  matrix products: 20.4 us -> 0 us
  other arithmetic: 16.8 us -> 2.2 us
  local copies, waits for them, and re-layouts: 22.5 us -> 9.19 us
    psum x16 -> x4, blocking collectives: 549 us -> 136 us  [the longest x2 103 us: summed(): return lax.psum(array, 'slab', axis_index_groups=across)]
    all_to_all x3 -> x1, waiting for transfers between devices: 57.3 us -> 4.58 us  [copy_for_each(): return lax.all_to_all(copies, axis, split_axis=0, concat_axis=0, tiled=True)]
    pallas_call x0 -> x7, Pallas kernels: none -> 38.2 us  [call(): pl.pallas_call(body, in_specs=[SMEM if k == 's' else VMEM for k in kinds]...]
    all_to_all x0 -> x1, blocking collectives: none -> 35.7 us  [on_device(): lax.all_to_all(lines, 'slab', split_axis=0, concat_axis=0, tiled=True)]
    all_to_all x1, blocking collectives: 51.2 us -> 19.7 us  [copy_for_each(): return lax.all_to_all(copies, axis, split_axis=0, concat_axis=0, tiled=True)]
    dot_general x17 -> x0, matrix products: 19.2 us -> none  [the longest x4 6.74 us: apply_section(): lax.dot_general(flat_spread, flat_beta, (((0,), (0,)), ((), ())), precisi...]
    ppermute x16 -> x10, starting transfers between devices: 46 us -> 29.9 us  [the longest x3 15.7 us: from_neighbours(): lax.ppermute(down, 'slab', [(b, a) for a, b in ring])]
    all_to_all x3 -> x1, starting transfers between devices: 15.2 us -> 3.37 us  [copy_for_each(): return lax.all_to_all(copies, axis, split_axis=0, concat_axis=0, tiled=True)]
  transfers between devices with their start and end apart: 19 -> 11, of which waited for: 3 -> 8; matrix products, arithmetic and copies ran while one was open for 1% -> 1% of each run, Pallas kernels for 0% -> 0%
where the time goes in v1:
time: 290 us; the launch traced here: 289 us
  blocking collectives  191 us (66%)
  Pallas kernels  38.2 us (13%)
  starting transfers between devices  33.3 us (11%)
  waiting for transfers between devices  12.9 us (4%)
  local copies, waits for them, and re-layouts  9.19 us (3%)
    psum x2, blocking collectives, summed(): return lax.psum(array, 'slab', axis_index_groups=across)  103 us
    pallas_call x7, Pallas kernels, call(): pl.pallas_call(body, in_specs=[SMEM if k == 's' else VMEM for k in kinds]...  38.2 us
    all_to_all x1, blocking collectives, on_device(): lax.all_to_all(lines, 'slab', split_axis=0, concat_axis=0, tiled=True)  35.7 us
    psum x2, blocking collectives, summed(): array = lax.psum(array, 'slab', axis_index_groups=runs)  32.8 us
    all_to_all x1, blocking collectives, copy_for_each(): return lax.all_to_all(copies, axis, split_axis=0, concat_axis=0, tiled=True)  19.7 us
    ppermute x3, starting transfers between devices, from_neighbours(): lax.ppermute(down, 'slab', [(b, a) for a, b in ring])  15.7 us
    ppermute x4, starting transfers between devices, swap_cores(): return lax.ppermute(array, 'pen', [(0, 1), (1, 0)])  8.39 us
    ppermute x3, starting transfers between devices, from_neighbours(): lax.ppermute(up, 'slab', ring)  5.82 us
  transfers between devices with their start and end apart: 11, of which 8 were waited for; matrix products, arithmetic and copies ran while one was open for 1% of the time, Pallas kernels for 0%

profile of v1, /device:TPU:40, one launch (start us, length us, event | category | flops | bytes accessed | tf_op | source)
XLA Modules:
  0.0 288.8 jit_solution(4217790219367940623)
XLA Ops:
  0.6 0.0 copy-start
  0.6 1.1 reshape.69
  1.7 0.1 broadcast_in_dim.4
  1.8 0.0 copy-start.14
  1.8 0.0 copy-start.5
  1.8 19.7 %all_to_all.15 = f32[4,16,4096]{2,1,0:T(8,128)S(1)} all-to-all(f32[4,16,4096]{2,1,0:T(8,128)S(1)} %broadcast_in_dim.4), channel_id=1, replica_groups=mesh['parts'=2,'slab'=32,'orb'=4,'pen'=2] {'orb'}, dimensions={0} | all-to-all | bytes 2097152 | tf_op jit(solution)/shard_map/all_to_all | solution.py:275
  21.5 1.9 collective-permute-start
  23.5 0.0 copy-done.14
  23.5 0.0 copy-start.15
  23.5 0.7 copy-done.15
  24.2 0.0 copy-done.5
  24.2 0.1 copy.18
  24.4 0.0 copy-done.1
  24.4 0.0 copy-start.2
  24.4 2.4 collective-permute-start.1
  26.8 0.0 copy-start.18
  26.9 0.7 pad_add_fusion.where_ref
  27.5 0.9 collective-permute-done.1.stat_o
  28.4 0.0 collective-permute-done.other_ref
  28.4 0.0 copy-done.2
  28.4 0.8 copy-done.4
  29.2 1.0 copy-done.3
  30.2 5.9 %shard_map.104 = f32[24,128]{1,0:T(8,128)} custom-call(s32[2]{0:T(128)} %pad_add_fusion.where_ref, f32[64,4096]{1,0:T(8,128)} %bitcast.13, f32[64,4096]{1,0:T(8,128)} %copy-done.3, f32[136,1024]{1,0:T(8,128)} %copy-done.2, f32[136,1024]{1,0:T(8,128)} %copy-done.4), custom_call_target="tpu_custom_call" | custom-call | tf_op jit(solution)/shard_map/pallas_call | solution.py:29
  36.1 23.2 %psum.28 = f32[24,128]{1,0:T(8,128)S(1)} all-reduce(f32[24,128]{1,0:T(8,128)} %shard_map.104), channel_id=1, replica_groups={{0,8,16,24},{32,40,48,56},{64,72,80,88},{96,104,112,120},{128,136,144,1..., use_global_device_ids=true, to_apply=%region_0.1 | all-reduce | flops 3072 | bytes 24576 | tf_op jit(solution)/shard_map/psum | solution.py:286
  59.3 77.2 %psum.29.sums_ref = f32[24,128]{1,0:T(8,128)S(1)} all-reduce(f32[24,128]{1,0:T(8,128)S(1)} %psum.28), channel_id=1, replica_groups={{0,32,64,96,128,160,192,224},{8,40,72,104,136,168,200,232},{16,48,80,11..., use_global_device_ids=true, to_apply=%region_1.2 | all-reduce | flops 3072 | bytes 24576 | tf_op jit(solution)/shard_map/psum | solution.py:287
  136.5 2.1 collective-permute-start.2
  138.6 0.7 select_reduce_fusion.w_ref
  139.3 0.0 copy-done.7
  139.3 0.5 collective-permute-done.2.swapped_ref
  139.7 0.6 copy-done.16
  140.3 13.2 %shard_map.105 = (f32[32,2048]{1,0:T(8,128)}, f32[8,2176]{1,0:T(8,128)}, f32[8,2176]{1,0:T(8,128)}, f32[8,128]{1,0:T(8,128)}, f32[64,64]{1,0:T(8,128)}) custom-call(s32[2]{0:T(128)} %pad_add_fusion.where_ref, f32[24,128]{1,0:T(8,128)} %copy-done.7, f32[16,128]{1,0:T(8,128)} %copy-done.16, f32[64,4096]{1,0:T(8,128)} %bitcast.14, f32[64,4096]{1,0:T(8,128)} %copy-done.3, ...), custom_call_target="tpu_custom_call" | custom-call | tf_op jit(solution)/shard_map/pallas_call | solution.py:29
  153.6 1.9 collective-permute-start.3
  155.5 5.2 %collective-permute-start.4 = (f32[8,2176]{1,0:T(8,128)}, f32[8,2176]{1,0:T(8,128)S(1)}, u32[]{:S(2)}, u32[]{:S(2)}) collective-permute-start(f32[8,2176]{1,0:T(8,128)} %get-tuple-element.25), channel_id=1, source_target_pairs={{8,0},{16,8},{24,16},{32,24},{40,32},{48,40},{56,48},{64,56},{72,6... | collective-permute-start | bytes 208904 | tf_op jit(solution)/shard_map/ppermute | solution.py:293
  160.7 0.1 dynamic-slice_bitcast_fusion
  160.8 0.7 copy.15.en_ref
  161.4 0.0 collective-permute-done.3.lo_ref
  161.5 1.5 collective-permute-done.4.hi_ref
  162.9 0.6 copy-done.9
  163.5 3.7 %shard_map.106 = (f32[32,2048]{1,0:T(8,128)}, f32[8,2176]{1,0:T(8,128)}, f32[8,2176]{1,0:T(8,128)}, f32[8,128]{1,0:T(8,128)}) custom-call(f32[32,2048]{1,0:T(8,128)} %get-tuple-element.22.v_ref.r_ref, f32[8,128]{1,0:T(8,128)} %get-tuple-element.23.pc_ref, f32[8,2176]{1,0:T(8,128)} %copy-done.8, f32[8,2176]{1,0:T(8,128)} %copy-done.9, f32[136,1024]{1,0:T(8,128)} %copy-done.2, ...), custom_call_target="tpu_custom_call" | custom-call | tf_op jit(solution)/shard_map/pallas_call | solution.py:29
  167.2 1.9 collective-permute-start.5
  169.2 5.4 %collective-permute-start.6 = (f32[8,2176]{1,0:T(8,128)}, f32[8,2176]{1,0:T(8,128)S(1)}, u32[]{:S(2)}, u32[]{:S(2)}) collective-permute-start(f32[8,2176]{1,0:T(8,128)} %get-tuple-element.29), channel_id=1, source_target_pairs={{8,0},{16,8},{24,16},{32,24},{40,32},{48,40},{56,48},{64,56},{72,6... | collective-permute-start | bytes 208904 | tf_op jit(solution)/shard_map/ppermute | solution.py:293
  175.3 0.0 collective-permute-done.5.lo_ref
  175.3 1.6 collective-permute-done.6.hi_ref
  176.8 0.6 copy-done.13
  177.5 5.1 %shard_map.107 = (f32[32,2048]{1,0:T(8,128)}, f32[8,128]{1,0:T(8,128)}) custom-call(f32[1]{0:T(128)S(6)} %copy.21.freq_ref, f32[32,2048]{1,0:T(8,128)} %get-tuple-element.26.v_ref.f_ref, f32[8,128]{1,0:T(8,128)} %get-tuple-element.27.pc_ref, f32[8,2176]{1,0:T(8,128)} %copy-done.12, f32[8,2176]{1,0:T(8,128)} %copy-done.13, f32[136,1024]{1,0:T(8,128)} %copy-done.2, ...), custom_call_target="tpu_custom_call" | custom-call | tf_op jit(solution)/shard_map/pallas_call | solution.py:29
  182.6 9.5 %psum.30 = f32[8,128]{1,0:T(8,128)S(1)} all-reduce(f32[8,128]{1,0:T(8,128)} %get-tuple-element.30), channel_id=1, replica_groups={{0,8,16,24},{32,40,48,56},{64,72,80,88},{96,104,112,120},{128,136,144,1..., use_global_device_ids=true, to_apply=%region_3.4 | all-reduce | flops 1024 | bytes 8192 | tf_op jit(solution)/shard_map/psum | solution.py:286
  192.1 26.1 %psum.31.sums_ref = f32[8,128]{1,0:T(8,128)} all-reduce(f32[8,128]{1,0:T(8,128)S(1)} %psum.30), channel_id=1, replica_groups={{0,32,64,96,128,160,192,224},{8,40,72,104,136,168,200,232},{16,48,80,11..., use_global_device_ids=true, to_apply=%region_4.5 | all-reduce | flops 1024 | bytes 8192 | tf_op jit(solution)/shard_map/psum | solution.py:287
  218.1 4.7 %shard_map.108 = (f32[32,2048]{1,0:T(8,128)}, f32[8,2176]{1,0:T(8,128)}, f32[8,2176]{1,0:T(8,128)}, f32[8,128]{1,0:T(8,128)}) custom-call(f32[1]{0:T(128)S(6)} %copy.21.freq_ref, f32[8,128]{1,0:T(8,128)} %psum.31.sums_ref, f32[64,64]{1,0:T(8,128)} %get-tuple-element.31.inv_ref, f32[32,2048]{1,0:T(8,128)} %get-tuple-element.22.v_ref.r_ref, ...), custom_call_target="tpu_custom_call" | custom-call | tf_op jit(solution)/shard_map/pallas_call | solution.py:29
  222.8 1.9 collective-permute-start.7
  224.8 5.2 %collective-permute-start.8 = (f32[8,2176]{1,0:T(8,128)}, f32[8,2176]{1,0:T(8,128)S(1)}, u32[]{:S(2)}, u32[]{:S(2)}) collective-permute-start(f32[8,2176]{1,0:T(8,128)} %get-tuple-element.36), channel_id=1, source_target_pairs={{8,0},{16,8},{24,16},{32,24},{40,32},{48,40},{56,48},{64,56},{72,6... | collective-permute-start | bytes 208904 | tf_op jit(solution)/shard_map/ppermute | solution.py:293
  230.0 0.5 collective-permute-done.7.lo_ref
  230.5 1.7 collective-permute-done.8.hi_ref
  232.2 0.6 copy-done.11
  232.8 2.8 shard_map.109
  235.7 35.7 %all_to_all.16.lines_ref = f32[32,2,128]{2,1,0:T(2,128)} all-to-all(f32[32,2,128]{2,1,0:T(2,128)} %get-tuple-element.37), channel_id=1, replica_groups=mesh['parts'=2,'slab'=32,'orb'=4,'pen'=2] {'slab'}, dimensions={0} | all-to-all | bytes 65536 | tf_op jit(solution)/shard_map/all_to_all | solution.py:365
  271.4 2.7 shard_map.110
  274.1 1.9 collective-permute-start.9
  276.1 1.7 collective-permute-done.9
  277.8 0.8 fusion
  278.6 0.6 broadcast_in_dim.5
  279.2 3.4 %all-to-all-start.2 = ((f32[4,4,1024]{2,1,0:T(4,128)}), f32[4,4,1024]{2,1,0:T(4,128)S(1)}, u32[]{:S(2)}, u32[]{:S(2)}) async-start(f32[4,4,1024]{2,1,0:T(4,128)} %broadcast_in_dim.5), calls=%async_computation.2 | async-start | bytes 131072 | tf_op jit(solution)/shard_map/all_to_all | solution.py:275
  282.7 0.9 reshape.76
  283.6 4.6 %all-to-all-done.2 = f32[4,4,1024]{2,1,0:T(4,128)S(1)} async-done(((f32[4,4,1024]{2,1,0:T(4,128)}), f32[4,4,1024]{2,1,0:T(4,128)S(1)}, u32[]{:S(2)}, u32[]{:S(2)}) %all-to-all-start.2) | async-done | bytes 65568 | tf_op jit(solution)/shard_map/all_to_all | solution.py:275
  288.2 0.6 mul.35
  (31 shorter events, 0.2 us)
Async XLA Ops:
  0.6 160.1 %copy-start = (f32[16]{0:T(128)S(1)}, f32[16]{0:T(128)}, u32[]{:S(2)}) copy-start(f32[16]{0:T(128)} %param.10) | copy-start | bytes 196
  1.8 21.7 %copy-start.14 = (f32[4,4,256]{2,1,0:T(4,128)S(1)}, f32[4,4,256]{2,1,0:T(4,128)}, u32[]{:S(2)}) copy-start(f32[4,4,256]{2,1,0:T(4,128)} %param.12) | copy-start | bytes 49156
  1.8 22.4 %copy-start.5 = (f32[128,4,256]{2,1,0:T(4,128)S(1)}, f32[128,4,256]{2,1,0:T(4,128)}, u32[]{:S(2)}) copy-start(f32[128,4,256]{2,1,0:T(4,128)} %param.14) | copy-start | bytes 1572868
  21.5 2.8 copy-start.1
  21.5 6.9 %collective-permute-start = (f32[64,4096]{1,0:T(8,128)S(1)}, f32[64,4096]{1,0:T(8,128)S(1)}, u32[]{:S(2)}, u32[]{:S(2)}) collective-permute-start(f32[64,4096]{1,0:T(8,128)S(1)} %bitcast.12), channel_id=1, source_target_pairs={{0,1},{1,0},{2,3},{3,2},{4,5},{5,4},{6,7},{7,6},{8,9},{9,8},{10,11... | collective-permute-start | bytes 3145736 | tf_op jit(solution)/shard_map/ppermute | solution.py:279
  23.5 0.7 copy-start.15
  24.4 4.0 %copy-start.2 = (f32[136,1024]{1,0:T(8,128)}, f32[136,1024]{1,0:T(8,128)S(1)}, u32[]{:S(2)}) copy-start(f32[136,1024]{1,0:T(8,128)S(1)} %pad_maximum_fusion.stat_m) | copy-start | bytes 1671172
  24.4 4.0 %collective-permute-start.1 = (f32[136,1024]{1,0:T(8,128)S(1)}, f32[136,1024]{1,0:T(8,128)S(1)}, u32[]{:S(2)}, u32[]{:S(2)}) collective-permute-start(f32[136,1024]{1,0:T(8,128)S(1)} %pad_maximum_fusion.stat_m), channel_id=1, source_target_pairs={{0,1},{1,0},{2,3},{3,2},{4,5},{5,4},{6,7},{7,6},{8,9},{9,8},{10,11... | collective-permute-start | bytes 1671176 | tf_op jit(solution)/shard_map/ppermute | solution.py:279
  26.8 0.7 copy-start.18
  28.4 0.8 copy-start.4
  29.2 1.0 copy-start.3
  136.5 2.8 copy-start.7
  136.5 2.1 copy-start.17
  136.5 3.2 %collective-permute-start.2 = (f32[16,128]{1,0:T(8,128)S(1)}, f32[16,128]{1,0:T(8,128)S(1)}, u32[]{:S(2)}, u32[]{:S(2)}) collective-permute-start(f32[16,128]{1,0:T(8,128)S(1)} %slice.12), channel_id=1, source_target_pairs={{0,1},{1,0},{2,3},{3,2},{4,5},{5,4},{6,7},{7,6},{8,9},{9,8},{10,11... | collective-permute-start | bytes 24584 | tf_op jit(solution)/shard_map/ppermute | solution.py:279
  139.7 0.6 copy-start.16
  153.6 7.9 %collective-permute-start.3 = (f32[8,2176]{1,0:T(8,128)}, f32[8,2176]{1,0:T(8,128)S(1)}, u32[]{:S(2)}, u32[]{:S(2)}) collective-permute-start(f32[8,2176]{1,0:T(8,128)} %get-tuple-element.24), channel_id=1, source_target_pairs={{0,8},{8,16},{16,24},{24,32},{32,40},{40,48},{48,56},{56,64},{64,7... | collective-permute-start | bytes 208904 | tf_op jit(solution)/shard_map/ppermute | solution.py:293
  155.5 7.4 %collective-permute-start.4 = (f32[8,2176]{1,0:T(8,128)}, f32[8,2176]{1,0:T(8,128)S(1)}, u32[]{:S(2)}, u32[]{:S(2)}) collective-permute-start(f32[8,2176]{1,0:T(8,128)} %get-tuple-element.25), channel_id=1, source_target_pairs={{8,0},{16,8},{24,16},{32,24},{40,32},{48,40},{56,48},{64,56},{72,6... | collective-permute-start | bytes 208904 | tf_op jit(solution)/shard_map/ppermute | solution.py:293
  161.5 1.5 copy-start.8
  162.9 0.6 copy-start.9
  167.2 8.0 %collective-permute-start.5 = (f32[8,2176]{1,0:T(8,128)}, f32[8,2176]{1,0:T(8,128)S(1)}, u32[]{:S(2)}, u32[]{:S(2)}) collective-permute-start(f32[8,2176]{1,0:T(8,128)} %get-tuple-element.28), channel_id=1, source_target_pairs={{0,8},{8,16},{16,24},{24,32},{32,40},{40,48},{48,56},{56,64},{64,7... | collective-permute-start | bytes 208904 | tf_op jit(solution)/shard_map/ppermute | solution.py:293
  169.2 7.7 %collective-permute-start.6 = (f32[8,2176]{1,0:T(8,128)}, f32[8,2176]{1,0:T(8,128)S(1)}, u32[]{:S(2)}, u32[]{:S(2)}) collective-permute-start(f32[8,2176]{1,0:T(8,128)} %get-tuple-element.29), channel_id=1, source_target_pairs={{8,0},{16,8},{24,16},{32,24},{40,32},{48,40},{56,48},{64,56},{72,6... | collective-permute-start | bytes 208904 | tf_op jit(solution)/shard_map/ppermute | solution.py:293
  175.3 1.6 copy-start.12
  176.8 0.6 copy-start.13
  222.8 7.6 %collective-permute-start.7 = (f32[8,2176]{1,0:T(8,128)}, f32[8,2176]{1,0:T(8,128)S(1)}, u32[]{:S(2)}, u32[]{:S(2)}) collective-permute-start(f32[8,2176]{1,0:T(8,128)} %get-tuple-element.35), channel_id=1, source_target_pairs={{0,8},{8,16},{16,24},{24,32},{32,40},{40,48},{48,56},{56,64},{64,7... | collective-permute-start | bytes 208904 | tf_op jit(solution)/shard_map/ppermute | solution.py:293
  224.8 7.4 %collective-permute-start.8 = (f32[8,2176]{1,0:T(8,128)}, f32[8,2176]{1,0:T(8,128)S(1)}, u32[]{:S(2)}, u32[]{:S(2)}) collective-permute-start(f32[8,2176]{1,0:T(8,128)} %get-tuple-element.36), channel_id=1, source_target_pairs={{8,0},{16,8},{24,16},{32,24},{40,32},{48,40},{56,48},{64,56},{72,6... | collective-permute-start | bytes 208904 | tf_op jit(solution)/shard_map/ppermute | solution.py:293
  230.5 1.7 copy-start.10
  232.2 0.6 copy-start.11
  274.1 3.7 %collective-permute-start.9 = (f32[16,4096]{1,0:T(8,128)}, f32[16,4096]{1,0:T(8,128)S(1)}, u32[]{:S(2)}, u32[]{:S(2)}) collective-permute-start(f32[16,4096]{1,0:T(8,128)} %get-tuple-element.40), channel_id=1, source_target_pairs={{0,1},{1,0},{2,3},{3,2},{4,5},{5,4},{6,7},{7,6},{8,9},{9,8},{10,11... | collective-permute-start | bytes 786440 | tf_op jit(solution)/shard_map/ppermute | solution.py:279
  278.6 4.0 %copy-start.6 = (f32[8,4096]{1,0:T(8,128)S(1)}, f32[8,4096]{1,0:T(8,128)}, u32[]{:S(2)}) copy-start(f32[8,4096]{1,0:T(8,128)} %get-tuple-element.39) | copy-start | bytes 393220
  279.2 8.9 %all-to-all-start.2 = ((f32[4,4,1024]{2,1,0:T(4,128)}), f32[4,4,1024]{2,1,0:T(4,128)S(1)}, u32[]{:S(2)}, u32[]{:S(2)}) async-start(f32[4,4,1024]{2,1,0:T(4,128)} %broadcast_in_dim.5), calls=%async_computation.2 | async-start | bytes 131072 | tf_op jit(solution)/shard_map/all_to_all | solution.py:275

commit v2 on v1

--- a/solution.py
+++ b/solution.py
@@ -25,13 +25,13 @@
     return lax.dot_general(a, b, (((1,), (1,)), ((), ())), precision=highest, preferred_element_type=f32)
 
 
-def call(body, args, kinds, outs, scratch=()):
+def call(body, args, kinds, outs):
+    args = [pltpu.with_memory_space_constraint(a, pltpu.VMEM) if k == "k" else a for a, k in zip(args, kinds, strict=True)]
     return pl.pallas_call(
         body,
         in_specs=[SMEM if k == "s" else VMEM for k in kinds],
         out_specs=[VMEM] * len(outs),
-        out_shape=[jax.ShapeDtypeStruct(s, f32) for s in outs],
-        scratch_shapes=list(scratch),
+        out_shape=[pltpu.VMEM(s, f32) for s in outs],
     )(*args)
 
 
@@ -96,19 +96,40 @@
 def gram_body(where_ref, mine_ref, other_ref, stat_m, stat_o, out_ref, *, own, planes, natoms):
     half = stat_m.shape[1]
     total = mine_ref.shape[0]
-    span = total // 2
+    span, quarter = total // 2, total // 4
     rows = pl.ds(pl.multiple_of(where_ref[1] * span, span), span)
     start = pl.multiple_of(where_ref[0], own)
-    gram = dot_nt(mine_ref[rows, :], mine_ref[...]) + dot_nt(other_ref[rows, :], other_ref[...])
-    corr = jnp.zeros((own, total), f32)
+    sums = jnp.zeros((span + own, total), f32)
     for orb_ref, stat in ((mine_ref, stat_m), (other_ref, stat_o)):
         for z in range(planes):
             at = slice(z * half, (z + 1) * half)
             source = stat[natoms + planes + z : natoms + planes + z + 1, :] * orb_ref[pl.ds(start, own), at]
-            corr = corr + dot_nt(source, orb_ref[:, at])
-    quarter = span // 2
-    out_ref[0:quarter, :] = jnp.concatenate([gram[0:quarter], gram[quarter:]], axis=1)
-    out_ref[quarter:, :] = jnp.concatenate([corr, jnp.zeros((own, total), f32)], axis=1)
+            sums = sums + dot_nt(jnp.concatenate([orb_ref[rows, at], source], axis=0), orb_ref[:, at])
+    gram, corr = sums[0:span], sums[span:]
+    twice = jnp.concatenate([gram, gram], axis=1)
+    ahead = jnp.where(where_ref[1] == 0, twice[:, 0:total], twice[:, span : span + total])
+    out_ref[...] = jnp.concatenate(
+        [
+            ahead[0:quarter, 0 : 3 * quarter],
+            ahead[quarter:, quarter:],
+            jnp.concatenate([corr[:, 0:span], corr[:, span:]], axis=0),
+        ],
+        axis=1,
+    )
+
+
+def gram_from(low, high):
+    quarter = low.shape[0]
+    blocks = [
+        [part[:, i + d * quarter : i + (d + 1) * quarter] * (1.0 if d == 1 else 0.5) for d in range(3)]
+        + [jnp.zeros((quarter, quarter), f32)]
+        for part in (low, high)
+        for i in (0, 3 * quarter)
+    ]
+    upper = jnp.concatenate(
+        [jnp.concatenate([blocks[j][(k - j) % 4] for k in range(4)], axis=1) for j in range(4)], axis=0
+    )
+    return upper + upper.T
 
 
 def inverse_of(gram):
@@ -117,15 +138,21 @@
     work = jnp.concatenate([gram, eye], axis=1)
     tiles = [work[i : i + 8] for i in range(0, n, 8)]
     sub = lax.broadcasted_iota(jnp.int32, (8, 2 * n), 0)
-    for k in range(n):
+    for k in range(0, n, 2):
         t, r = divmod(k, 8)
-        row = tiles[t][r : r + 1, :]
-        scaled = row * (1.0 / row[:, k : k + 1])
-        scale = lax.rsqrt(row[:, k : k + 1])
+        row0, row1 = tiles[t][r : r + 1, :], tiles[t][r + 1 : r + 2, :]
+        a, b, d = row0[:, k : k + 1], row0[:, k + 1 : k + 2], row1[:, k + 1 : k + 2]
+        det = a * d - b * b
+        over = 1.0 / det
+        x0 = row0 * (d * over) - row1 * (b * over)
+        x1 = row1 * (a * over) - row0 * (b * over)
         for i in range(t, n // 8):
-            step = tiles[i] - tiles[i][:, k : k + 1] * scaled
+            step = tiles[i] - tiles[i][:, k : k + 1] * x0 - tiles[i][:, k + 1 : k + 2] * x1
             if i == t:
-                step = jnp.where(sub > r, step, jnp.where(sub == r, tiles[i] * scale, tiles[i]))
+                first = row0 * lax.rsqrt(a)
+                second = (row1 - row0 * (b / a)) * lax.rsqrt(det / a)
+                kept = jnp.where(sub == r, first, jnp.where(sub == r + 1, second, tiles[i]))
+                step = jnp.where(sub > r + 1, step, kept)
             tiles[i] = step
     lower_inverse = jnp.concatenate(tiles, axis=0)[:, n:]
     inv = lax.dot_general(
@@ -140,14 +167,13 @@
 ):
     half = stat_m.shape[1]
     total = mine_ref.shape[0]
-    quarter = total // 4
-    ours, theirs = sums_ref[0:quarter, :], swapped_ref[...]
+    ours, theirs = sums_ref[...], swapped_ref[...]
     first = where_ref[1] == 0
-    low, high = jnp.where(first, ours, theirs), jnp.where(first, theirs, ours)
-    gram = jnp.concatenate([low[:, :total], low[:, total:], high[:, :total], high[:, total:]], axis=0) / cells
+    gram = gram_from(jnp.where(first, ours, theirs), jnp.where(first, theirs, ours)) / cells
     inv = inverse_of(gram)
     inv_ref[...] = inv
-    g = dot_nn(sums_ref[quarter:, 0:total] / cells, inv)
+    folded = ours[:, 2 * total - total // 2 :] / cells
+    g = dot_nn(jnp.concatenate([folded[0:own], folded[own:]], axis=1), inv)
     start = pl.multiple_of(where_ref[0], own)
     for h, (orb_ref, stat) in enumerate(((mine_ref, stat_m), (other_ref, stat_o))):
         for z in range(planes):
@@ -331,41 +357,41 @@
 
     (gram_part,) = call(
         functools.partial(gram_body, own=own, planes=planes, natoms=natoms),
-        (where, mine, other, *stats), "svvvv", [(total // 4 + own, 2 * total)],
+        (where, mine, other, *stats), "svvkk", [(total // 4, 2 * total)],
     )
     gram_sum = summed(gram_part)
-    gram_other = swap_cores(gram_sum[0 : total // 4])
+    gram_other = swap_cores(gram_sum)
     r0, up, down, pc, inv = call(
         functools.partial(source_body, own=own, planes=planes, natoms=natoms, cells=cells),
-        (where, gram_sum, gram_other, mine, other, *stats, weights), "svvvvvvv",
+        (where, gram_sum, gram_other, mine, other, *stats, weights), "skkvvkkk",
         [field, edge, edge, part, (total, total)],
     )
     lo, hi = from_neighbours(up, down)
     first, up, down, first_pc = call(
         functools.partial(first_body, own=own, natoms=natoms, cols=cols),
-        (r0, pc, lo, hi, *stats, weights, coup, own_energies), "v" * 9, [field, edge, edge, part],
+        (r0, pc, lo, hi, *stats, weights, coup, own_energies), "kkkkkkkkk", [field, edge, edge, part],
     )
     lo, hi = from_neighbours(up, down)
     target, sums_part = call(
         functools.partial(target_body, own=own, planes=planes, cols=cols),
-        (frequency, first, first_pc, lo, hi, *stats, weights, coup, own_energies, r0, mine, other), "s" + "v" * 12,
+        (frequency, first, first_pc, lo, hi, *stats, weights, coup, own_energies, r0, mine, other), "skkkkkkkkkkvv",
         [field, (own, 2 * total)],
     )
     sums = summed(sums_part)
     r1, up, down, pc = call(
         functools.partial(residual_body, own=own, planes=planes, natoms=natoms, cells=cells),
-        (frequency, sums, inv, r0, target, mine, other, *stats, weights), "s" + "v" * 9, [field, edge, edge, part],
+        (frequency, sums, inv, r0, target, mine, other, *stats, weights), "skkkkvvkkk", [field, edge, edge, part],
     )
     lo, hi = from_neighbours(up, down)
     last, lines = call(
         functools.partial(last_body, own=own, cols=cols),
-        (r1, pc, lo, hi, *stats, weights, coup, own_energies, r0, first), "v" * 11,
+        (r1, pc, lo, hi, *stats, weights, coup, own_energies, r0, first), "kkkkkkkkkkk",
         [field, (slabs, 2, 2 * total)],
     )
     lines = lax.all_to_all(lines, "slab", split_axis=0, concat_axis=0, tiled=True)
     response, to_other, dens = call(
         functools.partial(response_body, own=own, planes=planes),
-        (where, frequency, sums, lines, first, last, mine, other), "ss" + "v" * 6,
+        (where, frequency, sums, lines, first, last, mine, other), "sskkkkvv",
         [(own, planes * half), (2 * own, planes * half), (1, planes * half)],
     )
     got = swap_cores(to_other)

time: 290 us -> 247 us (0.85)
  blocking collectives: 191 us -> 165 us
  Pallas kernels: 38.2 us -> 26.8 us
  local copies, waits for them, and re-layouts: 9.19 us -> 4.98 us
    psum x2, blocking collectives: 103 us -> 84.8 us  [summed(): return lax.psum(array, 'slab', axis_index_groups=across)]
    pallas_call x7, Pallas kernels: 38.2 us -> 26.8 us  [call(): pl.pallas_call(body, in_specs=[SMEM if k == 's' else VMEM for k in kinds]...]
    psum x2, blocking collectives: 32.8 us -> 25.2 us  [summed(): array = lax.psum(array, 'slab', axis_index_groups=runs)]
    unnamed x41 -> x19, local copies, waits for them, and re-layouts: 5.11 us -> 1.5 us
  transfers between devices with their start and end apart: 11 -> 11, of which waited for: 8 -> 9; matrix products, arithmetic and copies ran while one was open for 1% -> 1% of each run, Pallas kernels for 0% -> 0%
where the time goes in v2:
time: 247 us; the launch traced here: 246 us
  blocking collectives  165 us (67%)
  starting transfers between devices  33.4 us (14%)
  Pallas kernels  26.8 us (11%)
  waiting for transfers between devices  12.9 us (5%)
  local copies, waits for them, and re-layouts  4.98 us (2%)
    psum x2, blocking collectives, summed(): return lax.psum(array, 'slab', axis_index_groups=across)  84.8 us
    all_to_all x1, blocking collectives, on_device(): lax.all_to_all(lines, 'slab', split_axis=0, concat_axis=0, tiled=True)  35.7 us
    pallas_call x7, Pallas kernels, call(): pl.pallas_call(body, in_specs=[SMEM if k == 's' else VMEM for k in kinds]...  26.8 us
    psum x2, blocking collectives, summed(): array = lax.psum(array, 'slab', axis_index_groups=runs)  25.2 us
    all_to_all x1, blocking collectives, copy_for_each(): return lax.all_to_all(copies, axis, split_axis=0, concat_axis=0, tiled=True)  19.7 us
    ppermute x3, starting transfers between devices, from_neighbours(): lax.ppermute(down, 'slab', [(b, a) for a, b in ring])  15.7 us
    ppermute x4, starting transfers between devices, swap_cores(): return lax.ppermute(array, 'pen', [(0, 1), (1, 0)])  8.28 us
    ppermute x3, starting transfers between devices, from_neighbours(): lax.ppermute(up, 'slab', ring)  6.04 us
  transfers between devices with their start and end apart: 11, of which 9 were waited for; matrix products, arithmetic and copies ran while one was open for 1% of the time, Pallas kernels for 0%

profile of v2, /device:TPU:40, one launch (start us, length us, event | category | flops | bytes accessed | tf_op | source)
XLA Modules:
  0.0 246.0 jit_solution(16325346307981993767)
XLA Ops:
  0.6 0.0 copy-start
  0.6 1.1 reshape.69
  1.7 0.1 broadcast_in_dim.4
  1.8 0.0 copy-start.4
  1.8 0.0 copy-start.3
  1.8 19.7 %all_to_all.15 = f32[4,16,4096]{2,1,0:T(8,128)S(1)} all-to-all(f32[4,16,4096]{2,1,0:T(8,128)S(1)} %broadcast_in_dim.4), channel_id=1, replica_groups=mesh['parts'=2,'slab'=32,'orb'=4,'pen'=2] {'orb'}, dimensions={0} | all-to-all | bytes 2097152 | tf_op jit(solution)/shard_map/all_to_all | solution.py:301
  21.5 0.0 copy-start.2
  21.5 1.9 collective-permute-start
  23.5 0.0 copy-done.4
  23.5 0.0 copy-start.5
  23.5 0.7 copy-done.5
  24.2 0.0 copy-done.3
  24.2 0.1 copy.18
  24.4 0.0 copy-done.2
  24.4 2.4 collective-permute-start.1
  26.8 0.0 copy-start.7
  26.8 0.7 pad_add_fusion.where_ref
  27.5 0.0 copy-done.7
  27.5 0.9 collective-permute-done.1.stat_o
  28.4 0.0 collective-permute-done.other_ref
  28.4 3.5 %shard_map.104 = f32[16,128]{1,0:T(8,128)S(1)} custom-call(s32[2]{0:T(128)} %pad_add_fusion.where_ref, f32[64,4096]{1,0:T(8,128)} %bitcast.16, f32[64,4096]{1,0:T(8,128)} %collective-permute-done.other_ref, f32[136,1024]{1,0:T(8,128)S(1)} %pad_maximum_fusion.stat_m, f32[136,1024]{1,0:T(8,128)S(1)} %collective-permute-done.1.stat_o), custom_call_target="tpu_custom_call" | custom-call | tf_op jit(solution)/shard_map/pallas_call | solution.py:30
  31.9 15.7 %psum.28 = f32[16,128]{1,0:T(8,128)S(1)} all-reduce(f32[16,128]{1,0:T(8,128)S(1)} %shard_map.104), channel_id=1, replica_groups={{0,8,16,24},{32,40,48,56},{64,72,80,88},{96,104,112,120},{128,136,144,1..., use_global_device_ids=true, to_apply=%region_0.1 | all-reduce | flops 2048 | bytes 16384 | tf_op jit(solution)/shard_map/psum | solution.py:312
  47.6 0.0 copy-start.6
  47.6 59.4 %psum.29.sums_ref = f32[16,128]{1,0:T(8,128)S(1)} all-reduce(f32[16,128]{1,0:T(8,128)S(1)} %psum.28), channel_id=1, replica_groups={{0,32,64,96,128,160,192,224},{8,40,72,104,136,168,200,232},{16,48,80,11..., use_global_device_ids=true, to_apply=%region_1.2 | all-reduce | flops 2048 | bytes 16384 | tf_op jit(solution)/shard_map/psum | solution.py:313
  107.0 2.0 collective-permute-start.2
  109.0 0.0 copy-done.6
  109.0 0.1 select_reduce_fusion.w_ref
  109.1 1.0 collective-permute-done.2.swapped_ref
  110.1 11.7 %shard_map.105 = (f32[32,2048]{1,0:T(8,128)S(1)}, f32[8,2176]{1,0:T(8,128)S(1)}, f32[8,2176]{1,0:T(8,128)S(1)}, f32[8,128]{1,0:T(8,128)S(1)}, f32[64,64]{1,0:T(8,128)S(1)}) custom-call(s32[2]{0:T(128)} %pad_add_fusion.where_ref, f32[16,128]{1,0:T(8,128)S(1)} %psum.29.sums_ref, f32[16,128]{1,0:T(8,128)S(1)} %collective-permute-done.2.swapped_ref, ...), custom_call_target="tpu_custom_call" | custom-call | tf_op jit(solution)/shard_map/pallas_call | solution.py:30
  121.8 2.0 collective-permute-start.3
  123.8 5.2 %collective-permute-start.4 = (f32[8,2176]{1,0:T(8,128)S(1)}, f32[8,2176]{1,0:T(8,128)S(1)}, u32[]{:S(2)}, u32[]{:S(2)}) collective-permute-start(f32[8,2176]{1,0:T(8,128)S(1)} %get-tuple-element.25), channel_id=1, source_target_pairs={{8,0},{16,8},{24,16},{32,24},{40,32},{48,40},{56,48},{64,56},{72,6... | collective-permute-start | bytes 208904 | tf_op jit(solution)/shard_map/ppermute | solution.py:319
  128.9 0.0 copy-done
  128.9 0.1 dynamic-slice_bitcast_fusion
  129.0 0.1 copy.15.en_ref
  129.1 0.1 collective-permute-done.3.lo_ref
  129.2 1.6 collective-permute-done.4.hi_ref
  130.9 0.0 copy-start.1
  130.9 0.7 copy-done.1
  131.5 1.6 shard_map.106
  133.2 2.0 collective-permute-start.5
  135.1 5.5 %collective-permute-start.6 = (f32[8,2176]{1,0:T(8,128)S(1)}, f32[8,2176]{1,0:T(8,128)S(1)}, u32[]{:S(2)}, u32[]{:S(2)}) collective-permute-start(f32[8,2176]{1,0:T(8,128)S(1)} %get-tuple-element.29), channel_id=1, source_target_pairs={{8,0},{16,8},{24,16},{32,24},{40,32},{48,40},{56,48},{64,56},{72,6... | collective-permute-start | bytes 208904 | tf_op jit(solution)/shard_map/ppermute | solution.py:319
  141.3 0.0 collective-permute-done.5.lo_ref
  141.3 1.3 collective-permute-done.6.hi_ref
  142.6 3.9 %shard_map.107 = (f32[32,2048]{1,0:T(8,128)S(1)}, f32[8,128]{1,0:T(8,128)S(1)}) custom-call(f32[1]{0:T(128)S(6)} %copy.21.freq_ref, f32[32,2048]{1,0:T(8,128)S(1)} %get-tuple-element.26.v_ref.f_ref, f32[8,128]{1,0:T(8,128)S(1)} %get-tuple-element.27.pc_ref, f32[8,2176]{1,0:T(8,128)S(1)} %collective-permute-done.5.lo_ref, ...), custom_call_target="tpu_custom_call" | custom-call | tf_op jit(solution)/shard_map/pallas_call | solution.py:30
  146.4 9.5 %psum.30 = f32[8,128]{1,0:T(8,128)S(1)} all-reduce(f32[8,128]{1,0:T(8,128)S(1)} %get-tuple-element.30), channel_id=1, replica_groups={{0,8,16,24},{32,40,48,56},{64,72,80,88},{96,104,112,120},{128,136,144,1..., use_global_device_ids=true, to_apply=%region_3.4 | all-reduce | flops 1024 | bytes 8192 | tf_op jit(solution)/shard_map/psum | solution.py:312
  155.9 25.4 %psum.31.sums_ref = f32[8,128]{1,0:T(8,128)S(1)} all-reduce(f32[8,128]{1,0:T(8,128)S(1)} %psum.30), channel_id=1, replica_groups={{0,32,64,96,128,160,192,224},{8,40,72,104,136,168,200,232},{16,48,80,11..., use_global_device_ids=true, to_apply=%region_4.5 | all-reduce | flops 1024 | bytes 8192 | tf_op jit(solution)/shard_map/psum | solution.py:313
  181.3 3.5 %shard_map.108 = (f32[32,2048]{1,0:T(8,128)S(1)}, f32[8,2176]{1,0:T(8,128)S(1)}, f32[8,2176]{1,0:T(8,128)S(1)}, f32[8,128]{1,0:T(8,128)S(1)}) custom-call(f32[1]{0:T(128)S(6)} %copy.21.freq_ref, f32[8,128]{1,0:T(8,128)S(1)} %psum.31.sums_ref, f32[64,64]{1,0:T(8,128)S(1)} %get-tuple-element.31.inv_ref, f32[32,2048]{1,0:T(8,128)S(1)} %get-tuple-element.22.v_ref.r_ref, ...), custom_call_target="tpu_custom_call" | custom-call | tf_op jit(solution)/shard_map/pallas_call | solution.py:30
  184.9 2.1 collective-permute-start.7
  187.0 5.0 %collective-permute-start.8 = (f32[8,2176]{1,0:T(8,128)S(1)}, f32[8,2176]{1,0:T(8,128)S(1)}, u32[]{:S(2)}, u32[]{:S(2)}) collective-permute-start(f32[8,2176]{1,0:T(8,128)S(1)} %get-tuple-element.36), channel_id=1, source_target_pairs={{8,0},{16,8},{24,16},{32,24},{40,32},{48,40},{56,48},{64,56},{72,6... | collective-permute-start | bytes 208904 | tf_op jit(solution)/shard_map/ppermute | solution.py:319
  192.0 0.3 collective-permute-done.7.lo_ref
  192.3 1.6 collective-permute-done.8.hi_ref
  193.9 0.7 shard_map.109
  194.7 35.7 %all_to_all.16.lines_ref = f32[32,2,128]{2,1,0:T(2,128)S(1)} all-to-all(f32[32,2,128]{2,1,0:T(2,128)S(1)} %get-tuple-element.37), channel_id=1, replica_groups=mesh['parts'=2,'slab'=32,'orb'=4,'pen'=2] {'slab'}, dimensions={0} | all-to-all | bytes 65536 | tf_op jit(solution)/shard_map/all_to_all | solution.py:391
  230.4 1.9 shard_map.110
  232.2 2.0 collective-permute-start.9
  234.2 1.5 collective-permute-done.9
  235.7 0.6 broadcast_in_dim.5
  236.4 3.4 %all-to-all-start.2 = ((f32[4,4,1024]{2,1,0:T(4,128)}), f32[4,4,1024]{2,1,0:T(4,128)S(1)}, u32[]{:S(2)}, u32[]{:S(2)}) async-start(f32[4,4,1024]{2,1,0:T(4,128)} %broadcast_in_dim.5), calls=%async_computation.2 | async-start | bytes 131072 | tf_op jit(solution)/shard_map/all_to_all | solution.py:301
  239.8 0.9 reshape.76
  240.7 4.6 %all-to-all-done.2 = f32[4,4,1024]{2,1,0:T(4,128)S(1)} async-done(((f32[4,4,1024]{2,1,0:T(4,128)}), f32[4,4,1024]{2,1,0:T(4,128)S(1)}, u32[]{:S(2)}, u32[]{:S(2)}) %all-to-all-start.2) | async-done | bytes 65568 | tf_op jit(solution)/shard_map/all_to_all | solution.py:301
  245.3 0.6 mul.35
  (11 shorter events, 0.2 us)
Async XLA Ops:
  0.6 128.3 %copy-start = (f32[16]{0:T(128)S(1)}, f32[16]{0:T(128)}, u32[]{:S(2)}) copy-start(f32[16]{0:T(128)} %param.10) | copy-start | bytes 196
  1.8 21.7 %copy-start.4 = (f32[4,4,256]{2,1,0:T(4,128)S(1)}, f32[4,4,256]{2,1,0:T(4,128)}, u32[]{:S(2)}) copy-start(f32[4,4,256]{2,1,0:T(4,128)} %param.12) | copy-start | bytes 49156
  1.8 22.4 %copy-start.3 = (f32[128,4,256]{2,1,0:T(4,128)S(1)}, f32[128,4,256]{2,1,0:T(4,128)}, u32[]{:S(2)}) copy-start(f32[128,4,256]{2,1,0:T(4,128)} %param.14) | copy-start | bytes 1572868
  21.5 2.8 %copy-start.2 = (f32[4,16,4096]{2,1,0:T(8,128)}, f32[4,16,4096]{2,1,0:T(8,128)S(1)}, u32[]{:S(2)}) copy-start(f32[4,16,4096]{2,1,0:T(8,128)S(1)} %all_to_all.15) | copy-start | bytes 3145732
  21.5 6.9 %collective-permute-start = (f32[64,4096]{1,0:T(8,128)S(1)}, f32[64,4096]{1,0:T(8,128)}, u32[]{:S(2)}, u32[]{:S(2)}) collective-permute-start(f32[64,4096]{1,0:T(8,128)S(1)} %bitcast.15), channel_id=1, source_target_pairs={{0,1},{1,0},{2,3},{3,2},{4,5},{5,4},{6,7},{7,6},{8,9},{9,8},{10,11... | collective-permute-start | bytes 3145736 | tf_op jit(solution)/shard_map/ppermute | solution.py:305
  23.5 0.7 copy-start.5
  24.4 4.0 %collective-permute-start.1 = (f32[136,1024]{1,0:T(8,128)S(1)}, f32[136,1024]{1,0:T(8,128)S(1)}, u32[]{:S(2)}, u32[]{:S(2)}) collective-permute-start(f32[136,1024]{1,0:T(8,128)S(1)} %pad_maximum_fusion.stat_m), channel_id=1, source_target_pairs={{0,1},{1,0},{2,3},{3,2},{4,5},{5,4},{6,7},{7,6},{8,9},{9,8},{10,11... | collective-permute-start | bytes 1671176 | tf_op jit(solution)/shard_map/ppermute | solution.py:305
  26.8 0.7 copy-start.7
  47.6 61.4 %copy-start.6 = (f32[128,5]{0,1:T(8,128)S(1)}, f32[128,5]{0,1:T(8,128)}, u32[]{:S(2)}) copy-start(f32[128,5]{0,1:T(8,128)} %param.15) | copy-start | bytes 7684
  107.0 3.1 %collective-permute-start.2 = (f32[16,128]{1,0:T(8,128)S(1)}, f32[16,128]{1,0:T(8,128)S(1)}, u32[]{:S(2)}, u32[]{:S(2)}) collective-permute-start(f32[16,128]{1,0:T(8,128)S(1)} %psum.29.sums_ref), channel_id=1, source_target_pairs={{0,1},{1,0},{2,3},{3,2},{4,5},{5,4},{6,7},{7,6},{8,9},{9,8},{10,11... | collective-permute-start | bytes 24584 | tf_op jit(solution)/shard_map/ppermute | solution.py:305
  121.8 7.4 %collective-permute-start.3 = (f32[8,2176]{1,0:T(8,128)S(1)}, f32[8,2176]{1,0:T(8,128)S(1)}, u32[]{:S(2)}, u32[]{:S(2)}) collective-permute-start(f32[8,2176]{1,0:T(8,128)S(1)} %get-tuple-element.24), channel_id=1, source_target_pairs={{0,8},{8,16},{16,24},{24,32},{32,40},{40,48},{48,56},{56,64},{64,7... | collective-permute-start | bytes 208904 | tf_op jit(solution)/shard_map/ppermute | solution.py:319
  123.8 7.1 %collective-permute-start.4 = (f32[8,2176]{1,0:T(8,128)S(1)}, f32[8,2176]{1,0:T(8,128)S(1)}, u32[]{:S(2)}, u32[]{:S(2)}) collective-permute-start(f32[8,2176]{1,0:T(8,128)S(1)} %get-tuple-element.25), channel_id=1, source_target_pairs={{8,0},{16,8},{24,16},{32,24},{40,32},{48,40},{56,48},{64,56},{72,6... | collective-permute-start | bytes 208904 | tf_op jit(solution)/shard_map/ppermute | solution.py:319
  130.9 0.7 copy-start.1
  133.2 8.1 %collective-permute-start.5 = (f32[8,2176]{1,0:T(8,128)S(1)}, f32[8,2176]{1,0:T(8,128)S(1)}, u32[]{:S(2)}, u32[]{:S(2)}) collective-permute-start(f32[8,2176]{1,0:T(8,128)S(1)} %get-tuple-element.28), channel_id=1, source_target_pairs={{0,8},{8,16},{16,24},{24,32},{32,40},{40,48},{48,56},{56,64},{64,7... | collective-permute-start | bytes 208904 | tf_op jit(solution)/shard_map/ppermute | solution.py:319
  135.1 7.4 %collective-permute-start.6 = (f32[8,2176]{1,0:T(8,128)S(1)}, f32[8,2176]{1,0:T(8,128)S(1)}, u32[]{:S(2)}, u32[]{:S(2)}) collective-permute-start(f32[8,2176]{1,0:T(8,128)S(1)} %get-tuple-element.29), channel_id=1, source_target_pairs={{8,0},{16,8},{24,16},{32,24},{40,32},{48,40},{56,48},{64,56},{72,6... | collective-permute-start | bytes 208904 | tf_op jit(solution)/shard_map/ppermute | solution.py:319
  184.9 7.4 %collective-permute-start.7 = (f32[8,2176]{1,0:T(8,128)S(1)}, f32[8,2176]{1,0:T(8,128)S(1)}, u32[]{:S(2)}, u32[]{:S(2)}) collective-permute-start(f32[8,2176]{1,0:T(8,128)S(1)} %get-tuple-element.35), channel_id=1, source_target_pairs={{0,8},{8,16},{16,24},{24,32},{32,40},{40,48},{48,56},{56,64},{64,7... | collective-permute-start | bytes 208904 | tf_op jit(solution)/shard_map/ppermute | solution.py:319
  187.0 6.9 %collective-permute-start.8 = (f32[8,2176]{1,0:T(8,128)S(1)}, f32[8,2176]{1,0:T(8,128)S(1)}, u32[]{:S(2)}, u32[]{:S(2)}) collective-permute-start(f32[8,2176]{1,0:T(8,128)S(1)} %get-tuple-element.36), channel_id=1, source_target_pairs={{8,0},{16,8},{24,16},{32,24},{40,32},{48,40},{56,48},{64,56},{72,6... | collective-permute-start | bytes 208904 | tf_op jit(solution)/shard_map/ppermute | solution.py:319
  232.2 3.5 %collective-permute-start.9 = (f32[16,4096]{1,0:T(8,128)S(1)}, f32[16,4096]{1,0:T(8,128)S(1)}, u32[]{:S(2)}, u32[]{:S(2)}) collective-permute-start(f32[16,4096]{1,0:T(8,128)S(1)} %get-tuple-element.40), channel_id=1, source_target_pairs={{0,1},{1,0},{2,3},{3,2},{4,5},{5,4},{6,7},{7,6},{8,9},{9,8},{10,11... | collective-permute-start | bytes 786440 | tf_op jit(solution)/shard_map/ppermute | solution.py:305
  236.4 8.9 %all-to-all-start.2 = ((f32[4,4,1024]{2,1,0:T(4,128)}), f32[4,4,1024]{2,1,0:T(4,128)S(1)}, u32[]{:S(2)}, u32[]{:S(2)}) async-start(f32[4,4,1024]{2,1,0:T(4,128)} %broadcast_in_dim.5), calls=%async_computation.2 | async-start | bytes 131072 | tf_op jit(solution)/shard_map/all_to_all | solution.py:301

commit v3 on v2

--- a/solution.py
+++ b/solution.py
@@ -54,12 +54,16 @@
     return sum(sums[z * own : (z + 1) * own] * w_ref[z : z + 1, :] for z in range(planes))
 
 
-def pack_edges(v_ref, pc, up_ref, down_ref, own):
+def pack_edges(where_ref, v_ref, pc, up_ref, down_ref, own):
     width = v_ref.shape[1]
-    up_ref[:, 0:width] = v_ref[v_ref.shape[0] - own :, :]
-    up_ref[:, width:] = pc
-    down_ref[:, 0:width] = v_ref[0:own, :]
-    down_ref[:, width:] = pc
+    half = width // 2
+    for ref, edge, crossing in (
+        (up_ref, v_ref[v_ref.shape[0] - own :, :], where_ref[2] == 1),
+        (down_ref, v_ref[0:own, :], where_ref[3] == 1),
+    ):
+        ref[:, 0:half] = jnp.where(crossing, edge[:, half:], edge[:, 0:half])
+        ref[:, half:width] = jnp.where(crossing, edge[:, 0:half], edge[:, half:])
+        ref[:, width:] = pc
 
 
 def apply_shift(emit, v_ref, pc_ref, lo_ref, hi_ref, stat_refs, w_ref, coup_ref, en_ref, cols):
@@ -182,11 +186,11 @@
             r_ref[z * own : (z + 1) * own, h * half : (h + 1) * half] = dot_nn(g, orb_ref[:, at]) - source
     pc = inner_partials(r_ref, (stat_m, stat_o), w_ref, own, natoms)
     pc_ref[...] = pc
-    pack_edges(r_ref, pc, up_ref, down_ref, own)
+    pack_edges(where_ref, r_ref, pc, up_ref, down_ref, own)
 
 
 def first_body(
-    v_ref, pc_ref, lo_ref, hi_ref, stat_m, stat_o, w_ref, coup_ref, en_ref,
+    where_ref, v_ref, pc_ref, lo_ref, hi_ref, stat_m, stat_o, w_ref, coup_ref, en_ref,
     f_ref, up_ref, down_ref, out_pc_ref, *, own, natoms, cols,
 ):
     def emit(at, block):
@@ -195,7 +199,7 @@
     apply_shift(emit, v_ref, pc_ref, lo_ref, hi_ref, (stat_m, stat_o), w_ref, coup_ref, en_ref, cols)
     pc = inner_partials(f_ref, (stat_m, stat_o), w_ref, own, natoms)
     out_pc_ref[...] = pc
-    pack_edges(f_ref, pc, up_ref, down_ref, own)
+    pack_edges(where_ref, f_ref, pc, up_ref, down_ref, own)
 
 
 def target_body(
@@ -224,7 +228,7 @@
 
 
 def residual_body(
-    freq_ref, sums_ref, inv_ref, r_ref, t_ref, mine_ref, other_ref, stat_m, stat_o, w_ref,
+    where_ref, freq_ref, sums_ref, inv_ref, r_ref, t_ref, mine_ref, other_ref, stat_m, stat_o, w_ref,
     out_ref, up_ref, down_ref, pc_ref, *, own, planes, natoms, cells,
 ):
     half = stat_m.shape[1]
@@ -240,7 +244,7 @@
             out_ref[rows, at] = r_ref[rows, at] - step * image
     pc = inner_partials(out_ref, (stat_m, stat_o), w_ref, own, natoms)
     pc_ref[...] = pc
-    pack_edges(out_ref, pc, up_ref, down_ref, own)
+    pack_edges(where_ref, out_ref, pc, up_ref, down_ref, own)
 
 
 def last_body(
@@ -254,12 +258,11 @@
     values = [
         orbital_row_sums([a * b for a, b in zip(x, y)], own) for x, y in ((r1, r1), (u1, u1), (u1, u0), (r1, r0))
     ]
-    lanes = out_ref.shape[2]
+    lanes = out_ref.shape[1]
     lane = lax.broadcasted_iota(jnp.int32, (own, lanes), 1)
     row = lax.broadcasted_iota(jnp.int32, (own, lanes), 0)
     placed = sum(jnp.where(lane == own * s + row, value, 0.0) for s, value in enumerate(values))
-    line = jnp.sum(placed, axis=0, keepdims=True)
-    out_ref[...] = jnp.broadcast_to(line[None], out_ref.shape)
+    out_ref[...] = jnp.sum(placed, axis=0, keepdims=True)
 
 
 def response_body(
@@ -269,7 +272,7 @@
     half = f_ref.shape[1] // 2
     square = freq_ref[0] * freq_ref[0]
     rr0, ff = sums_ref[:, total : total + 1], sums_ref[:, total + 1 : total + 2]
-    line = jnp.sum(lines_ref[...], axis=0)[0:1, :]
+    line = lines_ref[...]
     lanes = line.shape[1]
     lane = lax.broadcasted_iota(jnp.int32, (own, lanes), 1)
     row = lax.broadcasted_iota(jnp.int32, (own, lanes), 0)
@@ -305,18 +308,27 @@
     return lax.ppermute(array, "pen", [(0, 1), (1, 0)])
 
 
+def turn(slab):
+    return (slab + slab // NEAR) % 2
+
+
+def place(slab, part):
+    return 2 * slab + (part + turn(slab)) % 2
+
+
 def summed(array):
     count = lax.axis_size("slab")
-    runs = [[i + j for j in range(NEAR)] for i in range(0, count, NEAR)]
-    across = [[i + j for i in range(0, count, NEAR)] for j in range(NEAR)]
-    array = lax.psum(array, "slab", axis_index_groups=runs)
-    return lax.psum(array, "slab", axis_index_groups=across)
+    runs = [[place(i + j, part) for j in range(NEAR)] for part in range(2) for i in range(0, count, NEAR)]
+    across = [[place(i + j, part) for i in range(0, count, NEAR)] for part in range(2) for j in range(NEAR)]
+    array = lax.psum(array, ("slab", "pen"), axis_index_groups=runs)
+    return lax.psum(array, ("slab", "pen"), axis_index_groups=across)
 
 
 def from_neighbours(up, down):
     count = lax.axis_size("slab")
-    ring = [(i, (i + 1) % count) for i in range(count)]
-    return lax.ppermute(up, "slab", ring), lax.ppermute(down, "slab", [(b, a) for a, b in ring])
+    ring = [(place(i, part), place((i + 1) % count, part)) for i in range(count) for part in range(2)]
+    axes = ("slab", "pen")
+    return lax.ppermute(up, axes, ring), lax.ppermute(down, axes, [(b, a) for a, b in ring])
 
 
 def plane_weights(atom_planes, profiles, planes, depth_total):
@@ -338,10 +350,12 @@
     depth_total = planes * slabs
     cells = float(depth_total * 2 * half)
     own = chip_count // 2
-    core = lax.axis_index("pen")
-    first_plane = lax.axis_index("slab") * planes
+    slab = lax.axis_index("slab")
+    core = (lax.axis_index("pen") + turn(slab)) % 2
+    crossings = [(turn(slab) + turn((slab + step) % slabs)) % 2 for step in (1, slabs - 1)]
+    first_plane = slab * planes
     weights = plane_weights(atom_planes, profiles, first_plane + jnp.arange(planes, dtype=jnp.int32), depth_total)
-    where = jnp.stack([lax.axis_index("orb") * chip_count + core * own, core]).astype(jnp.int32)
+    where = jnp.stack([lax.axis_index("orb") * chip_count + core * own, core, *crossings]).astype(jnp.int32)
     own_energies = lax.dynamic_slice(energies, (core * own,), (own,)).reshape(own, 1)
     coup = couplings.reshape(1, natoms)
 
@@ -369,7 +383,7 @@
     lo, hi = from_neighbours(up, down)
     first, up, down, first_pc = call(
         functools.partial(first_body, own=own, natoms=natoms, cols=cols),
-        (r0, pc, lo, hi, *stats, weights, coup, own_energies), "kkkkkkkkk", [field, edge, edge, part],
+        (where, r0, pc, lo, hi, *stats, weights, coup, own_energies), "skkkkkkkkk", [field, edge, edge, part],
     )
     lo, hi = from_neighbours(up, down)
     target, sums_part = call(
@@ -380,15 +394,15 @@
     sums = summed(sums_part)
     r1, up, down, pc = call(
         functools.partial(residual_body, own=own, planes=planes, natoms=natoms, cells=cells),
-        (frequency, sums, inv, r0, target, mine, other, *stats, weights), "skkkkvvkkk", [field, edge, edge, part],
+        (where, frequency, sums, inv, r0, target, mine, other, *stats, weights), "sskkkkvvkkk", [field, edge, edge, part],
     )
     lo, hi = from_neighbours(up, down)
     last, lines = call(
         functools.partial(last_body, own=own, cols=cols),
         (r1, pc, lo, hi, *stats, weights, coup, own_energies, r0, first), "kkkkkkkkkkk",
-        [field, (slabs, 2, 2 * total)],
-    )
-    lines = lax.all_to_all(lines, "slab", split_axis=0, concat_axis=0, tiled=True)
+        [field, (1, 2 * total)],
+    )
+    lines = summed(lines)
     response, to_other, dens = call(
         functools.partial(response_body, own=own, planes=planes),
         (where, frequency, sums, lines, first, last, mine, other), "sskkkkvv",

time: 247 us -> 238 us (0.964)
  blocking collectives: 165 us -> 156 us
    all_to_all x1 -> x0, blocking collectives: 35.7 us -> none  [on_device(): lax.all_to_all(lines, 'slab', split_axis=0, concat_axis=0, tiled=True)]
    psum x4 -> x6, blocking collectives: 110 us -> 136 us  [the longest x3 106 us: summed(): return lax.psum(array, ('slab', 'pen'), axis_index_groups=across)]
where the time goes in v3:
time: 238 us; the launch traced here: 237 us
  blocking collectives  156 us (66%)
  starting transfers between devices  33.7 us (14%)
  Pallas kernels  27.5 us (12%)
  waiting for transfers between devices  12.4 us (5%)
  local copies, waits for them, and re-layouts  5.01 us (2%)
    psum x3, blocking collectives, summed(): return lax.psum(array, ('slab', 'pen'), axis_index_groups=across)  106 us
    psum x3, blocking collectives, summed(): array = lax.psum(array, ('slab', 'pen'), axis_index_groups=runs)  30 us
    pallas_call x7, Pallas kernels, call(): pl.pallas_call(body, in_specs=[SMEM if k == 's' else VMEM for k in kinds]...  27.5 us
    all_to_all x1, blocking collectives, copy_for_each(): return lax.all_to_all(copies, axis, split_axis=0, concat_axis=0, tiled=True)  19.7 us
    ppermute x3, starting transfers between devices, from_neighbours(): lax.ppermute(down, axes, [(b, a) for a, b in ring])  15.8 us
    ppermute x4, starting transfers between devices, swap_cores(): return lax.ppermute(array, 'pen', [(0, 1), (1, 0)])  8.64 us
    ppermute x3, starting transfers between devices, from_neighbours(): lax.ppermute(up, axes, ring)  5.86 us
  transfers between devices with their start and end apart: 11, of which 9 were waited for; matrix products, arithmetic and copies ran while one was open for 1% of the time, Pallas kernels for 0%

profile of v3, /device:TPU:40, one launch (start us, length us, event | category | flops | bytes accessed | tf_op | source)
XLA Modules:
  0.0 237.2 jit_solution(14988031813593912873)
XLA Ops:
  0.6 0.0 copy-start
  0.6 1.1 reshape.69
  1.7 0.1 broadcast_in_dim.4
  1.8 0.0 copy-start.4
  1.8 0.0 copy-start.3
  1.8 19.7 %all_to_all.10 = f32[4,16,4096]{2,1,0:T(8,128)S(1)} all-to-all(f32[4,16,4096]{2,1,0:T(8,128)S(1)} %broadcast_in_dim.4), channel_id=1, replica_groups=mesh['parts'=2,'slab'=32,'orb'=4,'pen'=2] {'orb'}, dimensions={0} | all-to-all | bytes 2097152 | tf_op jit(solution)/shard_map/all_to_all | solution.py:304
  21.5 0.0 copy-start.2
  21.5 1.9 collective-permute-start
  23.5 0.0 copy-done.4
  23.5 0.0 copy-start.5
  23.5 0.7 copy-done.5
  24.2 0.0 copy-done.3
  24.2 0.1 copy.18
  24.4 0.0 copy-done.2
  24.4 2.4 %collective-permute-start.1 = (f32[136,1024]{1,0:T(8,128)S(1)}, f32[136,1024]{1,0:T(8,128)S(1)}, u32[]{:S(2)}, u32[]{:S(2)}) collective-permute-start(f32[136,1024]{1,0:T(8,128)S(1)} %pad_maximum_fusion.stat_m), channel_id=1, source_target_pairs={{0,1},{1,0},{2,3},{3,2},{4,5},{5,4},{6,7},{7,6},{8,9},{9,8},{10,11... | collective-permute-start | bytes 1671176 | tf_op jit(solution)/shard_map/ppermute | solution.py:308
  27.0 0.0 copy-start.7
  27.0 0.6 pad_add_fusion.where_ref
  27.6 0.0 copy-done.7
  27.7 0.7 collective-permute-done.1.stat_o
  28.4 0.0 collective-permute-done.other_ref
  28.4 3.5 %shard_map.104 = f32[16,128]{1,0:T(8,128)S(1)} custom-call(s32[4]{0:T(128)} %pad_add_fusion.where_ref, f32[64,4096]{1,0:T(8,128)} %bitcast.18, f32[64,4096]{1,0:T(8,128)} %collective-permute-done.other_ref, f32[136,1024]{1,0:T(8,128)S(1)} %pad_maximum_fusion.stat_m, f32[136,1024]{1,0:T(8,128)S(1)} %collective-permute-done.1.stat_o), custom_call_target="tpu_custom_call" | custom-call | tf_op jit(solution)/shard_map/pallas_call | solution.py:30
  31.9 14.9 %psum.42 = f32[16,128]{1,0:T(8,128)S(1)} all-reduce(f32[16,128]{1,0:T(8,128)S(1)} %shard_map.104), channel_id=1, replica_groups={{0,9,16,25},{33,40,49,56},{64,73,80,89},{97,104,113,120},{128,137,144,1..., use_global_device_ids=true, to_apply=%region_0.1 | all-reduce | flops 2048 | bytes 16384 | tf_op jit(solution)/shard_map/psum | solution.py:323
  46.7 0.0 copy-start.6
  46.8 57.3 %psum.43.sums_ref = f32[16,128]{1,0:T(8,128)S(1)} all-reduce(f32[16,128]{1,0:T(8,128)S(1)} %psum.42), channel_id=1, replica_groups={{0,33,64,97,128,161,192,225},{9,40,73,104,137,168,201,232},{16,49,80,11..., use_global_device_ids=true, to_apply=%region_1.2 | all-reduce | flops 2048 | bytes 16384 | tf_op jit(solution)/shard_map/psum | solution.py:324
  104.1 2.3 collective-permute-start.2
  106.4 0.0 copy-done.6
  106.4 0.1 select_reduce_fusion.w_ref
  106.5 0.7 collective-permute-done.2.swapped_ref
  107.2 11.7 %shard_map.105 = (f32[32,2048]{1,0:T(8,128)S(1)}, f32[8,2176]{1,0:T(8,128)S(1)}, f32[8,2176]{1,0:T(8,128)S(1)}, f32[8,128]{1,0:T(8,128)S(1)}, f32[64,64]{1,0:T(8,128)S(1)}) custom-call(s32[4]{0:T(128)} %pad_add_fusion.where_ref, f32[16,128]{1,0:T(8,128)S(1)} %psum.43.sums_ref, f32[16,128]{1,0:T(8,128)S(1)} %collective-permute-done.2.swapped_ref, ...), custom_call_target="tpu_custom_call" | custom-call | tf_op jit(solution)/shard_map/pallas_call | solution.py:30
  118.9 2.0 collective-permute-start.3
  120.8 5.2 %collective-permute-start.4 = (f32[8,2176]{1,0:T(8,128)S(1)}, f32[8,2176]{1,0:T(8,128)S(1)}, u32[]{:S(2)}, u32[]{:S(2)}) collective-permute-start(f32[8,2176]{1,0:T(8,128)S(1)} %get-tuple-element.25), channel_id=1, source_target_pairs={{9,0},{8,1},{16,9},{17,8},{25,16},{24,17},{33,25},{32,24},{40,33},... | collective-permute-start | bytes 208904 | tf_op jit(solution)/shard_map/ppermute | solution.py:331
  126.0 0.0 copy-done
  126.0 0.1 dynamic-slice_bitcast_fusion
  126.1 0.1 copy.15.en_ref
  126.2 0.3 collective-permute-done.3.lo_ref
  126.4 1.5 collective-permute-done.4.hi_ref
  127.9 0.0 copy-start.1
  127.9 0.7 copy-done.1
  128.6 2.3 shard_map.106
  130.9 2.0 collective-permute-start.5
  132.9 5.5 %collective-permute-start.6 = (f32[8,2176]{1,0:T(8,128)S(1)}, f32[8,2176]{1,0:T(8,128)S(1)}, u32[]{:S(2)}, u32[]{:S(2)}) collective-permute-start(f32[8,2176]{1,0:T(8,128)S(1)} %get-tuple-element.29), channel_id=1, source_target_pairs={{9,0},{8,1},{16,9},{17,8},{25,16},{24,17},{33,25},{32,24},{40,33},... | collective-permute-start | bytes 208904 | tf_op jit(solution)/shard_map/ppermute | solution.py:331
  139.0 0.0 collective-permute-done.5.lo_ref
  139.0 1.3 collective-permute-done.6.hi_ref
  140.3 3.9 %shard_map.107 = (f32[32,2048]{1,0:T(8,128)S(1)}, f32[8,128]{1,0:T(8,128)S(1)}) custom-call(f32[1]{0:T(128)S(6)} %copy.21.freq_ref, f32[32,2048]{1,0:T(8,128)S(1)} %get-tuple-element.26.v_ref.f_ref, f32[8,128]{1,0:T(8,128)S(1)} %get-tuple-element.27.pc_ref, f32[8,2176]{1,0:T(8,128)S(1)} %collective-permute-done.5.lo_ref, ...), custom_call_target="tpu_custom_call" | custom-call | tf_op jit(solution)/shard_map/pallas_call | solution.py:30
  144.2 7.6 %psum.44 = f32[8,128]{1,0:T(8,128)S(1)} all-reduce(f32[8,128]{1,0:T(8,128)S(1)} %get-tuple-element.30), channel_id=1, replica_groups={{0,9,16,25},{33,40,49,56},{64,73,80,89},{97,104,113,120},{128,137,144,1..., use_global_device_ids=true, to_apply=%region_3.4 | all-reduce | flops 1024 | bytes 8192 | tf_op jit(solution)/shard_map/psum | solution.py:323
  151.8 24.5 %psum.45.sums_ref = f32[8,128]{1,0:T(8,128)S(1)} all-reduce(f32[8,128]{1,0:T(8,128)S(1)} %psum.44), channel_id=1, replica_groups={{0,33,64,97,128,161,192,225},{9,40,73,104,137,168,201,232},{16,49,80,11..., use_global_device_ids=true, to_apply=%region_4.5 | all-reduce | flops 1024 | bytes 8192 | tf_op jit(solution)/shard_map/psum | solution.py:324
  176.3 3.5 %shard_map.108 = (f32[32,2048]{1,0:T(8,128)S(1)}, f32[8,2176]{1,0:T(8,128)S(1)}, f32[8,2176]{1,0:T(8,128)S(1)}, f32[8,128]{1,0:T(8,128)S(1)}) custom-call(s32[4]{0:T(128)} %pad_add_fusion.where_ref, f32[1]{0:T(128)S(6)} %copy.21.freq_ref, f32[8,128]{1,0:T(8,128)S(1)} %psum.45.sums_ref, f32[64,64]{1,0:T(8,128)S(1)} %get-tuple-element.31.inv_ref, ...), custom_call_target="tpu_custom_call" | custom-call | tf_op jit(solution)/shard_map/pallas_call | solution.py:30
  179.9 2.0 collective-permute-start.7
  181.8 5.2 %collective-permute-start.8 = (f32[8,2176]{1,0:T(8,128)S(1)}, f32[8,2176]{1,0:T(8,128)S(1)}, u32[]{:S(2)}, u32[]{:S(2)}) collective-permute-start(f32[8,2176]{1,0:T(8,128)S(1)} %get-tuple-element.36), channel_id=1, source_target_pairs={{9,0},{8,1},{16,9},{17,8},{25,16},{24,17},{33,25},{32,24},{40,33},... | collective-permute-start | bytes 208904 | tf_op jit(solution)/shard_map/ppermute | solution.py:331
  187.0 0.3 collective-permute-done.7.lo_ref
  187.3 1.6 collective-permute-done.8.hi_ref
  188.9 0.7 shard_map.109
  189.7 7.6 %psum.46 = f32[1,128]{1,0:T(1,128)S(1)} all-reduce(f32[1,128]{1,0:T(1,128)S(1)} %get-tuple-element.37), channel_id=1, replica_groups={{0,9,16,25},{33,40,49,56},{64,73,80,89},{97,104,113,120},{128,137,144,1..., use_global_device_ids=true, to_apply=%region_5.6 | all-reduce | flops 128 | bytes 1024 | tf_op jit(solution)/shard_map/psum | solution.py:323
  197.2 24.4 %psum.47.lines_ref = f32[1,128]{1,0:T(1,128)S(1)} all-reduce(f32[1,128]{1,0:T(1,128)S(1)} %psum.46), channel_id=1, replica_groups={{0,33,64,97,128,161,192,225},{9,40,73,104,137,168,201,232},{16,49,80,11..., use_global_device_ids=true, to_apply=%region_6.7 | all-reduce | flops 128 | bytes 1024 | tf_op jit(solution)/shard_map/psum | solution.py:324
  221.6 1.9 shard_map.110
  223.4 2.0 collective-permute-start.9
  225.4 1.5 collective-permute-done.9
  227.0 0.6 broadcast_in_dim.5
  227.6 3.4 %all-to-all-start.1 = ((f32[4,4,1024]{2,1,0:T(4,128)}), f32[4,4,1024]{2,1,0:T(4,128)S(1)}, u32[]{:S(2)}, u32[]{:S(2)}) async-start(f32[4,4,1024]{2,1,0:T(4,128)} %broadcast_in_dim.5), calls=%async_computation.1 | async-start | bytes 131072 | tf_op jit(solution)/shard_map/all_to_all | solution.py:304
  231.0 0.9 reshape.76
  231.9 4.6 %all-to-all-done.1 = f32[4,4,1024]{2,1,0:T(4,128)S(1)} async-done(((f32[4,4,1024]{2,1,0:T(4,128)}), f32[4,4,1024]{2,1,0:T(4,128)S(1)}, u32[]{:S(2)}, u32[]{:S(2)}) %all-to-all-start.1) | async-done | bytes 65568 | tf_op jit(solution)/shard_map/all_to_all | solution.py:304
  236.5 0.6 mul.35
  (11 shorter events, 0.2 us)
Async XLA Ops:
  0.6 125.4 %copy-start = (f32[16]{0:T(128)S(1)}, f32[16]{0:T(128)}, u32[]{:S(2)}) copy-start(f32[16]{0:T(128)} %param.10) | copy-start | bytes 196
  1.8 21.7 %copy-start.4 = (f32[4,4,256]{2,1,0:T(4,128)S(1)}, f32[4,4,256]{2,1,0:T(4,128)}, u32[]{:S(2)}) copy-start(f32[4,4,256]{2,1,0:T(4,128)} %param.12) | copy-start | bytes 49156
  1.8 22.4 %copy-start.3 = (f32[128,4,256]{2,1,0:T(4,128)S(1)}, f32[128,4,256]{2,1,0:T(4,128)}, u32[]{:S(2)}) copy-start(f32[128,4,256]{2,1,0:T(4,128)} %param.14) | copy-start | bytes 1572868
  21.5 2.8 %copy-start.2 = (f32[4,16,4096]{2,1,0:T(8,128)}, f32[4,16,4096]{2,1,0:T(8,128)S(1)}, u32[]{:S(2)}) copy-start(f32[4,16,4096]{2,1,0:T(8,128)S(1)} %all_to_all.10) | copy-start | bytes 3145732
  21.5 6.9 %collective-permute-start = (f32[64,4096]{1,0:T(8,128)S(1)}, f32[64,4096]{1,0:T(8,128)}, u32[]{:S(2)}, u32[]{:S(2)}) collective-permute-start(f32[64,4096]{1,0:T(8,128)S(1)} %bitcast.17), channel_id=1, source_target_pairs={{0,1},{1,0},{2,3},{3,2},{4,5},{5,4},{6,7},{7,6},{8,9},{9,8},{10,11... | collective-permute-start | bytes 3145736 | tf_op jit(solution)/shard_map/ppermute | solution.py:308
  23.5 0.7 copy-start.5
  24.4 4.0 %collective-permute-start.1 = (f32[136,1024]{1,0:T(8,128)S(1)}, f32[136,1024]{1,0:T(8,128)S(1)}, u32[]{:S(2)}, u32[]{:S(2)}) collective-permute-start(f32[136,1024]{1,0:T(8,128)S(1)} %pad_maximum_fusion.stat_m), channel_id=1, source_target_pairs={{0,1},{1,0},{2,3},{3,2},{4,5},{5,4},{6,7},{7,6},{8,9},{9,8},{10,11... | collective-permute-start | bytes 1671176 | tf_op jit(solution)/shard_map/ppermute | solution.py:308
  27.0 0.7 copy-start.7
  46.7 59.7 %copy-start.6 = (f32[128,5]{0,1:T(8,128)S(1)}, f32[128,5]{0,1:T(8,128)}, u32[]{:S(2)}) copy-start(f32[128,5]{0,1:T(8,128)} %param.15) | copy-start | bytes 7684
  104.1 3.1 %collective-permute-start.2 = (f32[16,128]{1,0:T(8,128)S(1)}, f32[16,128]{1,0:T(8,128)S(1)}, u32[]{:S(2)}, u32[]{:S(2)}) collective-permute-start(f32[16,128]{1,0:T(8,128)S(1)} %psum.43.sums_ref), channel_id=1, source_target_pairs={{0,1},{1,0},{2,3},{3,2},{4,5},{5,4},{6,7},{7,6},{8,9},{9,8},{10,11... | collective-permute-start | bytes 24584 | tf_op jit(solution)/shard_map/ppermute | solution.py:308
  118.9 7.6 %collective-permute-start.3 = (f32[8,2176]{1,0:T(8,128)S(1)}, f32[8,2176]{1,0:T(8,128)S(1)}, u32[]{:S(2)}, u32[]{:S(2)}) collective-permute-start(f32[8,2176]{1,0:T(8,128)S(1)} %get-tuple-element.24), channel_id=1, source_target_pairs={{0,9},{1,8},{9,16},{8,17},{16,25},{17,24},{25,33},{24,32},{33,40},... | collective-permute-start | bytes 208904 | tf_op jit(solution)/shard_map/ppermute | solution.py:331
  120.8 7.1 %collective-permute-start.4 = (f32[8,2176]{1,0:T(8,128)S(1)}, f32[8,2176]{1,0:T(8,128)S(1)}, u32[]{:S(2)}, u32[]{:S(2)}) collective-permute-start(f32[8,2176]{1,0:T(8,128)S(1)} %get-tuple-element.25), channel_id=1, source_target_pairs={{9,0},{8,1},{16,9},{17,8},{25,16},{24,17},{33,25},{32,24},{40,33},... | collective-permute-start | bytes 208904 | tf_op jit(solution)/shard_map/ppermute | solution.py:331
  127.9 0.7 copy-start.1
  130.9 8.1 %collective-permute-start.5 = (f32[8,2176]{1,0:T(8,128)S(1)}, f32[8,2176]{1,0:T(8,128)S(1)}, u32[]{:S(2)}, u32[]{:S(2)}) collective-permute-start(f32[8,2176]{1,0:T(8,128)S(1)} %get-tuple-element.28), channel_id=1, source_target_pairs={{0,9},{1,8},{9,16},{8,17},{16,25},{17,24},{25,33},{24,32},{33,40},... | collective-permute-start | bytes 208904 | tf_op jit(solution)/shard_map/ppermute | solution.py:331
  132.9 7.4 %collective-permute-start.6 = (f32[8,2176]{1,0:T(8,128)S(1)}, f32[8,2176]{1,0:T(8,128)S(1)}, u32[]{:S(2)}, u32[]{:S(2)}) collective-permute-start(f32[8,2176]{1,0:T(8,128)S(1)} %get-tuple-element.29), channel_id=1, source_target_pairs={{9,0},{8,1},{16,9},{17,8},{25,16},{24,17},{33,25},{32,24},{40,33},... | collective-permute-start | bytes 208904 | tf_op jit(solution)/shard_map/ppermute | solution.py:331
  179.9 7.4 %collective-permute-start.7 = (f32[8,2176]{1,0:T(8,128)S(1)}, f32[8,2176]{1,0:T(8,128)S(1)}, u32[]{:S(2)}, u32[]{:S(2)}) collective-permute-start(f32[8,2176]{1,0:T(8,128)S(1)} %get-tuple-element.35), channel_id=1, source_target_pairs={{0,9},{1,8},{9,16},{8,17},{16,25},{17,24},{25,33},{24,32},{33,40},... | collective-permute-start | bytes 208904 | tf_op jit(solution)/shard_map/ppermute | solution.py:331
  181.8 7.1 %collective-permute-start.8 = (f32[8,2176]{1,0:T(8,128)S(1)}, f32[8,2176]{1,0:T(8,128)S(1)}, u32[]{:S(2)}, u32[]{:S(2)}) collective-permute-start(f32[8,2176]{1,0:T(8,128)S(1)} %get-tuple-element.36), channel_id=1, source_target_pairs={{9,0},{8,1},{16,9},{17,8},{25,16},{24,17},{33,25},{32,24},{40,33},... | collective-permute-start | bytes 208904 | tf_op jit(solution)/shard_map/ppermute | solution.py:331
  223.4 3.5 %collective-permute-start.9 = (f32[16,4096]{1,0:T(8,128)S(1)}, f32[16,4096]{1,0:T(8,128)S(1)}, u32[]{:S(2)}, u32[]{:S(2)}) collective-permute-start(f32[16,4096]{1,0:T(8,128)S(1)} %get-tuple-element.40), channel_id=1, source_target_pairs={{0,1},{1,0},{2,3},{3,2},{4,5},{5,4},{6,7},{7,6},{8,9},{9,8},{10,11... | collective-permute-start | bytes 786440 | tf_op jit(solution)/shard_map/ppermute | solution.py:308
  227.6 8.9 %all-to-all-start.1 = ((f32[4,4,1024]{2,1,0:T(4,128)}), f32[4,4,1024]{2,1,0:T(4,128)S(1)}, u32[]{:S(2)}, u32[]{:S(2)}) async-start(f32[4,4,1024]{2,1,0:T(4,128)} %broadcast_in_dim.5), calls=%async_computation.1 | async-start | bytes 131072 | tf_op jit(solution)/shard_map/all_to_all | solution.py:304

commit v4 on v3

--- a/solution.py
+++ b/solution.py
@@ -11,28 +11,34 @@
 NEAR = 4
 
 kinetic_scale = 0.125
-highest = lax.Precision.HIGHEST
+three_passes = lax.Precision.HIGH
 f32 = jnp.float32
 VMEM = pl.BlockSpec(memory_space=pltpu.VMEM)
 SMEM = pl.BlockSpec(memory_space=pltpu.SMEM)
 
 
 def dot_nn(a, b):
-    return lax.dot_general(a, b, (((1,), (0,)), ((), ())), precision=highest, preferred_element_type=f32)
+    return lax.dot_general(a, b, (((1,), (0,)), ((), ())), precision=three_passes, preferred_element_type=f32)
 
 
 def dot_nt(a, b):
-    return lax.dot_general(a, b, (((1,), (1,)), ((), ())), precision=highest, preferred_element_type=f32)
+    return lax.dot_general(a, b, (((1,), (1,)), ((), ())), precision=three_passes, preferred_element_type=f32)
 
 
 def call(body, args, kinds, outs):
+    late = [pltpu.VMEM(a.shape, f32) for a, k in zip(args, kinds, strict=True) if k == "h"]
     args = [pltpu.with_memory_space_constraint(a, pltpu.VMEM) if k == "k" else a for a, k in zip(args, kinds, strict=True)]
     return pl.pallas_call(
         body,
-        in_specs=[SMEM if k == "s" else VMEM for k in kinds],
+        in_specs=[SMEM if k == "s" else pl.BlockSpec(memory_space=pl.ANY) if k == "h" else VMEM for k in kinds],
         out_specs=[VMEM] * len(outs),
         out_shape=[pltpu.VMEM(s, f32) for s in outs],
+        scratch_shapes=[*late, pltpu.SemaphoreType.DMA((len(late),))] if late else [],
     )(*args)
+
+
+def copies(pairs, sems):
+    return [pltpu.make_async_copy(a, b, sems.at[i]) for i, (a, b) in enumerate(pairs)]
 
 
 def orbital_row_sums(products, own):
@@ -50,7 +56,7 @@
     sums = sum(
         dot_nt(v_ref[:, h * half : (h + 1) * half], stat_refs[h][0:natoms, :]) for h in range(2)
     )
-    planes = w_ref.shape[0]
+    planes = w_ref.shape[0] - 1
     return sum(sums[z * own : (z + 1) * own] * w_ref[z : z + 1, :] for z in range(planes))
 
 
@@ -66,13 +72,12 @@
         ref[:, width:] = pc
 
 
-def apply_shift(emit, v_ref, pc_ref, lo_ref, hi_ref, stat_refs, w_ref, coup_ref, en_ref, cols):
+def apply_shift(emit, v_ref, pc_ref, lo_ref, hi_ref, stat_refs, w_ref, en_ref, cols):
     own = lo_ref.shape[0]
-    planes = w_ref.shape[0]
-    natoms = w_ref.shape[1]
+    planes, natoms = w_ref.shape[0] - 1, w_ref.shape[1]
     width = v_ref.shape[1]
     half = width // 2
-    c = coup_ref[...] * (pc_ref[...] + lo_ref[:, width:] + hi_ref[:, width:])
+    c = w_ref[planes : planes + 1, :] * (pc_ref[...] + lo_ref[:, width:] + hi_ref[:, width:])
     spread = jnp.concatenate([c * w_ref[z : z + 1, :] for z in range(planes)], axis=0)
     shift = jnp.concatenate([6.0 * kinetic_scale - en_ref[...]] * planes, axis=0)
     blocks = width // cols
@@ -160,15 +165,18 @@
             tiles[i] = step
     lower_inverse = jnp.concatenate(tiles, axis=0)[:, n:]
     inv = lax.dot_general(
-        lower_inverse, lower_inverse, (((0,), (0,)), ((), ())), precision=highest, preferred_element_type=f32
+        lower_inverse, lower_inverse, (((0,), (0,)), ((), ())), precision=three_passes, preferred_element_type=f32
     )
     return 2.0 * inv - dot_nn(dot_nn(inv, gram), inv)
 
 
 def source_body(
-    where_ref, sums_ref, swapped_ref, mine_ref, other_ref, stat_m, stat_o, w_ref,
-    r_ref, up_ref, down_ref, pc_ref, inv_ref, *, own, planes, natoms, cells,
-):
+    where_ref, sums_ref, swapped_ref, mine_hbm, other_hbm, stat_m, stat_o, w_ref,
+    r_ref, down_ref, up_ref, pc_ref, inv_ref, own_ref, mine_ref, other_ref, sems, *, own, planes, natoms, cells,
+):
+    arriving = copies([(mine_hbm, mine_ref), (other_hbm, other_ref)], sems)
+    for copy in arriving:
+        copy.start()
     half = stat_m.shape[1]
     total = mine_ref.shape[0]
     ours, theirs = sums_ref[...], swapped_ref[...]
@@ -179,10 +187,14 @@
     folded = ours[:, 2 * total - total // 2 :] / cells
     g = dot_nn(jnp.concatenate([folded[0:own], folded[own:]], axis=1), inv)
     start = pl.multiple_of(where_ref[0], own)
+    for copy in arriving:
+        copy.wait()
     for h, (orb_ref, stat) in enumerate(((mine_ref, stat_m), (other_ref, stat_o))):
         for z in range(planes):
             at = slice(z * half, (z + 1) * half)
-            source = stat[natoms + planes + z : natoms + planes + z + 1, :] * orb_ref[pl.ds(start, own), at]
+            mine = orb_ref[pl.ds(start, own), at]
+            source = stat[natoms + planes + z : natoms + planes + z + 1, :] * mine
+            own_ref[z * own : (z + 1) * own, h * half : (h + 1) * half] = mine
             r_ref[z * own : (z + 1) * own, h * half : (h + 1) * half] = dot_nn(g, orb_ref[:, at]) - source
     pc = inner_partials(r_ref, (stat_m, stat_o), w_ref, own, natoms)
     pc_ref[...] = pc
@@ -190,31 +202,36 @@
 
 
 def first_body(
-    where_ref, v_ref, pc_ref, lo_ref, hi_ref, stat_m, stat_o, w_ref, coup_ref, en_ref,
-    f_ref, up_ref, down_ref, out_pc_ref, *, own, natoms, cols,
+    where_ref, v_ref, pc_ref, lo_ref, hi_ref, stat_m, stat_o, w_ref, en_ref,
+    f_ref, down_ref, up_ref, out_pc_ref, *, own, natoms, cols,
 ):
     def emit(at, block):
         f_ref[:, at] = block
 
-    apply_shift(emit, v_ref, pc_ref, lo_ref, hi_ref, (stat_m, stat_o), w_ref, coup_ref, en_ref, cols)
+    apply_shift(emit, v_ref, pc_ref, lo_ref, hi_ref, (stat_m, stat_o), w_ref, en_ref, cols)
     pc = inner_partials(f_ref, (stat_m, stat_o), w_ref, own, natoms)
     out_pc_ref[...] = pc
     pack_edges(where_ref, f_ref, pc, up_ref, down_ref, own)
 
 
 def target_body(
-    freq_ref, v_ref, pc_ref, lo_ref, hi_ref, stat_m, stat_o, w_ref, coup_ref, en_ref, r_ref, mine_ref, other_ref,
-    t_ref, out_ref, *, own, planes, cols,
-):
+    freq_ref, v_ref, pc_ref, lo_ref, hi_ref, stat_m, stat_o, w_ref, en_ref, r_ref, mine_hbm, other_hbm,
+    t_ref, out_ref, mine_ref, other_ref, sems, *, own, planes, cols,
+):
+    arriving = copies([(mine_hbm, mine_ref), (other_hbm, other_ref)], sems)
+    for copy in arriving:
+        copy.start()
     square = freq_ref[0] * freq_ref[0]
 
     def emit(at, block):
         t_ref[:, at] = block + square * r_ref[:, at]
 
-    apply_shift(emit, v_ref, pc_ref, lo_ref, hi_ref, (stat_m, stat_o), w_ref, coup_ref, en_ref, cols)
+    apply_shift(emit, v_ref, pc_ref, lo_ref, hi_ref, (stat_m, stat_o), w_ref, en_ref, cols)
     half = stat_m.shape[1]
     total = mine_ref.shape[0]
     corr = jnp.zeros((own, total), f32)
+    for copy in arriving:
+        copy.wait()
     for h, orb_ref in enumerate((mine_ref, other_ref)):
         for z in range(planes):
             block = t_ref[z * own : (z + 1) * own, h * half : (h + 1) * half]
@@ -229,7 +246,7 @@
 
 def residual_body(
     where_ref, freq_ref, sums_ref, inv_ref, r_ref, t_ref, mine_ref, other_ref, stat_m, stat_o, w_ref,
-    out_ref, up_ref, down_ref, pc_ref, *, own, planes, natoms, cells,
+    out_ref, down_ref, up_ref, pc_ref, *, own, planes, natoms, cells,
 ):
     half = stat_m.shape[1]
     total = mine_ref.shape[0]
@@ -248,12 +265,12 @@
 
 
 def last_body(
-    v_ref, pc_ref, lo_ref, hi_ref, stat_m, stat_o, w_ref, coup_ref, en_ref, r_ref, f_ref, u_ref, out_ref, *, own, cols
+    v_ref, pc_ref, lo_ref, hi_ref, stat_m, stat_o, w_ref, en_ref, r_ref, f_ref, u_ref, out_ref, *, own, cols
 ):
     def emit(at, block):
         u_ref[:, at] = block
 
-    apply_shift(emit, v_ref, pc_ref, lo_ref, hi_ref, (stat_m, stat_o), w_ref, coup_ref, en_ref, cols)
+    apply_shift(emit, v_ref, pc_ref, lo_ref, hi_ref, (stat_m, stat_o), w_ref, en_ref, cols)
     r1, r0, u1, u0 = (lane_blocks(ref, cols) for ref in (v_ref, r_ref, u_ref, f_ref))
     values = [
         orbital_row_sums([a * b for a, b in zip(x, y)], own) for x, y in ((r1, r1), (u1, u1), (u1, u0), (r1, r0))
@@ -266,9 +283,9 @@
 
 
 def response_body(
-    where_ref, freq_ref, sums_ref, lines_ref, f_ref, u_ref, mine_ref, other_ref, out_ref, swap_ref, dens_ref, *, own, planes
-):
-    total = mine_ref.shape[0]
+    freq_ref, sums_ref, lines_ref, f_ref, u_ref, own_ref, out_ref, swap_ref, dens_ref, *, own, planes
+):
+    total = sums_ref.shape[1] // 2
     half = f_ref.shape[1] // 2
     square = freq_ref[0] * freq_ref[0]
     rr0, ff = sums_ref[:, total : total + 1], sums_ref[:, total + 1 : total + 2]
@@ -283,14 +300,13 @@
     beta = rr1 / rr0
     curvature = uu + 2.0 * beta * uf + beta * beta * ff + square * (rr1 + 2.0 * beta * rx + beta * beta * rr0)
     step1 = rr1 / curvature
-    start = pl.multiple_of(where_ref[0], own)
     swap_ref[own:, :] = jnp.zeros((swap_ref.shape[0] - own, swap_ref.shape[1]), f32)
-    for h, orb_ref in enumerate((mine_ref, other_ref)):
+    for h in range(2):
         for z in range(planes):
             rows, at = slice(z * own, (z + 1) * own), slice(h * half, (h + 1) * half)
             to = slice(z * half, (z + 1) * half)
             response = (step0 + step1 * beta) * f_ref[rows, at] + step1 * u_ref[rows, at]
-            dens = jnp.sum(orb_ref[pl.ds(start, own), to] * response, axis=0, keepdims=True)
+            dens = jnp.sum(own_ref[rows, at] * response, axis=0, keepdims=True)
             if h == 0:
                 out_ref[:, to] = response
                 dens_ref[:, to] = dens
@@ -328,7 +344,8 @@
     count = lax.axis_size("slab")
     ring = [(place(i, part), place((i + 1) % count, part)) for i in range(count) for part in range(2)]
     axes = ("slab", "pen")
-    return lax.ppermute(up, axes, ring), lax.ppermute(down, axes, [(b, a) for a, b in ring])
+    hi = lax.ppermute(down, axes, [(b, a) for a, b in ring])
+    return lax.ppermute(up, axes, ring), hi
 
 
 def plane_weights(atom_planes, profiles, planes, depth_total):
@@ -357,7 +374,7 @@
     weights = plane_weights(atom_planes, profiles, first_plane + jnp.arange(planes, dtype=jnp.int32), depth_total)
     where = jnp.stack([lax.axis_index("orb") * chip_count + core * own, core, *crossings]).astype(jnp.int32)
     own_energies = lax.dynamic_slice(energies, (core * own,), (own,)).reshape(own, 1)
-    coup = couplings.reshape(1, natoms)
+    weights = jnp.concatenate([weights, couplings.reshape(1, natoms)], axis=0)
 
     stat_m = jnp.concatenate(
         [a.reshape(-1, half) for a in (projectors, local_potential, perturbation)], axis=0
@@ -375,37 +392,37 @@
     )
     gram_sum = summed(gram_part)
     gram_other = swap_cores(gram_sum)
-    r0, up, down, pc, inv = call(
+    r0, down, up, pc, inv, own_orbitals = call(
         functools.partial(source_body, own=own, planes=planes, natoms=natoms, cells=cells),
-        (where, gram_sum, gram_other, mine, other, *stats, weights), "skkvvkkk",
-        [field, edge, edge, part, (total, total)],
+        (where, gram_sum, gram_other, mine, other, *stats, weights), "skkhhkkk",
+        [field, edge, edge, part, (total, total), field],
     )
     lo, hi = from_neighbours(up, down)
-    first, up, down, first_pc = call(
+    first, down, up, first_pc = call(
         functools.partial(first_body, own=own, natoms=natoms, cols=cols),
-        (where, r0, pc, lo, hi, *stats, weights, coup, own_energies), "skkkkkkkkk", [field, edge, edge, part],
+        (where, r0, pc, lo, hi, *stats, weights, own_energies), "skkkkkkkk", [field, edge, edge, part],
     )
     lo, hi = from_neighbours(up, down)
     target, sums_part = call(
         functools.partial(target_body, own=own, planes=planes, cols=cols),
-        (frequency, first, first_pc, lo, hi, *stats, weights, coup, own_energies, r0, mine, other), "skkkkkkkkkkvv",
+        (frequency, first, first_pc, lo, hi, *stats, weights, own_energies, r0, mine, other), "skkkkkkkkkhh",
         [field, (own, 2 * total)],
     )
     sums = summed(sums_part)
-    r1, up, down, pc = call(
+    r1, down, up, pc = call(
         functools.partial(residual_body, own=own, planes=planes, natoms=natoms, cells=cells),
         (where, frequency, sums, inv, r0, target, mine, other, *stats, weights), "sskkkkvvkkk", [field, edge, edge, part],
     )
     lo, hi = from_neighbours(up, down)
     last, lines = call(
         functools.partial(last_body, own=own, cols=cols),
-        (r1, pc, lo, hi, *stats, weights, coup, own_energies, r0, first), "kkkkkkkkkkk",
+        (r1, pc, lo, hi, *stats, weights, own_energies, r0, first), "kkkkkkkkkk",
         [field, (1, 2 * total)],
     )
     lines = summed(lines)
     response, to_other, dens = call(
         functools.partial(response_body, own=own, planes=planes),
-        (where, frequency, sums, lines, first, last, mine, other), "sskkkkvv",
+        (frequency, sums, lines, first, last, own_orbitals), "skkkkk",
         [(own, planes * half), (2 * own, planes * half), (1, planes * half)],
     )
     got = swap_cores(to_other)

time: 238 us -> 231 us (0.971)
  Pallas kernels: 27.5 us -> 21.6 us
    pallas_call x7, Pallas kernels: 27.5 us -> 21.6 us  [call(): pl.pallas_call(body, in_specs=[SMEM if k == 's' else pl.BlockSpec(memory_...]
where the time goes in v4:
time: 231 us; the launch traced here: 230 us
  blocking collectives  156 us (68%)
  starting transfers between devices  33.7 us (15%)
  Pallas kernels  21.6 us (9%)
  waiting for transfers between devices  12.4 us (5%)
  local copies, waits for them, and re-layouts  4.38 us (2%)
    psum x3, blocking collectives, summed(): return lax.psum(array, ('slab', 'pen'), axis_index_groups=across)  106 us
    psum x3, blocking collectives, summed(): array = lax.psum(array, ('slab', 'pen'), axis_index_groups=runs)  30 us
    pallas_call x7, Pallas kernels, call(): pl.pallas_call(body, in_specs=[SMEM if k == 's' else pl.BlockSpec(memory_...  21.6 us
    all_to_all x1, blocking collectives, copy_for_each(): return lax.all_to_all(copies, axis, split_axis=0, concat_axis=0, tiled=True)  19.7 us
    ppermute x3, starting transfers between devices, from_neighbours(): hi = lax.ppermute(down, axes, [(b, a) for a, b in ring])  15.8 us
    ppermute x4, starting transfers between devices, swap_cores(): return lax.ppermute(array, 'pen', [(0, 1), (1, 0)])  8.64 us
    ppermute x3, starting transfers between devices, from_neighbours(): return (lax.ppermute(up, axes, ring), hi)  5.87 us
  transfers between devices with their start and end apart: 11, of which 9 were waited for; matrix products, arithmetic and copies ran while one was open for 1% of the time, Pallas kernels for 0%

profile of v4, /device:TPU:40, one launch (start us, length us, event | category | flops | bytes accessed | tf_op | source)
XLA Modules:
  0.0 230.5 jit_solution(12821436345185135435)
XLA Ops:
  0.6 0.0 copy-start
  0.6 1.1 reshape.69
  1.7 0.1 broadcast_in_dim.4
  1.8 0.0 copy-start.3
  1.8 0.0 copy-start.2
  1.8 19.7 %all_to_all.10 = f32[4,16,4096]{2,1,0:T(8,128)S(1)} all-to-all(f32[4,16,4096]{2,1,0:T(8,128)S(1)} %broadcast_in_dim.4), channel_id=1, replica_groups=mesh['parts'=2,'slab'=32,'orb'=4,'pen'=2] {'orb'}, dimensions={0} | all-to-all | bytes 2097152 | tf_op jit(solution)/shard_map/all_to_all | solution.py:320
  21.5 0.0 copy-start.1
  21.5 1.9 collective-permute-start
  23.5 0.0 copy-done.3
  23.5 0.0 copy-start.4
  23.5 0.7 copy-done.4
  24.2 0.0 copy-done.2
  24.2 0.1 copy.18
  24.4 0.0 copy-done.1
  24.4 2.4 %collective-permute-start.1 = (f32[136,1024]{1,0:T(8,128)S(1)}, f32[136,1024]{1,0:T(8,128)S(1)}, u32[]{:S(2)}, u32[]{:S(2)}) collective-permute-start(f32[136,1024]{1,0:T(8,128)S(1)} %pad_maximum_fusion.stat_m), channel_id=1, source_target_pairs={{0,1},{1,0},{2,3},{3,2},{4,5},{5,4},{6,7},{7,6},{8,9},{9,8},{10,11... | collective-permute-start | bytes 1671176 | tf_op jit(solution)/shard_map/ppermute | solution.py:324
  26.9 0.0 copy-start.6
  27.0 0.0 copy-start.5
  27.0 0.6 pad_add_fusion.where_ref
  27.6 0.0 copy-done.6
  27.6 0.1 copy-done.5
  27.7 0.1 select_reduce_fusion
  27.8 0.6 collective-permute-done.1.stat_o
  28.4 0.0 collective-permute-done.other_ref.other_hbm
  28.4 2.7 %shard_map.104 = f32[16,128]{1,0:T(8,128)S(1)} custom-call(s32[4]{0:T(128)} %pad_add_fusion.where_ref, f32[64,4096]{1,0:T(8,128)} %bitcast.15, f32[64,4096]{1,0:T(8,128)} %collective-permute-done.other_ref.other_hbm, f32[136,1024]{1,0:T(8,128)S(1)} %pad_maximum_fusion.stat_m, f32[136,1024]{1,0:T(8,128)S(1)} %collective-permute-done.1.stat_o), custom_call_target="tpu_custom_call" | custom-call | tf_op jit(solution)/shard_map/pallas_call | solution.py:31
  31.1 14.8 %psum.42 = f32[16,128]{1,0:T(8,128)S(1)} all-reduce(f32[16,128]{1,0:T(8,128)S(1)} %shard_map.104), channel_id=1, replica_groups={{0,9,16,25},{33,40,49,56},{64,73,80,89},{97,104,113,120},{128,137,144,1..., use_global_device_ids=true, to_apply=%region_0.1 | all-reduce | flops 2048 | bytes 16384 | tf_op jit(solution)/shard_map/psum | solution.py:339
  45.9 57.3 %psum.43.sums_ref = f32[16,128]{1,0:T(8,128)S(1)} all-reduce(f32[16,128]{1,0:T(8,128)S(1)} %psum.42), channel_id=1, replica_groups={{0,33,64,97,128,161,192,225},{9,40,73,104,137,168,201,232},{16,49,80,11..., use_global_device_ids=true, to_apply=%region_1.2 | all-reduce | flops 2048 | bytes 16384 | tf_op jit(solution)/shard_map/psum | solution.py:340
  103.2 0.0 copy-start.7
  103.2 2.3 %collective-permute-start.2 = (f32[16,128]{1,0:T(8,128)S(1)}, f32[16,128]{1,0:T(8,128)S(1)}, u32[]{:S(2)}, u32[]{:S(2)}) collective-permute-start(f32[16,128]{1,0:T(8,128)S(1)} %psum.43.sums_ref), channel_id=1, source_target_pairs={{0,1},{1,0},{2,3},{3,2},{4,5},{5,4},{6,7},{7,6},{8,9},{9,8},{10,11... | collective-permute-start | bytes 24584 | tf_op jit(solution)/shard_map/ppermute | solution.py:324
  105.6 0.0 copy-done.7
  105.6 0.8 collective-permute-done.2.swapped_ref
  106.4 10.9 %shard_map.105 = (f32[32,2048]{1,0:T(8,128)S(1)}, f32[8,2176]{1,0:T(8,128)S(1)}, f32[8,2176]{1,0:T(8,128)S(1)}, f32[8,128]{1,0:T(8,128)S(1)}, f32[64,64]{1,0:T(8,128)S(1)}, /*index=5*/f32[32,2048]{1,0:T(8,128)S(1)}) custom-call(s32[4]{0:T(128)} %pad_add_fusion.where_ref, f32[16,128]{1,0:T(8,128)S(1)} %psum.43.sums_ref, ...), custom_call_target="tpu_custom_call" | custom-call | tf_op jit(solution)/shard_map/pallas_call | solution.py:31
  117.3 2.0 collective-permute-start.3
  119.3 5.2 %collective-permute-start.4 = (f32[8,2176]{1,0:T(8,128)S(1)}, f32[8,2176]{1,0:T(8,128)S(1)}, u32[]{:S(2)}, u32[]{:S(2)}) collective-permute-start(f32[8,2176]{1,0:T(8,128)S(1)} %get-tuple-element.26), channel_id=1, source_target_pairs={{9,0},{8,1},{16,9},{17,8},{25,16},{24,17},{33,25},{32,24},{40,33},... | collective-permute-start | bytes 208904 | tf_op jit(solution)/shard_map/ppermute | solution.py:347
  124.4 0.0 copy-done
  124.4 0.1 dynamic-slice_bitcast_fusion
  124.5 0.1 copy.15.en_ref
  124.6 0.3 collective-permute-done.3.lo_ref
  124.9 1.5 collective-permute-done.4.hi_ref
  126.3 1.6 shard_map.106
  127.9 2.0 collective-permute-start.5
  129.9 5.5 %collective-permute-start.6 = (f32[8,2176]{1,0:T(8,128)S(1)}, f32[8,2176]{1,0:T(8,128)S(1)}, u32[]{:S(2)}, u32[]{:S(2)}) collective-permute-start(f32[8,2176]{1,0:T(8,128)S(1)} %get-tuple-element.30), channel_id=1, source_target_pairs={{9,0},{8,1},{16,9},{17,8},{25,16},{24,17},{33,25},{32,24},{40,33},... | collective-permute-start | bytes 208904 | tf_op jit(solution)/shard_map/ppermute | solution.py:347
  136.1 0.0 collective-permute-done.5.lo_ref
  136.1 1.3 collective-permute-done.6.hi_ref
  137.4 2.9 %shard_map.107 = (f32[32,2048]{1,0:T(8,128)S(1)}, f32[8,128]{1,0:T(8,128)S(1)}) custom-call(f32[1]{0:T(128)S(6)} %copy.21.freq_ref, f32[32,2048]{1,0:T(8,128)S(1)} %get-tuple-element.27.v_ref.f_ref, f32[8,128]{1,0:T(8,128)S(1)} %get-tuple-element.28.pc_ref, f32[8,2176]{1,0:T(8,128)S(1)} %collective-permute-done.5.lo_ref, ...), custom_call_target="tpu_custom_call" | custom-call | tf_op jit(solution)/shard_map/pallas_call | solution.py:31
  140.3 7.6 %psum.44 = f32[8,128]{1,0:T(8,128)S(1)} all-reduce(f32[8,128]{1,0:T(8,128)S(1)} %get-tuple-element.31), channel_id=1, replica_groups={{0,9,16,25},{33,40,49,56},{64,73,80,89},{97,104,113,120},{128,137,144,1..., use_global_device_ids=true, to_apply=%region_3.4 | all-reduce | flops 1024 | bytes 8192 | tf_op jit(solution)/shard_map/psum | solution.py:339
  147.8 24.4 %psum.45.sums_ref = f32[8,128]{1,0:T(8,128)S(1)} all-reduce(f32[8,128]{1,0:T(8,128)S(1)} %psum.44), channel_id=1, replica_groups={{0,33,64,97,128,161,192,225},{9,40,73,104,137,168,201,232},{16,49,80,11..., use_global_device_ids=true, to_apply=%region_4.5 | all-reduce | flops 1024 | bytes 8192 | tf_op jit(solution)/shard_map/psum | solution.py:340
  172.2 2.7 %shard_map.108 = (f32[32,2048]{1,0:T(8,128)S(1)}, f32[8,2176]{1,0:T(8,128)S(1)}, f32[8,2176]{1,0:T(8,128)S(1)}, f32[8,128]{1,0:T(8,128)S(1)}) custom-call(s32[4]{0:T(128)} %pad_add_fusion.where_ref, f32[1]{0:T(128)S(6)} %copy.21.freq_ref, f32[8,128]{1,0:T(8,128)S(1)} %psum.45.sums_ref, f32[64,64]{1,0:T(8,128)S(1)} %get-tuple-element.32.inv_ref, ...), custom_call_target="tpu_custom_call" | custom-call | tf_op jit(solution)/shard_map/pallas_call | solution.py:31
  174.9 2.0 collective-permute-start.7
  176.9 5.2 %collective-permute-start.8 = (f32[8,2176]{1,0:T(8,128)S(1)}, f32[8,2176]{1,0:T(8,128)S(1)}, u32[]{:S(2)}, u32[]{:S(2)}) collective-permute-start(f32[8,2176]{1,0:T(8,128)S(1)} %get-tuple-element.37), channel_id=1, source_target_pairs={{9,0},{8,1},{16,9},{17,8},{25,16},{24,17},{33,25},{32,24},{40,33},... | collective-permute-start | bytes 208904 | tf_op jit(solution)/shard_map/ppermute | solution.py:347
  182.1 0.3 collective-permute-done.7.lo_ref
  182.4 1.6 collective-permute-done.8.hi_ref
  184.0 0.5 shard_map.109
  184.5 7.6 %psum.46 = f32[1,128]{1,0:T(1,128)S(1)} all-reduce(f32[1,128]{1,0:T(1,128)S(1)} %get-tuple-element.38), channel_id=1, replica_groups={{0,9,16,25},{33,40,49,56},{64,73,80,89},{97,104,113,120},{128,137,144,1..., use_global_device_ids=true, to_apply=%region_5.6 | all-reduce | flops 128 | bytes 1024 | tf_op jit(solution)/shard_map/psum | solution.py:339
  192.1 24.4 %psum.47.lines_ref = f32[1,128]{1,0:T(1,128)S(1)} all-reduce(f32[1,128]{1,0:T(1,128)S(1)} %psum.46), channel_id=1, replica_groups={{0,33,64,97,128,161,192,225},{9,40,73,104,137,168,201,232},{16,49,80,11..., use_global_device_ids=true, to_apply=%region_6.7 | all-reduce | flops 128 | bytes 1024 | tf_op jit(solution)/shard_map/psum | solution.py:340
  216.4 0.3 shard_map.110
  216.8 2.0 collective-permute-start.9
  218.7 1.5 collective-permute-done.9
  220.3 0.6 broadcast_in_dim.5
  220.9 3.4 %all-to-all-start.1 = ((f32[4,4,1024]{2,1,0:T(4,128)}), f32[4,4,1024]{2,1,0:T(4,128)S(1)}, u32[]{:S(2)}, u32[]{:S(2)}) async-start(f32[4,4,1024]{2,1,0:T(4,128)} %broadcast_in_dim.5), calls=%async_computation.1 | async-start | bytes 131072 | tf_op jit(solution)/shard_map/all_to_all | solution.py:320
  224.3 0.9 reshape.76
  225.2 4.6 %all-to-all-done.1 = f32[4,4,1024]{2,1,0:T(4,128)S(1)} async-done(((f32[4,4,1024]{2,1,0:T(4,128)}), f32[4,4,1024]{2,1,0:T(4,128)S(1)}, u32[]{:S(2)}, u32[]{:S(2)}) %all-to-all-start.1) | async-done | bytes 65568 | tf_op jit(solution)/shard_map/all_to_all | solution.py:320
  229.9 0.6 mul.35
  (12 shorter events, 0.2 us)
Async XLA Ops:
  0.6 123.8 %copy-start = (f32[16]{0:T(128)S(1)}, f32[16]{0:T(128)}, u32[]{:S(2)}) copy-start(f32[16]{0:T(128)} %param.10) | copy-start | bytes 196
  1.8 21.7 %copy-start.3 = (f32[4,4,256]{2,1,0:T(4,128)S(1)}, f32[4,4,256]{2,1,0:T(4,128)}, u32[]{:S(2)}) copy-start(f32[4,4,256]{2,1,0:T(4,128)} %param.12) | copy-start | bytes 49156
  1.8 22.4 %copy-start.2 = (f32[128,4,256]{2,1,0:T(4,128)S(1)}, f32[128,4,256]{2,1,0:T(4,128)}, u32[]{:S(2)}) copy-start(f32[128,4,256]{2,1,0:T(4,128)} %param.14) | copy-start | bytes 1572868
  21.5 2.8 %copy-start.1 = (f32[4,16,4096]{2,1,0:T(8,128)}, f32[4,16,4096]{2,1,0:T(8,128)S(1)}, u32[]{:S(2)}) copy-start(f32[4,16,4096]{2,1,0:T(8,128)S(1)} %all_to_all.10) | copy-start | bytes 3145732
  21.5 6.9 %collective-permute-start = (f32[64,4096]{1,0:T(8,128)S(1)}, f32[64,4096]{1,0:T(8,128)}, u32[]{:S(2)}, u32[]{:S(2)}) collective-permute-start(f32[64,4096]{1,0:T(8,128)S(1)} %bitcast.14), channel_id=1, source_target_pairs={{0,1},{1,0},{2,3},{3,2},{4,5},{5,4},{6,7},{7,6},{8,9},{9,8},{10,11... | collective-permute-start | bytes 3145736 | tf_op jit(solution)/shard_map/ppermute | solution.py:324
  23.5 0.7 copy-start.4
  24.4 4.0 %collective-permute-start.1 = (f32[136,1024]{1,0:T(8,128)S(1)}, f32[136,1024]{1,0:T(8,128)S(1)}, u32[]{:S(2)}, u32[]{:S(2)}) collective-permute-start(f32[136,1024]{1,0:T(8,128)S(1)} %pad_maximum_fusion.stat_m), channel_id=1, source_target_pairs={{0,1},{1,0},{2,3},{3,2},{4,5},{5,4},{6,7},{7,6},{8,9},{9,8},{10,11... | collective-permute-start | bytes 1671176 | tf_op jit(solution)/shard_map/ppermute | solution.py:324
  26.9 0.7 copy-start.6
  27.0 0.7 copy-start.5
  103.2 2.3 %copy-start.7 = (f32[128]{0:T(128)S(1)}, f32[128]{0:T(128)}, u32[]{:S(2)}) copy-start(f32[128]{0:T(128)} %param.16) | copy-start | bytes 1540
  103.2 3.1 %collective-permute-start.2 = (f32[16,128]{1,0:T(8,128)S(1)}, f32[16,128]{1,0:T(8,128)S(1)}, u32[]{:S(2)}, u32[]{:S(2)}) collective-permute-start(f32[16,128]{1,0:T(8,128)S(1)} %psum.43.sums_ref), channel_id=1, source_target_pairs={{0,1},{1,0},{2,3},{3,2},{4,5},{5,4},{6,7},{7,6},{8,9},{9,8},{10,11... | collective-permute-start | bytes 24584 | tf_op jit(solution)/shard_map/ppermute | solution.py:324
  117.3 7.6 %collective-permute-start.3 = (f32[8,2176]{1,0:T(8,128)S(1)}, f32[8,2176]{1,0:T(8,128)S(1)}, u32[]{:S(2)}, u32[]{:S(2)}) collective-permute-start(f32[8,2176]{1,0:T(8,128)S(1)} %get-tuple-element.25), channel_id=1, source_target_pairs={{0,9},{1,8},{9,16},{8,17},{16,25},{17,24},{25,33},{24,32},{33,40},... | collective-permute-start | bytes 208904 | tf_op jit(solution)/shard_map/ppermute | solution.py:348
  119.3 7.1 %collective-permute-start.4 = (f32[8,2176]{1,0:T(8,128)S(1)}, f32[8,2176]{1,0:T(8,128)S(1)}, u32[]{:S(2)}, u32[]{:S(2)}) collective-permute-start(f32[8,2176]{1,0:T(8,128)S(1)} %get-tuple-element.26), channel_id=1, source_target_pairs={{9,0},{8,1},{16,9},{17,8},{25,16},{24,17},{33,25},{32,24},{40,33},... | collective-permute-start | bytes 208904 | tf_op jit(solution)/shard_map/ppermute | solution.py:347
  127.9 8.1 %collective-permute-start.5 = (f32[8,2176]{1,0:T(8,128)S(1)}, f32[8,2176]{1,0:T(8,128)S(1)}, u32[]{:S(2)}, u32[]{:S(2)}) collective-permute-start(f32[8,2176]{1,0:T(8,128)S(1)} %get-tuple-element.29), channel_id=1, source_target_pairs={{0,9},{1,8},{9,16},{8,17},{16,25},{17,24},{25,33},{24,32},{33,40},... | collective-permute-start | bytes 208904 | tf_op jit(solution)/shard_map/ppermute | solution.py:348
  129.9 7.4 %collective-permute-start.6 = (f32[8,2176]{1,0:T(8,128)S(1)}, f32[8,2176]{1,0:T(8,128)S(1)}, u32[]{:S(2)}, u32[]{:S(2)}) collective-permute-start(f32[8,2176]{1,0:T(8,128)S(1)} %get-tuple-element.30), channel_id=1, source_target_pairs={{9,0},{8,1},{16,9},{17,8},{25,16},{24,17},{33,25},{32,24},{40,33},... | collective-permute-start | bytes 208904 | tf_op jit(solution)/shard_map/ppermute | solution.py:347
  174.9 7.4 %collective-permute-start.7 = (f32[8,2176]{1,0:T(8,128)S(1)}, f32[8,2176]{1,0:T(8,128)S(1)}, u32[]{:S(2)}, u32[]{:S(2)}) collective-permute-start(f32[8,2176]{1,0:T(8,128)S(1)} %get-tuple-element.36), channel_id=1, source_target_pairs={{0,9},{1,8},{9,16},{8,17},{16,25},{17,24},{25,33},{24,32},{33,40},... | collective-permute-start | bytes 208904 | tf_op jit(solution)/shard_map/ppermute | solution.py:348
  176.9 7.1 %collective-permute-start.8 = (f32[8,2176]{1,0:T(8,128)S(1)}, f32[8,2176]{1,0:T(8,128)S(1)}, u32[]{:S(2)}, u32[]{:S(2)}) collective-permute-start(f32[8,2176]{1,0:T(8,128)S(1)} %get-tuple-element.37), channel_id=1, source_target_pairs={{9,0},{8,1},{16,9},{17,8},{25,16},{24,17},{33,25},{32,24},{40,33},... | collective-permute-start | bytes 208904 | tf_op jit(solution)/shard_map/ppermute | solution.py:347
  216.8 3.5 %collective-permute-start.9 = (f32[16,4096]{1,0:T(8,128)S(1)}, f32[16,4096]{1,0:T(8,128)S(1)}, u32[]{:S(2)}, u32[]{:S(2)}) collective-permute-start(f32[16,4096]{1,0:T(8,128)S(1)} %get-tuple-element.42), channel_id=1, source_target_pairs={{0,1},{1,0},{2,3},{3,2},{4,5},{5,4},{6,7},{7,6},{8,9},{9,8},{10,11... | collective-permute-start | bytes 786440 | tf_op jit(solution)/shard_map/ppermute | solution.py:324
  220.9 8.9 %all-to-all-start.1 = ((f32[4,4,1024]{2,1,0:T(4,128)}), f32[4,4,1024]{2,1,0:T(4,128)S(1)}, u32[]{:S(2)}, u32[]{:S(2)}) async-start(f32[4,4,1024]{2,1,0:T(4,128)} %broadcast_in_dim.5), calls=%async_computation.1 | async-start | bytes 131072 | tf_op jit(solution)/shard_map/all_to_all | solution.py:320

commit v5 on v4

--- a/solution.py
+++ b/solution.py
@@ -11,18 +11,18 @@
 NEAR = 4
 
 kinetic_scale = 0.125
-three_passes = lax.Precision.HIGH
+highest, three_passes = lax.Precision.HIGHEST, lax.Precision.HIGH
 f32 = jnp.float32
 VMEM = pl.BlockSpec(memory_space=pltpu.VMEM)
 SMEM = pl.BlockSpec(memory_space=pltpu.SMEM)
 
 
-def dot_nn(a, b):
-    return lax.dot_general(a, b, (((1,), (0,)), ((), ())), precision=three_passes, preferred_element_type=f32)
-
-
-def dot_nt(a, b):
-    return lax.dot_general(a, b, (((1,), (1,)), ((), ())), precision=three_passes, preferred_element_type=f32)
+def dot_nn(a, b, precision=highest):
+    return lax.dot_general(a, b, (((1,), (0,)), ((), ())), precision=precision, preferred_element_type=f32)
+
+
+def dot_nt(a, b, precision=highest):
+    return lax.dot_general(a, b, (((1,), (1,)), ((), ())), precision=precision, preferred_element_type=f32)
 
 
 def call(body, args, kinds, outs):
@@ -54,30 +54,33 @@
 def inner_partials(v_ref, stat_refs, w_ref, own, natoms):
     half = stat_refs[0].shape[1]
     sums = sum(
-        dot_nt(v_ref[:, h * half : (h + 1) * half], stat_refs[h][0:natoms, :]) for h in range(2)
+        dot_nt(v_ref[:, h * half : (h + 1) * half], stat_refs[h][0:natoms, :], three_passes) for h in range(2)
     )
     planes = w_ref.shape[0] - 1
     return sum(sums[z * own : (z + 1) * own] * w_ref[z : z + 1, :] for z in range(planes))
 
 
-def pack_edges(where_ref, v_ref, pc, up_ref, down_ref, own):
+def pack_edges(where_ref, v_ref, pc, even_ref, odd_ref, own):
     width = v_ref.shape[1]
     half = width // 2
+    is_even = where_ref[4] == 0
+    top, bottom = v_ref[v_ref.shape[0] - own :, :], v_ref[0:own, :]
     for ref, edge, crossing in (
-        (up_ref, v_ref[v_ref.shape[0] - own :, :], where_ref[2] == 1),
-        (down_ref, v_ref[0:own, :], where_ref[3] == 1),
+        (even_ref, jnp.where(is_even, top, bottom), jnp.where(is_even, where_ref[2], where_ref[3]) == 1),
+        (odd_ref, jnp.where(is_even, bottom, top), jnp.where(is_even, where_ref[3], where_ref[2]) == 1),
     ):
         ref[:, 0:half] = jnp.where(crossing, edge[:, half:], edge[:, 0:half])
         ref[:, half:width] = jnp.where(crossing, edge[:, 0:half], edge[:, half:])
         ref[:, width:] = pc
 
 
-def apply_shift(emit, v_ref, pc_ref, lo_ref, hi_ref, stat_refs, w_ref, en_ref, cols):
-    own = lo_ref.shape[0]
+def apply_shift(emit, where_ref, v_ref, pc_ref, odd_ref, even_ref, stat_refs, w_ref, en_ref, cols):
+    own = odd_ref.shape[0]
+    is_even = where_ref[4] == 0
     planes, natoms = w_ref.shape[0] - 1, w_ref.shape[1]
     width = v_ref.shape[1]
     half = width // 2
-    c = w_ref[planes : planes + 1, :] * (pc_ref[...] + lo_ref[:, width:] + hi_ref[:, width:])
+    c = w_ref[planes : planes + 1, :] * (pc_ref[...] + odd_ref[:, width:] + even_ref[:, width:])
     spread = jnp.concatenate([c * w_ref[z : z + 1, :] for z in range(planes)], axis=0)
     shift = jnp.concatenate([6.0 * kinetic_scale - en_ref[...]] * planes, axis=0)
     blocks = width // cols
@@ -85,12 +88,13 @@
         at = slice(k * cols, (k + 1) * cols)
         stat = stat_refs[k * cols // half]
         inside = (k * cols) % half
-        nonlocal_term = dot_nn(spread, stat[0:natoms, inside : inside + cols])
+        odd, even = odd_ref[:, at], even_ref[:, at]
+        nonlocal_term = dot_nn(spread, stat[0:natoms, inside : inside + cols], three_passes)
         v = v_ref[:, at]
         after, before = (k + 1) % blocks, (k - 1) % blocks
         beside = v_ref[:, after * cols : (after + 1) * cols] + v_ref[:, before * cols : (before + 1) * cols]
-        beside = beside + jnp.concatenate([lo_ref[:, at], v_ref[0 : own * (planes - 1), at]], axis=0)
-        beside = beside + jnp.concatenate([v_ref[own:, at], hi_ref[:, at]], axis=0)
+        beside = beside + jnp.concatenate([jnp.where(is_even, odd, even), v_ref[0 : own * (planes - 1), at]], axis=0)
+        beside = beside + jnp.concatenate([v_ref[own:, at], jnp.where(is_even, even, odd)], axis=0)
         beside = beside + pltpu.roll(v, 1, 1) + pltpu.roll(v, cols - 1, 1)
         local = jnp.concatenate(
             [
@@ -165,14 +169,14 @@
             tiles[i] = step
     lower_inverse = jnp.concatenate(tiles, axis=0)[:, n:]
     inv = lax.dot_general(
-        lower_inverse, lower_inverse, (((0,), (0,)), ((), ())), precision=three_passes, preferred_element_type=f32
+        lower_inverse, lower_inverse, (((0,), (0,)), ((), ())), precision=highest, preferred_element_type=f32
     )
     return 2.0 * inv - dot_nn(dot_nn(inv, gram), inv)
 
 
 def source_body(
     where_ref, sums_ref, swapped_ref, mine_hbm, other_hbm, stat_m, stat_o, w_ref,
-    r_ref, down_ref, up_ref, pc_ref, inv_ref, own_ref, mine_ref, other_ref, sems, *, own, planes, natoms, cells,
+    r_ref, even_edge, odd_edge, pc_ref, inv_ref, own_ref, mine_ref, other_ref, sems, *, own, planes, natoms, cells,
 ):
     arriving = copies([(mine_hbm, mine_ref), (other_hbm, other_ref)], sems)
     for copy in arriving:
@@ -198,24 +202,24 @@
             r_ref[z * own : (z + 1) * own, h * half : (h + 1) * half] = dot_nn(g, orb_ref[:, at]) - source
     pc = inner_partials(r_ref, (stat_m, stat_o), w_ref, own, natoms)
     pc_ref[...] = pc
-    pack_edges(where_ref, r_ref, pc, up_ref, down_ref, own)
+    pack_edges(where_ref, r_ref, pc, even_edge, odd_edge, own)
 
 
 def first_body(
-    where_ref, v_ref, pc_ref, lo_ref, hi_ref, stat_m, stat_o, w_ref, en_ref,
-    f_ref, down_ref, up_ref, out_pc_ref, *, own, natoms, cols,
+    where_ref, v_ref, pc_ref, odd_ref, even_ref, stat_m, stat_o, w_ref, en_ref,
+    f_ref, even_edge, odd_edge, out_pc_ref, *, own, natoms, cols,
 ):
     def emit(at, block):
         f_ref[:, at] = block
 
-    apply_shift(emit, v_ref, pc_ref, lo_ref, hi_ref, (stat_m, stat_o), w_ref, en_ref, cols)
+    apply_shift(emit, where_ref, v_ref, pc_ref, odd_ref, even_ref, (stat_m, stat_o), w_ref, en_ref, cols)
     pc = inner_partials(f_ref, (stat_m, stat_o), w_ref, own, natoms)
     out_pc_ref[...] = pc
-    pack_edges(where_ref, f_ref, pc, up_ref, down_ref, own)
+    pack_edges(where_ref, f_ref, pc, even_edge, odd_edge, own)
 
 
 def target_body(
-    freq_ref, v_ref, pc_ref, lo_ref, hi_ref, stat_m, stat_o, w_ref, en_ref, r_ref, mine_hbm, other_hbm,
+    where_ref, freq_ref, v_ref, pc_ref, odd_ref, even_ref, stat_m, stat_o, w_ref, en_ref, r_ref, mine_hbm, other_hbm,
     t_ref, out_ref, mine_ref, other_ref, sems, *, own, planes, cols,
 ):
     arriving = copies([(mine_hbm, mine_ref), (other_hbm, other_ref)], sems)
@@ -226,7 +230,7 @@
     def emit(at, block):
         t_ref[:, at] = block + square * r_ref[:, at]
 
-    apply_shift(emit, v_ref, pc_ref, lo_ref, hi_ref, (stat_m, stat_o), w_ref, en_ref, cols)
+    apply_shift(emit, where_ref, v_ref, pc_ref, odd_ref, even_ref, (stat_m, stat_o), w_ref, en_ref, cols)
     half = stat_m.shape[1]
     total = mine_ref.shape[0]
     corr = jnp.zeros((own, total), f32)
@@ -246,7 +250,7 @@
 
 def residual_body(
     where_ref, freq_ref, sums_ref, inv_ref, r_ref, t_ref, mine_ref, other_ref, stat_m, stat_o, w_ref,
-    out_ref, down_ref, up_ref, pc_ref, *, own, planes, natoms, cells,
+    out_ref, even_edge, odd_edge, pc_ref, *, own, planes, natoms, cells,
 ):
     half = stat_m.shape[1]
     total = mine_ref.shape[0]
@@ -261,16 +265,16 @@
             out_ref[rows, at] = r_ref[rows, at] - step * image
     pc = inner_partials(out_ref, (stat_m, stat_o), w_ref, own, natoms)
     pc_ref[...] = pc
-    pack_edges(where_ref, out_ref, pc, up_ref, down_ref, own)
+    pack_edges(where_ref, out_ref, pc, even_edge, odd_edge, own)
 
 
 def last_body(
-    v_ref, pc_ref, lo_ref, hi_ref, stat_m, stat_o, w_ref, en_ref, r_ref, f_ref, u_ref, out_ref, *, own, cols
+    where_ref, v_ref, pc_ref, odd_ref, even_ref, stat_m, stat_o, w_ref, en_ref, r_ref, f_ref, u_ref, out_ref, *, own, cols
 ):
     def emit(at, block):
         u_ref[:, at] = block
 
-    apply_shift(emit, v_ref, pc_ref, lo_ref, hi_ref, (stat_m, stat_o), w_ref, en_ref, cols)
+    apply_shift(emit, where_ref, v_ref, pc_ref, odd_ref, even_ref, (stat_m, stat_o), w_ref, en_ref, cols)
     r1, r0, u1, u0 = (lane_blocks(ref, cols) for ref in (v_ref, r_ref, u_ref, f_ref))
     values = [
         orbital_row_sums([a * b for a, b in zip(x, y)], own) for x, y in ((r1, r1), (u1, u1), (u1, u0), (r1, r0))
@@ -340,12 +344,15 @@
     return lax.psum(array, ("slab", "pen"), axis_index_groups=across)
 
 
-def from_neighbours(up, down):
+def from_neighbours(even_edge, odd_edge):
     count = lax.axis_size("slab")
-    ring = [(place(i, part), place((i + 1) % count, part)) for i in range(count) for part in range(2)]
+
+    def pairs(first):
+        both = [(i, (i + 1) % count) for i in range(first, count, 2)]
+        return [(place(a, part), place(b, part)) for i, j in both for a, b in ((i, j), (j, i)) for part in range(2)]
+
     axes = ("slab", "pen")
-    hi = lax.ppermute(down, axes, [(b, a) for a, b in ring])
-    return lax.ppermute(up, axes, ring), hi
+    return lax.ppermute(odd_edge, axes, pairs(1)), lax.ppermute(even_edge, axes, pairs(0))
 
 
 def plane_weights(atom_planes, profiles, planes, depth_total):
@@ -362,7 +369,7 @@
     natoms = projectors.shape[0]
     half = row_count * cols
     slabs = lax.axis_size("slab")
-    assert lax.axis_size("pen") == 2 and slabs > 2
+    assert lax.axis_size("pen") == 2 and slabs > 2 and slabs % 2 == 0
     assert profiles.shape[1] == planes + 1
     depth_total = planes * slabs
     cells = float(depth_total * 2 * half)
@@ -372,7 +379,7 @@
     crossings = [(turn(slab) + turn((slab + step) % slabs)) % 2 for step in (1, slabs - 1)]
     first_plane = slab * planes
     weights = plane_weights(atom_planes, profiles, first_plane + jnp.arange(planes, dtype=jnp.int32), depth_total)
-    where = jnp.stack([lax.axis_index("orb") * chip_count + core * own, core, *crossings]).astype(jnp.int32)
+    where = jnp.stack([lax.axis_index("orb") * chip_count + core * own, core, *crossings, slab % 2]).astype(jnp.int32)
     own_energies = lax.dynamic_slice(energies, (core * own,), (own,)).reshape(own, 1)
     weights = jnp.concatenate([weights, couplings.reshape(1, natoms)], axis=0)
 
@@ -392,31 +399,31 @@
     )
     gram_sum = summed(gram_part)
     gram_other = swap_cores(gram_sum)
-    r0, down, up, pc, inv, own_orbitals = call(
+    r0, even, odd, pc, inv, own_orbitals = call(
         functools.partial(source_body, own=own, planes=planes, natoms=natoms, cells=cells),
         (where, gram_sum, gram_other, mine, other, *stats, weights), "skkhhkkk",
         [field, edge, edge, part, (total, total), field],
     )
-    lo, hi = from_neighbours(up, down)
-    first, down, up, first_pc = call(
+    odd, even = from_neighbours(even, odd)
+    first, even, odd, first_pc = call(
         functools.partial(first_body, own=own, natoms=natoms, cols=cols),
-        (where, r0, pc, lo, hi, *stats, weights, own_energies), "skkkkkkkk", [field, edge, edge, part],
-    )
-    lo, hi = from_neighbours(up, down)
+        (where, r0, pc, odd, even, *stats, weights, own_energies), "skkkkkkkk", [field, edge, edge, part],
+    )
+    odd, even = from_neighbours(even, odd)
     target, sums_part = call(
         functools.partial(target_body, own=own, planes=planes, cols=cols),
-        (frequency, first, first_pc, lo, hi, *stats, weights, own_energies, r0, mine, other), "skkkkkkkkkhh",
+        (where, frequency, first, first_pc, odd, even, *stats, weights, own_energies, r0, mine, other), "sskkkkkkkkkhh",
         [field, (own, 2 * total)],
     )
     sums = summed(sums_part)
-    r1, down, up, pc = call(
+    r1, even, odd, pc = call(
         functools.partial(residual_body, own=own, planes=planes, natoms=natoms, cells=cells),
         (where, frequency, sums, inv, r0, target, mine, other, *stats, weights), "sskkkkvvkkk", [field, edge, edge, part],
     )
-    lo, hi = from_neighbours(up, down)
+    odd, even = from_neighbours(even, odd)
     last, lines = call(
         functools.partial(last_body, own=own, cols=cols),
-        (r1, pc, lo, hi, *stats, weights, own_energies, r0, first), "kkkkkkkkkk",
+        (where, r1, pc, odd, even, *stats, weights, own_energies, r0, first), "skkkkkkkkkk",
         [field, (1, 2 * total)],
     )
     lines = summed(lines)

time: 231 us -> 232 us (level)
  waiting for transfers between devices: 12.4 us -> 18.6 us
  blocking collectives: 156 us -> 150 us
  starting transfers between devices: 33.7 us -> 29.2 us
  Pallas kernels: 21.6 us -> 25.9 us
    psum x3, blocking collectives: 106 us -> 98.2 us  [summed(): return lax.psum(array, ('slab', 'pen'), axis_index_groups=across)]
    ppermute x6, waiting for transfers between devices: 4.94 us -> 11.9 us  [the longest x3 6.72 us: from_neighbours(): lax.ppermute(even_edge, axes, pairs(0))]
    ppermute x6, starting transfers between devices: 21.7 us -> 17 us  [the longest x3 11.1 us: from_neighbours(): lax.ppermute(odd_edge, axes, pairs(1))]
    pallas_call x7, Pallas kernels: 21.6 us -> 25.9 us  [call(): pl.pallas_call(body, in_specs=[SMEM if k == 's' else pl.BlockSpec(memory_...]
  transfers between devices with their start and end apart: 11 -> 11, of which waited for: 9 -> 8; matrix products, arithmetic and copies ran while one was open for 1% -> 1% of each run, Pallas kernels for 0% -> 0%
where the time goes in v5:
time: 232 us; the launch traced here: 231 us
  blocking collectives  150 us (65%)
  starting transfers between devices  29.2 us (13%)
  Pallas kernels  25.9 us (11%)
  waiting for transfers between devices  18.6 us (8%)
  local copies, waits for them, and re-layouts  5.59 us (2%)
    psum x3, blocking collectives, summed(): return lax.psum(array, ('slab', 'pen'), axis_index_groups=across)  98.2 us
    psum x3, blocking collectives, summed(): array = lax.psum(array, ('slab', 'pen'), axis_index_groups=runs)  31.9 us
    pallas_call x7, Pallas kernels, call(): pl.pallas_call(body, in_specs=[SMEM if k == 's' else pl.BlockSpec(memory_...  25.9 us
    all_to_all x1, blocking collectives, copy_for_each(): return lax.all_to_all(copies, axis, split_axis=0, concat_axis=0, tiled=True)  19.7 us
    ppermute x3, starting transfers between devices, from_neighbours(): lax.ppermute(odd_edge, axes, pairs(1))  11.1 us
    ppermute x4, starting transfers between devices, swap_cores(): return lax.ppermute(array, 'pen', [(0, 1), (1, 0)])  8.81 us
    ppermute x3, waiting for transfers between devices, from_neighbours(): lax.ppermute(even_edge, axes, pairs(0))  6.72 us
    ppermute x3, starting transfers between devices, from_neighbours(): lax.ppermute(even_edge, axes, pairs(0))  5.85 us
  transfers between devices with their start and end apart: 11, of which 8 were waited for; matrix products, arithmetic and copies ran while one was open for 1% of the time, Pallas kernels for 0%

profile of v5, /device:TPU:40, one launch (start us, length us, event | category | flops | bytes accessed | tf_op | source)
XLA Modules:
  0.0 231.1 jit_solution(14254197648398234048)
XLA Ops:
  0.6 0.0 copy-start
  0.6 1.1 reshape.69
  1.7 0.1 broadcast_in_dim.4
  1.8 0.0 copy-start.3
  1.8 0.0 copy-start.2
  1.8 19.7 %all_to_all.10 = f32[4,16,4096]{2,1,0:T(8,128)S(1)} all-to-all(f32[4,16,4096]{2,1,0:T(8,128)S(1)} %broadcast_in_dim.4), channel_id=1, replica_groups=mesh['parts'=2,'slab'=32,'orb'=4,'pen'=2] {'orb'}, dimensions={0} | all-to-all | bytes 2097152 | tf_op jit(solution)/shard_map/all_to_all | solution.py:324
  21.5 0.0 copy-start.1
  21.5 1.9 collective-permute-start
  23.5 0.0 copy-done.3
  23.5 0.0 copy-start.4
  23.5 0.7 copy-done.4
  24.2 0.0 copy-done.2
  24.2 0.1 copy.18
  24.4 0.0 copy-done.1
  24.4 2.4 %collective-permute-start.1 = (f32[136,1024]{1,0:T(8,128)S(1)}, f32[136,1024]{1,0:T(8,128)S(1)}, u32[]{:S(2)}, u32[]{:S(2)}) collective-permute-start(f32[136,1024]{1,0:T(8,128)S(1)} %pad_maximum_fusion.stat_m), channel_id=1, source_target_pairs={{0,1},{1,0},{2,3},{3,2},{4,5},{5,4},{6,7},{7,6},{8,9},{9,8},{10,11... | collective-permute-start | bytes 1671176 | tf_op jit(solution)/shard_map/ppermute | solution.py:328
  27.0 0.0 copy-start.5
  27.0 0.6 stack.23.where_ref
  27.6 0.0 copy-start.6
  27.6 0.6 copy-done.6
  28.3 0.0 copy-done.5
  28.3 0.1 select_reduce_fusion
  28.4 0.0 collective-permute-done.1.stat_o
  28.4 0.0 collective-permute-done.other_ref.other_hbm
  28.4 3.5 %shard_map.104 = f32[16,128]{1,0:T(8,128)S(1)} custom-call(s32[5]{0:T(128)} %stack.23.where_ref, f32[64,4096]{1,0:T(8,128)} %bitcast.16, f32[64,4096]{1,0:T(8,128)} %collective-permute-done.other_ref.other_hbm, f32[136,1024]{1,0:T(8,128)S(1)} %pad_maximum_fusion.stat_m, f32[136,1024]{1,0:T(8,128)S(1)} %collective-permute-done.1.stat_o), custom_call_target="tpu_custom_call" | custom-call | tf_op jit(solution)/shard_map/pallas_call | solution.py:31
  31.9 14.8 %psum.42 = f32[16,128]{1,0:T(8,128)S(1)} all-reduce(f32[16,128]{1,0:T(8,128)S(1)} %shard_map.104), channel_id=1, replica_groups={{0,9,16,25},{33,40,49,56},{64,73,80,89},{97,104,113,120},{128,137,144,1..., use_global_device_ids=true, to_apply=%region_0.1 | all-reduce | flops 2048 | bytes 16384 | tf_op jit(solution)/shard_map/psum | solution.py:343
  46.7 57.3 %psum.43.sums_ref = f32[16,128]{1,0:T(8,128)S(1)} all-reduce(f32[16,128]{1,0:T(8,128)S(1)} %psum.42), channel_id=1, replica_groups={{0,33,64,97,128,161,192,225},{9,40,73,104,137,168,201,232},{16,49,80,11..., use_global_device_ids=true, to_apply=%region_1.2 | all-reduce | flops 2048 | bytes 16384 | tf_op jit(solution)/shard_map/psum | solution.py:344
  104.1 0.0 copy-start.7
  104.1 2.3 collective-permute-start.2
  106.4 0.0 copy-done.7
  106.4 0.8 collective-permute-done.2.swapped_ref
  107.2 11.5 %shard_map.105 = (f32[32,2048]{1,0:T(8,128)S(1)}, f32[8,2176]{1,0:T(8,128)S(1)}, f32[8,2176]{1,0:T(8,128)S(1)}, f32[8,128]{1,0:T(8,128)S(1)}, f32[64,64]{1,0:T(8,128)S(1)}, /*index=5*/f32[32,2048]{1,0:T(8,128)S(1)}) custom-call(s32[5]{0:T(128)} %stack.23.where_ref, f32[16,128]{1,0:T(8,128)S(1)} %psum.43.sums_ref, ...), custom_call_target="tpu_custom_call" | custom-call | tf_op jit(solution)/shard_map/pallas_call | solution.py:31
  118.7 2.0 collective-permute-start.3
  120.6 2.0 collective-permute-start.4
  122.6 0.0 copy-done
  122.6 0.1 dynamic-slice_bitcast_fusion
  122.7 0.1 copy.15.en_ref
  122.8 3.5 %collective-permute-done.3.odd_ref = f32[8,2176]{1,0:T(8,128)S(1)} collective-permute-done((f32[8,2176]{1,0:T(8,128)S(1)}, f32[8,2176]{1,0:T(8,128)S(1)}, u32[]{:S(2)}, u32[]{:S(2)}) %collective-permute-start.3) | collective-permute-done | bytes 69664 | tf_op jit(solution)/shard_map/ppermute | solution.py:355
  126.2 0.3 collective-permute-done.4.even_ref
  126.5 1.6 shard_map.106
  128.1 5.5 %collective-permute-start.5 = (f32[8,2176]{1,0:T(8,128)S(1)}, f32[8,2176]{1,0:T(8,128)S(1)}, u32[]{:S(2)}, u32[]{:S(2)}) collective-permute-start(f32[8,2176]{1,0:T(8,128)S(1)} %get-tuple-element.29), channel_id=1, source_target_pairs={{9,16},{8,17},{16,9},{17,8},{25,33},{24,32},{33,25},{32,24},{40,49... | collective-permute-start | bytes 208904 | tf_op jit(solution)/shard_map/ppermute | solution.py:355
  133.6 2.0 collective-permute-start.6
  136.2 0.0 collective-permute-done.5.odd_ref
  136.2 3.8 %collective-permute-done.6.even_ref = f32[8,2176]{1,0:T(8,128)S(1)} collective-permute-done((f32[8,2176]{1,0:T(8,128)S(1)}, f32[8,2176]{1,0:T(8,128)S(1)}, u32[]{:S(2)}, u32[]{:S(2)}) %collective-permute-start.6) | collective-permute-done | bytes 69664 | tf_op jit(solution)/shard_map/ppermute | solution.py:355
  140.0 4.6 %shard_map.107 = (f32[32,2048]{1,0:T(8,128)S(1)}, f32[8,128]{1,0:T(8,128)S(1)}) custom-call(s32[5]{0:T(128)} %stack.23.where_ref, f32[1]{0:T(128)S(6)} %copy.21.freq_ref, f32[32,2048]{1,0:T(8,128)S(1)} %get-tuple-element.27.v_ref.f_ref, f32[8,128]{1,0:T(8,128)S(1)} %get-tuple-element.28.pc_ref, f32[8,2176]{1,0:T(8,128)S(1)} %collective-permute-done.5.odd_ref, ...), custom_call_target="tpu_custom_call" | custom-call | tf_op jit(solution)/shard_map/pallas_call | solution.py:31
  144.6 7.6 %psum.44 = f32[8,128]{1,0:T(8,128)S(1)} all-reduce(f32[8,128]{1,0:T(8,128)S(1)} %get-tuple-element.31), channel_id=1, replica_groups={{0,9,16,25},{33,40,49,56},{64,73,80,89},{97,104,113,120},{128,137,144,1..., use_global_device_ids=true, to_apply=%region_3.4 | all-reduce | flops 1024 | bytes 8192 | tf_op jit(solution)/shard_map/psum | solution.py:343
  152.2 20.6 %psum.45.sums_ref = f32[8,128]{1,0:T(8,128)S(1)} all-reduce(f32[8,128]{1,0:T(8,128)S(1)} %psum.44), channel_id=1, replica_groups={{0,33,64,97,128,161,192,225},{9,40,73,104,137,168,201,232},{16,49,80,11..., use_global_device_ids=true, to_apply=%region_4.5 | all-reduce | flops 1024 | bytes 8192 | tf_op jit(solution)/shard_map/psum | solution.py:344
  172.8 3.1 %shard_map.108 = (f32[32,2048]{1,0:T(8,128)S(1)}, f32[8,2176]{1,0:T(8,128)S(1)}, f32[8,2176]{1,0:T(8,128)S(1)}, f32[8,128]{1,0:T(8,128)S(1)}) custom-call(s32[5]{0:T(128)} %stack.23.where_ref, f32[1]{0:T(128)S(6)} %copy.21.freq_ref, f32[8,128]{1,0:T(8,128)S(1)} %psum.45.sums_ref, f32[64,64]{1,0:T(8,128)S(1)} %get-tuple-element.32.inv_ref, ...), custom_call_target="tpu_custom_call" | custom-call | tf_op jit(solution)/shard_map/pallas_call | solution.py:31
  175.9 3.7 %collective-permute-start.7 = (f32[8,2176]{1,0:T(8,128)S(1)}, f32[8,2176]{1,0:T(8,128)S(1)}, u32[]{:S(2)}, u32[]{:S(2)}) collective-permute-start(f32[8,2176]{1,0:T(8,128)S(1)} %get-tuple-element.36), channel_id=1, source_target_pairs={{9,16},{8,17},{16,9},{17,8},{25,33},{24,32},{33,25},{32,24},{40,49... | collective-permute-start | bytes 208904 | tf_op jit(solution)/shard_map/ppermute | solution.py:355
  179.6 2.0 collective-permute-start.8
  181.6 1.8 collective-permute-done.7.odd_ref
  183.4 2.7 %collective-permute-done.8.even_ref = f32[8,2176]{1,0:T(8,128)S(1)} collective-permute-done((f32[8,2176]{1,0:T(8,128)S(1)}, f32[8,2176]{1,0:T(8,128)S(1)}, u32[]{:S(2)}, u32[]{:S(2)}) %collective-permute-start.8) | collective-permute-done | bytes 69664 | tf_op jit(solution)/shard_map/ppermute | solution.py:355
  186.0 1.2 shard_map.109
  187.3 9.5 %psum.46 = f32[1,128]{1,0:T(1,128)S(1)} all-reduce(f32[1,128]{1,0:T(1,128)S(1)} %get-tuple-element.38), channel_id=1, replica_groups={{0,9,16,25},{33,40,49,56},{64,73,80,89},{97,104,113,120},{128,137,144,1..., use_global_device_ids=true, to_apply=%region_5.6 | all-reduce | flops 128 | bytes 1024 | tf_op jit(solution)/shard_map/psum | solution.py:343
  196.8 20.3 %psum.47.lines_ref = f32[1,128]{1,0:T(1,128)S(1)} all-reduce(f32[1,128]{1,0:T(1,128)S(1)} %psum.46), channel_id=1, replica_groups={{0,33,64,97,128,161,192,225},{9,40,73,104,137,168,201,232},{16,49,80,11..., use_global_device_ids=true, to_apply=%region_6.7 | all-reduce | flops 128 | bytes 1024 | tf_op jit(solution)/shard_map/psum | solution.py:344
  217.1 0.3 shard_map.110
  217.4 2.1 collective-permute-start.9
  219.5 1.3 collective-permute-done.9
  220.9 0.6 broadcast_in_dim.5
  221.5 3.4 %all-to-all-start.1 = ((f32[4,4,1024]{2,1,0:T(4,128)}), f32[4,4,1024]{2,1,0:T(4,128)S(1)}, u32[]{:S(2)}, u32[]{:S(2)}) async-start(f32[4,4,1024]{2,1,0:T(4,128)} %broadcast_in_dim.5), calls=%async_computation.1 | async-start | bytes 131072 | tf_op jit(solution)/shard_map/all_to_all | solution.py:324
  225.0 0.9 reshape.76
  225.8 4.6 %all-to-all-done.1 = f32[4,4,1024]{2,1,0:T(4,128)S(1)} async-done(((f32[4,4,1024]{2,1,0:T(4,128)}), f32[4,4,1024]{2,1,0:T(4,128)S(1)}, u32[]{:S(2)}, u32[]{:S(2)}) %all-to-all-start.1) | async-done | bytes 65568 | tf_op jit(solution)/shard_map/all_to_all | solution.py:324
  230.5 0.6 mul.35
  (12 shorter events, 0.2 us)
Async XLA Ops:
  0.6 122.0 %copy-start = (f32[16]{0:T(128)S(1)}, f32[16]{0:T(128)}, u32[]{:S(2)}) copy-start(f32[16]{0:T(128)} %param.10) | copy-start | bytes 196
  1.8 21.7 %copy-start.3 = (f32[4,4,256]{2,1,0:T(4,128)S(1)}, f32[4,4,256]{2,1,0:T(4,128)}, u32[]{:S(2)}) copy-start(f32[4,4,256]{2,1,0:T(4,128)} %param.12) | copy-start | bytes 49156
  1.8 22.4 %copy-start.2 = (f32[128,4,256]{2,1,0:T(4,128)S(1)}, f32[128,4,256]{2,1,0:T(4,128)}, u32[]{:S(2)}) copy-start(f32[128,4,256]{2,1,0:T(4,128)} %param.14) | copy-start | bytes 1572868
  21.5 2.8 %copy-start.1 = (f32[4,16,4096]{2,1,0:T(8,128)}, f32[4,16,4096]{2,1,0:T(8,128)S(1)}, u32[]{:S(2)}) copy-start(f32[4,16,4096]{2,1,0:T(8,128)S(1)} %all_to_all.10) | copy-start | bytes 3145732
  21.5 6.9 %collective-permute-start = (f32[64,4096]{1,0:T(8,128)S(1)}, f32[64,4096]{1,0:T(8,128)}, u32[]{:S(2)}, u32[]{:S(2)}) collective-permute-start(f32[64,4096]{1,0:T(8,128)S(1)} %bitcast.15), channel_id=1, source_target_pairs={{0,1},{1,0},{2,3},{3,2},{4,5},{5,4},{6,7},{7,6},{8,9},{9,8},{10,11... | collective-permute-start | bytes 3145736 | tf_op jit(solution)/shard_map/ppermute | solution.py:328
  23.5 0.7 copy-start.4
  24.4 4.0 %collective-permute-start.1 = (f32[136,1024]{1,0:T(8,128)S(1)}, f32[136,1024]{1,0:T(8,128)S(1)}, u32[]{:S(2)}, u32[]{:S(2)}) collective-permute-start(f32[136,1024]{1,0:T(8,128)S(1)} %pad_maximum_fusion.stat_m), channel_id=1, source_target_pairs={{0,1},{1,0},{2,3},{3,2},{4,5},{5,4},{6,7},{7,6},{8,9},{9,8},{10,11... | collective-permute-start | bytes 1671176 | tf_op jit(solution)/shard_map/ppermute | solution.py:328
  27.0 1.3 copy-start.5
  27.6 0.7 copy-start.6
  104.1 2.3 %copy-start.7 = (f32[128]{0:T(128)S(1)}, f32[128]{0:T(128)}, u32[]{:S(2)}) copy-start(f32[128]{0:T(128)} %param.16) | copy-start | bytes 1540
  104.1 3.1 %collective-permute-start.2 = (f32[16,128]{1,0:T(8,128)S(1)}, f32[16,128]{1,0:T(8,128)S(1)}, u32[]{:S(2)}, u32[]{:S(2)}) collective-permute-start(f32[16,128]{1,0:T(8,128)S(1)} %psum.43.sums_ref), channel_id=1, source_target_pairs={{0,1},{1,0},{2,3},{3,2},{4,5},{5,4},{6,7},{7,6},{8,9},{9,8},{10,11... | collective-permute-start | bytes 24584 | tf_op jit(solution)/shard_map/ppermute | solution.py:328
  118.7 7.6 %collective-permute-start.3 = (f32[8,2176]{1,0:T(8,128)S(1)}, f32[8,2176]{1,0:T(8,128)S(1)}, u32[]{:S(2)}, u32[]{:S(2)}) collective-permute-start(f32[8,2176]{1,0:T(8,128)S(1)} %get-tuple-element.25), channel_id=1, source_target_pairs={{9,16},{8,17},{16,9},{17,8},{25,33},{24,32},{33,25},{32,24},{40,49... | collective-permute-start | bytes 208904 | tf_op jit(solution)/shard_map/ppermute | solution.py:355
  120.6 5.9 %collective-permute-start.4 = (f32[8,2176]{1,0:T(8,128)S(1)}, f32[8,2176]{1,0:T(8,128)S(1)}, u32[]{:S(2)}, u32[]{:S(2)}) collective-permute-start(f32[8,2176]{1,0:T(8,128)S(1)} %get-tuple-element.26), channel_id=1, source_target_pairs={{0,9},{1,8},{9,0},{8,1},{16,25},{17,24},{25,16},{24,17},{33,40},{3... | collective-permute-start | bytes 208904 | tf_op jit(solution)/shard_map/ppermute | solution.py:355
  128.1 8.1 %collective-permute-start.5 = (f32[8,2176]{1,0:T(8,128)S(1)}, f32[8,2176]{1,0:T(8,128)S(1)}, u32[]{:S(2)}, u32[]{:S(2)}) collective-permute-start(f32[8,2176]{1,0:T(8,128)S(1)} %get-tuple-element.29), channel_id=1, source_target_pairs={{9,16},{8,17},{16,9},{17,8},{25,33},{24,32},{33,25},{32,24},{40,49... | collective-permute-start | bytes 208904 | tf_op jit(solution)/shard_map/ppermute | solution.py:355
  133.6 6.4 %collective-permute-start.6 = (f32[8,2176]{1,0:T(8,128)S(1)}, f32[8,2176]{1,0:T(8,128)S(1)}, u32[]{:S(2)}, u32[]{:S(2)}) collective-permute-start(f32[8,2176]{1,0:T(8,128)S(1)} %get-tuple-element.30), channel_id=1, source_target_pairs={{0,9},{1,8},{9,0},{8,1},{16,25},{17,24},{25,16},{24,17},{33,40},{3... | collective-permute-start | bytes 208904 | tf_op jit(solution)/shard_map/ppermute | solution.py:355
  175.9 7.4 %collective-permute-start.7 = (f32[8,2176]{1,0:T(8,128)S(1)}, f32[8,2176]{1,0:T(8,128)S(1)}, u32[]{:S(2)}, u32[]{:S(2)}) collective-permute-start(f32[8,2176]{1,0:T(8,128)S(1)} %get-tuple-element.36), channel_id=1, source_target_pairs={{9,16},{8,17},{16,9},{17,8},{25,33},{24,32},{33,25},{32,24},{40,49... | collective-permute-start | bytes 208904 | tf_op jit(solution)/shard_map/ppermute | solution.py:355
  179.6 6.4 %collective-permute-start.8 = (f32[8,2176]{1,0:T(8,128)S(1)}, f32[8,2176]{1,0:T(8,128)S(1)}, u32[]{:S(2)}, u32[]{:S(2)}) collective-permute-start(f32[8,2176]{1,0:T(8,128)S(1)} %get-tuple-element.37), channel_id=1, source_target_pairs={{0,9},{1,8},{9,0},{8,1},{16,25},{17,24},{25,16},{24,17},{33,40},{3... | collective-permute-start | bytes 208904 | tf_op jit(solution)/shard_map/ppermute | solution.py:355
  217.4 3.5 %collective-permute-start.9 = (f32[16,4096]{1,0:T(8,128)S(1)}, f32[16,4096]{1,0:T(8,128)S(1)}, u32[]{:S(2)}, u32[]{:S(2)}) collective-permute-start(f32[16,4096]{1,0:T(8,128)S(1)} %get-tuple-element.42), channel_id=1, source_target_pairs={{0,1},{1,0},{2,3},{3,2},{4,5},{5,4},{6,7},{7,6},{8,9},{9,8},{10,11... | collective-permute-start | bytes 786440 | tf_op jit(solution)/shard_map/ppermute | solution.py:328
  221.5 8.9 %all-to-all-start.1 = ((f32[4,4,1024]{2,1,0:T(4,128)}), f32[4,4,1024]{2,1,0:T(4,128)S(1)}, u32[]{:S(2)}, u32[]{:S(2)}) async-start(f32[4,4,1024]{2,1,0:T(4,128)} %broadcast_in_dim.5), calls=%async_computation.1 | async-start | bytes 131072 | tf_op jit(solution)/shard_map/all_to_all | solution.py:324

commit v6 on v5

--- a/solution.py
+++ b/solution.py
@@ -41,6 +41,19 @@
     return [pltpu.make_async_copy(a, b, sems.at[i]) for i, (a, b) in enumerate(pairs)]
 
 
+BELOW = 5
+
+
+def flag(w_ref, row, shape):
+    at = w_ref.shape[0] - BELOW + row
+    return jnp.broadcast_to(w_ref[at : at + 1, 0:1], shape) > 0.5
+
+
+def squared_frequency(w_ref):
+    at = w_ref.shape[0] - BELOW + 1
+    return w_ref[at : at + 1, 0:1]
+
+
 def orbital_row_sums(products, own):
     total = functools.reduce(jnp.add, products)
     folded = functools.reduce(jnp.add, [total[i : i + own] for i in range(0, total.shape[0], own)])
@@ -56,28 +69,26 @@
     sums = sum(
         dot_nt(v_ref[:, h * half : (h + 1) * half], stat_refs[h][0:natoms, :], three_passes) for h in range(2)
     )
-    planes = w_ref.shape[0] - 1
+    planes = w_ref.shape[0] - BELOW
     return sum(sums[z * own : (z + 1) * own] * w_ref[z : z + 1, :] for z in range(planes))
 
 
-def pack_edges(where_ref, v_ref, pc, even_ref, odd_ref, own):
+def pack_edges(w_ref, v_ref, pc, even_ref, odd_ref, own):
     width = v_ref.shape[1]
     half = width // 2
-    is_even = where_ref[4] == 0
+    is_even = flag(w_ref, 2, (own, width))
     top, bottom = v_ref[v_ref.shape[0] - own :, :], v_ref[0:own, :]
-    for ref, edge, crossing in (
-        (even_ref, jnp.where(is_even, top, bottom), jnp.where(is_even, where_ref[2], where_ref[3]) == 1),
-        (odd_ref, jnp.where(is_even, bottom, top), jnp.where(is_even, where_ref[3], where_ref[2]) == 1),
-    ):
+    for ref, edge, row in ((even_ref, jnp.where(is_even, top, bottom), 3), (odd_ref, jnp.where(is_even, bottom, top), 4)):
+        crossing = flag(w_ref, row, (own, half))
         ref[:, 0:half] = jnp.where(crossing, edge[:, half:], edge[:, 0:half])
         ref[:, half:width] = jnp.where(crossing, edge[:, 0:half], edge[:, half:])
         ref[:, width:] = pc
 
 
-def apply_shift(emit, where_ref, v_ref, pc_ref, odd_ref, even_ref, stat_refs, w_ref, en_ref, cols):
+def apply_shift(emit, v_ref, pc_ref, odd_ref, even_ref, stat_refs, w_ref, en_ref, cols):
     own = odd_ref.shape[0]
-    is_even = where_ref[4] == 0
-    planes, natoms = w_ref.shape[0] - 1, w_ref.shape[1]
+    is_even = flag(w_ref, 2, (own, cols))
+    planes, natoms = w_ref.shape[0] - BELOW, w_ref.shape[1]
     width = v_ref.shape[1]
     half = width // 2
     c = w_ref[planes : planes + 1, :] * (pc_ref[...] + odd_ref[:, width:] + even_ref[:, width:])
@@ -117,7 +128,7 @@
         for z in range(planes):
             at = slice(z * half, (z + 1) * half)
             source = stat[natoms + planes + z : natoms + planes + z + 1, :] * orb_ref[pl.ds(start, own), at]
-            sums = sums + dot_nt(jnp.concatenate([orb_ref[rows, at], source], axis=0), orb_ref[:, at])
+            sums = sums + dot_nt(jnp.concatenate([orb_ref[rows, at], source], axis=0), orb_ref[:, at], three_passes)
     gram, corr = sums[0:span], sums[span:]
     twice = jnp.concatenate([gram, gram], axis=1)
     ahead = jnp.where(where_ref[1] == 0, twice[:, 0:total], twice[:, span : span + total])
@@ -202,35 +213,35 @@
             r_ref[z * own : (z + 1) * own, h * half : (h + 1) * half] = dot_nn(g, orb_ref[:, at]) - source
     pc = inner_partials(r_ref, (stat_m, stat_o), w_ref, own, natoms)
     pc_ref[...] = pc
-    pack_edges(where_ref, r_ref, pc, even_edge, odd_edge, own)
+    pack_edges(w_ref, r_ref, pc, even_edge, odd_edge, own)
 
 
 def first_body(
-    where_ref, v_ref, pc_ref, odd_ref, even_ref, stat_m, stat_o, w_ref, en_ref,
+    v_ref, pc_ref, odd_ref, even_ref, stat_m, stat_o, w_ref, en_ref,
     f_ref, even_edge, odd_edge, out_pc_ref, *, own, natoms, cols,
 ):
     def emit(at, block):
         f_ref[:, at] = block
 
-    apply_shift(emit, where_ref, v_ref, pc_ref, odd_ref, even_ref, (stat_m, stat_o), w_ref, en_ref, cols)
+    apply_shift(emit, v_ref, pc_ref, odd_ref, even_ref, (stat_m, stat_o), w_ref, en_ref, cols)
     pc = inner_partials(f_ref, (stat_m, stat_o), w_ref, own, natoms)
     out_pc_ref[...] = pc
-    pack_edges(where_ref, f_ref, pc, even_edge, odd_edge, own)
+    pack_edges(w_ref, f_ref, pc, even_edge, odd_edge, own)
 
 
 def target_body(
-    where_ref, freq_ref, v_ref, pc_ref, odd_ref, even_ref, stat_m, stat_o, w_ref, en_ref, r_ref, mine_hbm, other_hbm,
+    v_ref, pc_ref, odd_ref, even_ref, stat_m, stat_o, w_ref, en_ref, r_ref, mine_hbm, other_hbm,
     t_ref, out_ref, mine_ref, other_ref, sems, *, own, planes, cols,
 ):
     arriving = copies([(mine_hbm, mine_ref), (other_hbm, other_ref)], sems)
     for copy in arriving:
         copy.start()
-    square = freq_ref[0] * freq_ref[0]
+    square = squared_frequency(w_ref)
 
     def emit(at, block):
         t_ref[:, at] = block + square * r_ref[:, at]
 
-    apply_shift(emit, where_ref, v_ref, pc_ref, odd_ref, even_ref, (stat_m, stat_o), w_ref, en_ref, cols)
+    apply_shift(emit, v_ref, pc_ref, odd_ref, even_ref, (stat_m, stat_o), w_ref, en_ref, cols)
     half = stat_m.shape[1]
     total = mine_ref.shape[0]
     corr = jnp.zeros((own, total), f32)
@@ -239,7 +250,7 @@
     for h, orb_ref in enumerate((mine_ref, other_ref)):
         for z in range(planes):
             block = t_ref[z * own : (z + 1) * own, h * half : (h + 1) * half]
-            corr = corr + dot_nt(block, orb_ref[:, z * half : (z + 1) * half])
+            corr = corr + dot_nt(block, orb_ref[:, z * half : (z + 1) * half], three_passes)
     rr = orbital_row_sums([b * b for b in lane_blocks(r_ref, cols)], own)
     ff = orbital_row_sums([b * b for b in lane_blocks(v_ref, cols)], own)
     lanes = out_ref.shape[1]
@@ -249,12 +260,12 @@
 
 
 def residual_body(
-    where_ref, freq_ref, sums_ref, inv_ref, r_ref, t_ref, mine_ref, other_ref, stat_m, stat_o, w_ref,
+    sums_ref, inv_ref, r_ref, t_ref, mine_ref, other_ref, stat_m, stat_o, w_ref,
     out_ref, even_edge, odd_edge, pc_ref, *, own, planes, natoms, cells,
 ):
     half = stat_m.shape[1]
     total = mine_ref.shape[0]
-    square = freq_ref[0] * freq_ref[0]
+    square = squared_frequency(w_ref)
     g = dot_nn(sums_ref[:, 0:total] / cells, inv_ref[...])
     rr, ff = sums_ref[:, total : total + 1], sums_ref[:, total + 1 : total + 2]
     step = rr / (ff + square * rr)
@@ -265,16 +276,16 @@
             out_ref[rows, at] = r_ref[rows, at] - step * image
     pc = inner_partials(out_ref, (stat_m, stat_o), w_ref, own, natoms)
     pc_ref[...] = pc
-    pack_edges(where_ref, out_ref, pc, even_edge, odd_edge, own)
+    pack_edges(w_ref, out_ref, pc, even_edge, odd_edge, own)
 
 
 def last_body(
-    where_ref, v_ref, pc_ref, odd_ref, even_ref, stat_m, stat_o, w_ref, en_ref, r_ref, f_ref, u_ref, out_ref, *, own, cols
+    v_ref, pc_ref, odd_ref, even_ref, stat_m, stat_o, w_ref, en_ref, r_ref, f_ref, u_ref, out_ref, *, own, cols
 ):
     def emit(at, block):
         u_ref[:, at] = block
 
-    apply_shift(emit, where_ref, v_ref, pc_ref, odd_ref, even_ref, (stat_m, stat_o), w_ref, en_ref, cols)
+    apply_shift(emit, v_ref, pc_ref, odd_ref, even_ref, (stat_m, stat_o), w_ref, en_ref, cols)
     r1, r0, u1, u0 = (lane_blocks(ref, cols) for ref in (v_ref, r_ref, u_ref, f_ref))
     values = [
         orbital_row_sums([a * b for a, b in zip(x, y)], own) for x, y in ((r1, r1), (u1, u1), (u1, u0), (r1, r0))
@@ -287,11 +298,11 @@
 
 
 def response_body(
-    freq_ref, sums_ref, lines_ref, f_ref, u_ref, own_ref, out_ref, swap_ref, dens_ref, *, own, planes
+    sums_ref, lines_ref, f_ref, u_ref, own_ref, w_ref, out_ref, swap_ref, dens_ref, *, own, planes
 ):
     total = sums_ref.shape[1] // 2
     half = f_ref.shape[1] // 2
-    square = freq_ref[0] * freq_ref[0]
+    square = squared_frequency(w_ref)
     rr0, ff = sums_ref[:, total : total + 1], sums_ref[:, total + 1 : total + 2]
     line = lines_ref[...]
     lanes = line.shape[1]
@@ -379,9 +390,14 @@
     crossings = [(turn(slab) + turn((slab + step) % slabs)) % 2 for step in (1, slabs - 1)]
     first_plane = slab * planes
     weights = plane_weights(atom_planes, profiles, first_plane + jnp.arange(planes, dtype=jnp.int32), depth_total)
-    where = jnp.stack([lax.axis_index("orb") * chip_count + core * own, core, *crossings, slab % 2]).astype(jnp.int32)
+    where = jnp.stack([lax.axis_index("orb") * chip_count + core * own, core]).astype(jnp.int32)
     own_energies = lax.dynamic_slice(energies, (core * own,), (own,)).reshape(own, 1)
-    weights = jnp.concatenate([weights, couplings.reshape(1, natoms)], axis=0)
+    up_even = slab % 2 == 0
+    flags = [up_even, jnp.where(up_even, *crossings), jnp.where(up_even, *crossings[::-1])]
+    below = jnp.stack([frequency[0] * frequency[0], *(f.astype(f32) for f in flags)])
+    weights = jnp.concatenate(
+        [weights, couplings.reshape(1, natoms), jnp.broadcast_to(below[:, None], (BELOW - 1, natoms))], axis=0
+    )
 
     stat_m = jnp.concatenate(
         [a.reshape(-1, half) for a in (projectors, local_potential, perturbation)], axis=0
@@ -407,29 +423,29 @@
     odd, even = from_neighbours(even, odd)
     first, even, odd, first_pc = call(
         functools.partial(first_body, own=own, natoms=natoms, cols=cols),
-        (where, r0, pc, odd, even, *stats, weights, own_energies), "skkkkkkkk", [field, edge, edge, part],
+        (r0, pc, odd, even, *stats, weights, own_energies), "kkkkkkkk", [field, edge, edge, part],
     )
     odd, even = from_neighbours(even, odd)
     target, sums_part = call(
         functools.partial(target_body, own=own, planes=planes, cols=cols),
-        (where, frequency, first, first_pc, odd, even, *stats, weights, own_energies, r0, mine, other), "sskkkkkkkkkhh",
+        (first, first_pc, odd, even, *stats, weights, own_energies, r0, mine, other), "kkkkkkkkkhh",
         [field, (own, 2 * total)],
     )
     sums = summed(sums_part)
     r1, even, odd, pc = call(
         functools.partial(residual_body, own=own, planes=planes, natoms=natoms, cells=cells),
-        (where, frequency, sums, inv, r0, target, mine, other, *stats, weights), "sskkkkvvkkk", [field, edge, edge, part],
+        (sums, inv, r0, target, mine, other, *stats, weights), "kkkkvvkkk", [field, edge, edge, part],
     )
     odd, even = from_neighbours(even, odd)
     last, lines = call(
         functools.partial(last_body, own=own, cols=cols),
-        (where, r1, pc, odd, even, *stats, weights, own_energies, r0, first), "skkkkkkkkkk",
+        (r1, pc, odd, even, *stats, weights, own_energies, r0, first), "kkkkkkkkkk",
         [field, (1, 2 * total)],
     )
     lines = summed(lines)
     response, to_other, dens = call(
         functools.partial(response_body, own=own, planes=planes),
-        (frequency, sums, lines, first, last, own_orbitals), "skkkkk",
+        (sums, lines, first, last, own_orbitals, weights), "kkkkkk",
         [(own, planes * half), (2 * own, planes * half), (1, planes * half)],
     )
     got = swap_cores(to_other)

time: 232 us -> 231 us (level)
  Pallas kernels: 25.9 us -> 21.9 us
    pallas_call x7, Pallas kernels: 25.9 us -> 21.9 us  [call(): pl.pallas_call(body, in_specs=[SMEM if k == 's' else pl.BlockSpec(memory_...]
  transfers between devices with their start and end apart: 11 -> 11, of which waited for: 8 -> 9; matrix products, arithmetic and copies ran while one was open for 1% -> 1% of each run, Pallas kernels for 0% -> 0%
where the time goes in v6:
time: 231 us; the launch traced here: 230 us
  blocking collectives  150 us (65%)
  starting transfers between devices  28.8 us (12%)
  Pallas kernels  21.9 us (9%)
  waiting for transfers between devices  19.7 us (9%)
  local copies, waits for them, and re-layouts  6.56 us (3%)
    psum x3, blocking collectives, summed(): return lax.psum(array, ('slab', 'pen'), axis_index_groups=across)  99.2 us
    psum x3, blocking collectives, summed(): array = lax.psum(array, ('slab', 'pen'), axis_index_groups=runs)  31.1 us
    pallas_call x7, Pallas kernels, call(): pl.pallas_call(body, in_specs=[SMEM if k == 's' else pl.BlockSpec(memory_...  21.9 us
    all_to_all x1, blocking collectives, copy_for_each(): return lax.all_to_all(copies, axis, split_axis=0, concat_axis=0, tiled=True)  19.7 us
    ppermute x3, starting transfers between devices, from_neighbours(): lax.ppermute(odd_edge, axes, pairs(1))  11.1 us
    ppermute x4, starting transfers between devices, swap_cores(): return lax.ppermute(array, 'pen', [(0, 1), (1, 0)])  8.49 us
    ppermute x3, waiting for transfers between devices, from_neighbours(): lax.ppermute(even_edge, axes, pairs(0))  7.12 us
    ppermute x3, starting transfers between devices, from_neighbours(): lax.ppermute(even_edge, axes, pairs(0))  5.85 us
  transfers between devices with their start and end apart: 11, of which 9 were waited for; matrix products, arithmetic and copies ran while one was open for 1% of the time, Pallas kernels for 0%

profile of v6, /device:TPU:40, one launch (start us, length us, event | category | flops | bytes accessed | tf_op | source)
XLA Modules:
  0.0 229.7 jit_solution(8801926668767462853)
XLA Ops:
  0.6 0.0 copy-start
  0.6 1.1 reshape.72
  1.7 0.1 broadcast_in_dim.6
  1.8 0.0 copy-start.5
  1.8 0.0 copy-start.4
  1.8 19.7 %all_to_all.10 = f32[4,16,4096]{2,1,0:T(8,128)S(1)} all-to-all(f32[4,16,4096]{2,1,0:T(8,128)S(1)} %broadcast_in_dim.6), channel_id=1, replica_groups=mesh['parts'=2,'slab'=32,'orb'=4,'pen'=2] {'orb'}, dimensions={0} | all-to-all | bytes 2097152 | tf_op jit(solution)/shard_map/all_to_all | solution.py:335
  21.5 1.9 collective-permute-start
  23.5 0.0 copy-done.5
  23.5 0.0 copy-start.6
  23.5 0.7 copy-done.6
  24.2 0.0 copy-done.4
  24.2 0.1 copy.18
  24.4 0.0 copy-done.3
  24.4 2.4 %collective-permute-start.1 = (f32[136,1024]{1,0:T(8,128)S(1)}, f32[136,1024]{1,0:T(8,128)S(1)}, u32[]{:S(2)}, u32[]{:S(2)}) collective-permute-start(f32[136,1024]{1,0:T(8,128)S(1)} %pad_maximum_fusion.stat_m), channel_id=1, source_target_pairs={{0,1},{1,0},{2,3},{3,2},{4,5},{5,4},{6,7},{7,6},{8,9},{9,8},{10,11... | collective-permute-start | bytes 1671176 | tf_op jit(solution)/shard_map/ppermute | solution.py:339
  27.0 0.0 copy-start.8
  27.7 0.6 pad_add_fusion.where_ref
  28.2 0.1 pad_maximum_fusion.2
  28.3 0.0 copy-done.8
  28.3 0.6 copy-done.7
  28.9 0.1 select_reduce_fusion
  29.0 0.0 collective-permute-done.1.stat_o
  29.0 0.0 collective-permute-done.other_ref.other_hbm
  29.0 2.7 %shard_map.104 = f32[16,128]{1,0:T(8,128)S(1)} custom-call(s32[2]{0:T(128)} %pad_add_fusion.where_ref, f32[64,4096]{1,0:T(8,128)} %bitcast.16, f32[64,4096]{1,0:T(8,128)} %collective-permute-done.other_ref.other_hbm, f32[136,1024]{1,0:T(8,128)S(1)} %pad_maximum_fusion.stat_m, f32[136,1024]{1,0:T(8,128)S(1)} %collective-permute-done.1.stat_o), custom_call_target="tpu_custom_call" | custom-call | tf_op jit(solution)/shard_map/pallas_call | solution.py:31
  31.7 14.6 %psum.42 = f32[16,128]{1,0:T(8,128)S(1)} all-reduce(f32[16,128]{1,0:T(8,128)S(1)} %shard_map.104), channel_id=1, replica_groups={{0,9,16,25},{33,40,49,56},{64,73,80,89},{97,104,113,120},{128,137,144,1..., use_global_device_ids=true, to_apply=%region_0.1 | all-reduce | flops 2048 | bytes 16384 | tf_op jit(solution)/shard_map/psum | solution.py:354
  46.3 57.6 %psum.43.sums_ref = f32[16,128]{1,0:T(8,128)S(1)} all-reduce(f32[16,128]{1,0:T(8,128)S(1)} %psum.42), channel_id=1, replica_groups={{0,33,64,97,128,161,192,225},{9,40,73,104,137,168,201,232},{16,49,80,11..., use_global_device_ids=true, to_apply=%region_1.2 | all-reduce | flops 2048 | bytes 16384 | tf_op jit(solution)/shard_map/psum | solution.py:355
  103.9 0.0 copy-start.9
  103.9 2.1 collective-permute-start.2
  106.0 0.0 copy-done.9
  106.0 0.1 maximum_maximum_fusion.w_ref
  106.1 0.9 collective-permute-done.2.swapped_ref
  107.0 11.5 %shard_map.105 = (f32[32,2048]{1,0:T(8,128)S(1)}, f32[8,2176]{1,0:T(8,128)S(1)}, f32[8,2176]{1,0:T(8,128)S(1)}, f32[8,128]{1,0:T(8,128)S(1)}, f32[64,64]{1,0:T(8,128)S(1)}, /*index=5*/f32[32,2048]{1,0:T(8,128)S(1)}) custom-call(s32[2]{0:T(128)} %pad_add_fusion.where_ref, f32[16,128]{1,0:T(8,128)S(1)} %psum.43.sums_ref, ...), custom_call_target="tpu_custom_call" | custom-call | tf_op jit(solution)/shard_map/pallas_call | solution.py:31
  118.5 2.0 collective-permute-start.3
  120.5 2.0 collective-permute-start.4
  122.4 0.1 dynamic-slice_bitcast_fusion
  122.5 0.1 copy.15.en_ref
  122.6 3.4 %collective-permute-done.3.odd_ref = f32[8,2176]{1,0:T(8,128)S(1)} collective-permute-done((f32[8,2176]{1,0:T(8,128)S(1)}, f32[8,2176]{1,0:T(8,128)S(1)}, u32[]{:S(2)}, u32[]{:S(2)}) %collective-permute-start.3) | collective-permute-done | bytes 69664 | tf_op jit(solution)/shard_map/ppermute | solution.py:366
  126.0 0.6 collective-permute-done.4.even_ref
  126.5 0.9 shard_map.106
  127.5 5.5 %collective-permute-start.5 = (f32[8,2176]{1,0:T(8,128)S(1)}, f32[8,2176]{1,0:T(8,128)S(1)}, u32[]{:S(2)}, u32[]{:S(2)}) collective-permute-start(f32[8,2176]{1,0:T(8,128)S(1)} %get-tuple-element.29), channel_id=1, source_target_pairs={{9,16},{8,17},{16,9},{17,8},{25,33},{24,32},{33,25},{32,24},{40,49... | collective-permute-start | bytes 208904 | tf_op jit(solution)/shard_map/ppermute | solution.py:366
  133.0 2.0 collective-permute-start.6
  134.9 0.5 collective-permute-done.5.odd_ref
  135.4 3.9 %collective-permute-done.6.even_ref = f32[8,2176]{1,0:T(8,128)S(1)} collective-permute-done((f32[8,2176]{1,0:T(8,128)S(1)}, f32[8,2176]{1,0:T(8,128)S(1)}, u32[]{:S(2)}, u32[]{:S(2)}) %collective-permute-start.6) | collective-permute-done | bytes 69664 | tf_op jit(solution)/shard_map/ppermute | solution.py:366
  139.3 2.7 %shard_map.107 = (f32[32,2048]{1,0:T(8,128)S(1)}, f32[8,128]{1,0:T(8,128)S(1)}) custom-call(f32[32,2048]{1,0:T(8,128)S(1)} %get-tuple-element.27.v_ref.f_ref, f32[8,128]{1,0:T(8,128)S(1)} %get-tuple-element.28.pc_ref, f32[8,2176]{1,0:T(8,128)S(1)} %collective-permute-done.5.odd_ref, f32[8,2176]{1,0:T(8,128)S(1)} %collective-permute-done.6.even_ref, ...), custom_call_target="tpu_custom_call" | custom-call | tf_op jit(solution)/shard_map/pallas_call | solution.py:31
  142.0 7.6 %psum.44 = f32[8,128]{1,0:T(8,128)S(1)} all-reduce(f32[8,128]{1,0:T(8,128)S(1)} %get-tuple-element.31), channel_id=1, replica_groups={{0,9,16,25},{33,40,49,56},{64,73,80,89},{97,104,113,120},{128,137,144,1..., use_global_device_ids=true, to_apply=%region_3.4 | all-reduce | flops 1024 | bytes 8192 | tf_op jit(solution)/shard_map/psum | solution.py:354
  149.6 20.5 %psum.45.sums_ref = f32[8,128]{1,0:T(8,128)S(1)} all-reduce(f32[8,128]{1,0:T(8,128)S(1)} %psum.44), channel_id=1, replica_groups={{0,33,64,97,128,161,192,225},{9,40,73,104,137,168,201,232},{16,49,80,11..., use_global_device_ids=true, to_apply=%region_4.5 | all-reduce | flops 1024 | bytes 8192 | tf_op jit(solution)/shard_map/psum | solution.py:355
  170.2 3.1 %shard_map.108 = (f32[32,2048]{1,0:T(8,128)S(1)}, f32[8,2176]{1,0:T(8,128)S(1)}, f32[8,2176]{1,0:T(8,128)S(1)}, f32[8,128]{1,0:T(8,128)S(1)}) custom-call(f32[8,128]{1,0:T(8,128)S(1)} %psum.45.sums_ref, f32[64,64]{1,0:T(8,128)S(1)} %get-tuple-element.32.inv_ref, f32[32,2048]{1,0:T(8,128)S(1)} %get-tuple-element.23.v_ref.r_ref, ...), custom_call_target="tpu_custom_call" | custom-call | tf_op jit(solution)/shard_map/pallas_call | solution.py:31
  173.3 0.0 copy-start.1
  173.3 0.7 copy-done.1
  174.0 3.6 %collective-permute-start.7 = (f32[8,2176]{1,0:T(8,128)S(1)}, f32[8,2176]{1,0:T(8,128)S(1)}, u32[]{:S(2)}, u32[]{:S(2)}) collective-permute-start(f32[8,2176]{1,0:T(8,128)S(1)} %get-tuple-element.36), channel_id=1, source_target_pairs={{9,16},{8,17},{16,9},{17,8},{25,33},{24,32},{33,25},{32,24},{40,49... | collective-permute-start | bytes 208904 | tf_op jit(solution)/shard_map/ppermute | solution.py:366
  177.7 2.0 collective-permute-start.8
  179.6 1.8 collective-permute-done.7.odd_ref
  181.5 2.6 %collective-permute-done.8.even_ref = f32[8,2176]{1,0:T(8,128)S(1)} collective-permute-done((f32[8,2176]{1,0:T(8,128)S(1)}, f32[8,2176]{1,0:T(8,128)S(1)}, u32[]{:S(2)}, u32[]{:S(2)}) %collective-permute-start.8) | collective-permute-done | bytes 69664 | tf_op jit(solution)/shard_map/ppermute | solution.py:366
  184.1 0.9 copy-done.2
  185.0 0.6 shard_map.109
  185.6 9.0 %psum.46 = f32[1,128]{1,0:T(1,128)S(1)} all-reduce(f32[1,128]{1,0:T(1,128)S(1)} %get-tuple-element.38), channel_id=1, replica_groups={{0,9,16,25},{33,40,49,56},{64,73,80,89},{97,104,113,120},{128,137,144,1..., use_global_device_ids=true, to_apply=%region_5.6 | all-reduce | flops 128 | bytes 1024 | tf_op jit(solution)/shard_map/psum | solution.py:354
  194.5 21.0 %psum.47.lines_ref = f32[1,128]{1,0:T(1,128)S(1)} all-reduce(f32[1,128]{1,0:T(1,128)S(1)} %psum.46), channel_id=1, replica_groups={{0,33,64,97,128,161,192,225},{9,40,73,104,137,168,201,232},{16,49,80,11..., use_global_device_ids=true, to_apply=%region_6.7 | all-reduce | flops 128 | bytes 1024 | tf_op jit(solution)/shard_map/psum | solution.py:355
  215.5 0.4 shard_map.110
  216.0 2.1 collective-permute-start.9
  218.0 1.4 collective-permute-done.9
  219.5 0.6 broadcast_in_dim.8
  220.1 3.4 %all-to-all-start.1 = ((f32[4,4,1024]{2,1,0:T(4,128)}), f32[4,4,1024]{2,1,0:T(4,128)S(1)}, u32[]{:S(2)}, u32[]{:S(2)}) async-start(f32[4,4,1024]{2,1,0:T(4,128)} %broadcast_in_dim.8), calls=%async_computation.1 | async-start | bytes 131072 | tf_op jit(solution)/shard_map/all_to_all | solution.py:335
  223.5 0.9 reshape.79
  224.4 4.6 %all-to-all-done.1 = f32[4,4,1024]{2,1,0:T(4,128)S(1)} async-done(((f32[4,4,1024]{2,1,0:T(4,128)}), f32[4,4,1024]{2,1,0:T(4,128)S(1)}, u32[]{:S(2)}, u32[]{:S(2)}) %all-to-all-start.1) | async-done | bytes 65568 | tf_op jit(solution)/shard_map/all_to_all | solution.py:335
  229.1 0.6 mul.40
  (15 shorter events, 0.2 us)
Async XLA Ops:
  0.6 121.8 %copy-start = (f32[16]{0:T(128)S(1)}, f32[16]{0:T(128)}, u32[]{:S(2)}) copy-start(f32[16]{0:T(128)} %param.10) | copy-start | bytes 196
  1.8 21.7 %copy-start.5 = (f32[4,4,256]{2,1,0:T(4,128)S(1)}, f32[4,4,256]{2,1,0:T(4,128)}, u32[]{:S(2)}) copy-start(f32[4,4,256]{2,1,0:T(4,128)} %param.12) | copy-start | bytes 49156
  1.8 22.4 %copy-start.4 = (f32[128,4,256]{2,1,0:T(4,128)S(1)}, f32[128,4,256]{2,1,0:T(4,128)}, u32[]{:S(2)}) copy-start(f32[128,4,256]{2,1,0:T(4,128)} %param.14) | copy-start | bytes 1572868
  21.5 2.8 %copy-start.3 = (f32[4,16,4096]{2,1,0:T(8,128)}, f32[4,16,4096]{2,1,0:T(8,128)S(1)}, u32[]{:S(2)}) copy-start(f32[4,16,4096]{2,1,0:T(8,128)S(1)} %all_to_all.10) | copy-start | bytes 3145732
  21.5 7.5 %collective-permute-start = (f32[64,4096]{1,0:T(8,128)S(1)}, f32[64,4096]{1,0:T(8,128)}, u32[]{:S(2)}, u32[]{:S(2)}) collective-permute-start(f32[64,4096]{1,0:T(8,128)S(1)} %bitcast.15), channel_id=1, source_target_pairs={{0,1},{1,0},{2,3},{3,2},{4,5},{5,4},{6,7},{7,6},{8,9},{9,8},{10,11... | collective-permute-start | bytes 3145736 | tf_op jit(solution)/shard_map/ppermute | solution.py:339
  23.5 0.7 copy-start.6
  24.4 4.6 %collective-permute-start.1 = (f32[136,1024]{1,0:T(8,128)S(1)}, f32[136,1024]{1,0:T(8,128)S(1)}, u32[]{:S(2)}, u32[]{:S(2)}) collective-permute-start(f32[136,1024]{1,0:T(8,128)S(1)} %pad_maximum_fusion.stat_m), channel_id=1, source_target_pairs={{0,1},{1,0},{2,3},{3,2},{4,5},{5,4},{6,7},{7,6},{8,9},{9,8},{10,11... | collective-permute-start | bytes 1671176 | tf_op jit(solution)/shard_map/ppermute | solution.py:339
  27.0 1.3 copy-start.8
  28.2 0.7 copy-start.7
  103.9 2.1 copy-start.9
  103.9 3.1 %collective-permute-start.2 = (f32[16,128]{1,0:T(8,128)S(1)}, f32[16,128]{1,0:T(8,128)S(1)}, u32[]{:S(2)}, u32[]{:S(2)}) collective-permute-start(f32[16,128]{1,0:T(8,128)S(1)} %psum.43.sums_ref), channel_id=1, source_target_pairs={{0,1},{1,0},{2,3},{3,2},{4,5},{5,4},{6,7},{7,6},{8,9},{9,8},{10,11... | collective-permute-start | bytes 24584 | tf_op jit(solution)/shard_map/ppermute | solution.py:339
  118.5 7.4 %collective-permute-start.3 = (f32[8,2176]{1,0:T(8,128)S(1)}, f32[8,2176]{1,0:T(8,128)S(1)}, u32[]{:S(2)}, u32[]{:S(2)}) collective-permute-start(f32[8,2176]{1,0:T(8,128)S(1)} %get-tuple-element.25), channel_id=1, source_target_pairs={{9,16},{8,17},{16,9},{17,8},{25,33},{24,32},{33,25},{32,24},{40,49... | collective-permute-start | bytes 208904 | tf_op jit(solution)/shard_map/ppermute | solution.py:366
  120.5 6.1 %collective-permute-start.4 = (f32[8,2176]{1,0:T(8,128)S(1)}, f32[8,2176]{1,0:T(8,128)S(1)}, u32[]{:S(2)}, u32[]{:S(2)}) collective-permute-start(f32[8,2176]{1,0:T(8,128)S(1)} %get-tuple-element.26), channel_id=1, source_target_pairs={{0,9},{1,8},{9,0},{8,1},{16,25},{17,24},{25,16},{24,17},{33,40},{3... | collective-permute-start | bytes 208904 | tf_op jit(solution)/shard_map/ppermute | solution.py:366
  127.5 7.9 %collective-permute-start.5 = (f32[8,2176]{1,0:T(8,128)S(1)}, f32[8,2176]{1,0:T(8,128)S(1)}, u32[]{:S(2)}, u32[]{:S(2)}) collective-permute-start(f32[8,2176]{1,0:T(8,128)S(1)} %get-tuple-element.29), channel_id=1, source_target_pairs={{9,16},{8,17},{16,9},{17,8},{25,33},{24,32},{33,25},{32,24},{40,49... | collective-permute-start | bytes 208904 | tf_op jit(solution)/shard_map/ppermute | solution.py:366
  133.0 6.4 %collective-permute-start.6 = (f32[8,2176]{1,0:T(8,128)S(1)}, f32[8,2176]{1,0:T(8,128)S(1)}, u32[]{:S(2)}, u32[]{:S(2)}) collective-permute-start(f32[8,2176]{1,0:T(8,128)S(1)} %get-tuple-element.30), channel_id=1, source_target_pairs={{0,9},{1,8},{9,0},{8,1},{16,25},{17,24},{25,16},{24,17},{33,40},{3... | collective-permute-start | bytes 208904 | tf_op jit(solution)/shard_map/ppermute | solution.py:366
  173.3 0.7 copy-start.1
  174.0 7.4 %collective-permute-start.7 = (f32[8,2176]{1,0:T(8,128)S(1)}, f32[8,2176]{1,0:T(8,128)S(1)}, u32[]{:S(2)}, u32[]{:S(2)}) collective-permute-start(f32[8,2176]{1,0:T(8,128)S(1)} %get-tuple-element.36), channel_id=1, source_target_pairs={{9,16},{8,17},{16,9},{17,8},{25,33},{24,32},{33,25},{32,24},{40,49... | collective-permute-start | bytes 208904 | tf_op jit(solution)/shard_map/ppermute | solution.py:366
  177.7 6.4 %collective-permute-start.8 = (f32[8,2176]{1,0:T(8,128)S(1)}, f32[8,2176]{1,0:T(8,128)S(1)}, u32[]{:S(2)}, u32[]{:S(2)}) collective-permute-start(f32[8,2176]{1,0:T(8,128)S(1)} %get-tuple-element.37), channel_id=1, source_target_pairs={{0,9},{1,8},{9,0},{8,1},{16,25},{17,24},{25,16},{24,17},{33,40},{3... | collective-permute-start | bytes 208904 | tf_op jit(solution)/shard_map/ppermute | solution.py:366
  184.1 1.0 copy-start.2
  216.0 3.5 %collective-permute-start.9 = (f32[16,4096]{1,0:T(8,128)S(1)}, f32[16,4096]{1,0:T(8,128)S(1)}, u32[]{:S(2)}, u32[]{:S(2)}) collective-permute-start(f32[16,4096]{1,0:T(8,128)S(1)} %get-tuple-element.42), channel_id=1, source_target_pairs={{0,1},{1,0},{2,3},{3,2},{4,5},{5,4},{6,7},{7,6},{8,9},{9,8},{10,11... | collective-permute-start | bytes 786440 | tf_op jit(solution)/shard_map/ppermute | solution.py:339
  220.1 8.9 %all-to-all-start.1 = ((f32[4,4,1024]{2,1,0:T(4,128)}), f32[4,4,1024]{2,1,0:T(4,128)S(1)}, u32[]{:S(2)}, u32[]{:S(2)}) async-start(f32[4,4,1024]{2,1,0:T(4,128)} %broadcast_in_dim.8), calls=%async_computation.1 | async-start | bytes 131072 | tf_op jit(solution)/shard_map/all_to_all | solution.py:335

commit v7 on v6

--- a/solution.py
+++ b/solution.py
@@ -25,14 +25,17 @@
     return lax.dot_general(a, b, (((1,), (1,)), ((), ())), precision=precision, preferred_element_type=f32)
 
 
-def call(body, args, kinds, outs):
+def call(body, args, kinds, outs, last_in_hbm=False):
     late = [pltpu.VMEM(a.shape, f32) for a, k in zip(args, kinds, strict=True) if k == "h"]
     args = [pltpu.with_memory_space_constraint(a, pltpu.VMEM) if k == "k" else a for a, k in zip(args, kinds, strict=True)]
     return pl.pallas_call(
         body,
         in_specs=[SMEM if k == "s" else pl.BlockSpec(memory_space=pl.ANY) if k == "h" else VMEM for k in kinds],
         out_specs=[VMEM] * len(outs),
-        out_shape=[pltpu.VMEM(s, f32) for s in outs],
+        out_shape=[
+            jax.ShapeDtypeStruct(s, f32) if last_in_hbm and i == len(outs) - 1 else pltpu.VMEM(s, f32)
+            for i, s in enumerate(outs)
+        ],
         scratch_shapes=[*late, pltpu.SemaphoreType.DMA((len(late),))] if late else [],
     )(*args)
 
@@ -418,7 +421,7 @@
     r0, even, odd, pc, inv, own_orbitals = call(
         functools.partial(source_body, own=own, planes=planes, natoms=natoms, cells=cells),
         (where, gram_sum, gram_other, mine, other, *stats, weights), "skkhhkkk",
-        [field, edge, edge, part, (total, total), field],
+        [field, edge, edge, part, (total, total), field], last_in_hbm=True,
     )
     odd, even = from_neighbours(even, odd)
     first, even, odd, first_pc = call(
@@ -445,7 +448,7 @@
     lines = summed(lines)
     response, to_other, dens = call(
         functools.partial(response_body, own=own, planes=planes),
-        (sums, lines, first, last, own_orbitals, weights), "kkkkkk",
+        (sums, lines, first, last, own_orbitals, weights), "kkkkvk",
         [(own, planes * half), (2 * own, planes * half), (1, planes * half)],
     )
     got = swap_cores(to_other)

time: 231 us -> 230 us (level)
  no operation moved by 1% of the time
where the time goes in v7:
time: 230 us; the launch traced here: 229 us
  blocking collectives  150 us (65%)
  starting transfers between devices  28.9 us (13%)
  Pallas kernels  23.3 us (10%)
  waiting for transfers between devices  19.7 us (9%)
  local copies, waits for them, and re-layouts  4.91 us (2%)
    psum x3, blocking collectives, summed(): return lax.psum(array, ('slab', 'pen'), axis_index_groups=across)  99.3 us
    psum x3, blocking collectives, summed(): array = lax.psum(array, ('slab', 'pen'), axis_index_groups=runs)  30.9 us
    pallas_call x7, Pallas kernels, call(): pl.pallas_call(body, in_specs=[SMEM if k == 's' else pl.BlockSpec(memory_...  23.3 us
    all_to_all x1, blocking collectives, copy_for_each(): return lax.all_to_all(copies, axis, split_axis=0, concat_axis=0, tiled=True)  19.7 us
    ppermute x3, starting transfers between devices, from_neighbours(): lax.ppermute(odd_edge, axes, pairs(1))  11.1 us
    ppermute x4, starting transfers between devices, swap_cores(): return lax.ppermute(array, 'pen', [(0, 1), (1, 0)])  8.55 us
    ppermute x3, waiting for transfers between devices, from_neighbours(): lax.ppermute(even_edge, axes, pairs(0))  7.17 us
    ppermute x3, starting transfers between devices, from_neighbours(): lax.ppermute(even_edge, axes, pairs(0))  5.85 us
  transfers between devices with their start and end apart: 11, of which 9 were waited for; matrix products, arithmetic and copies ran while one was open for 1% of the time, Pallas kernels for 0%

profile of v7, /device:TPU:40, one launch (start us, length us, event | category | flops | bytes accessed | tf_op | source)
XLA Modules:
  0.0 229.5 jit_solution(5224554910376779705)
XLA Ops:
  0.6 0.0 copy-start
  0.6 1.1 reshape.72
  1.7 0.1 broadcast_in_dim.6
  1.8 0.0 copy-start.3
  1.8 0.0 copy-start.2
  1.8 19.7 %all_to_all.10 = f32[4,16,4096]{2,1,0:T(8,128)S(1)} all-to-all(f32[4,16,4096]{2,1,0:T(8,128)S(1)} %broadcast_in_dim.6), channel_id=1, replica_groups=mesh['parts'=2,'slab'=32,'orb'=4,'pen'=2] {'orb'}, dimensions={0} | all-to-all | bytes 2097152 | tf_op jit(solution)/shard_map/all_to_all | solution.py:338
  21.5 0.0 copy-start.1
  21.5 1.9 collective-permute-start
  23.5 0.0 copy-done.3
  23.5 0.0 copy-start.4
  23.5 0.7 copy-done.4
  24.2 0.0 copy-done.2
  24.2 0.1 copy.18
  24.4 0.0 copy-done.1
  24.4 2.4 %collective-permute-start.1 = (f32[136,1024]{1,0:T(8,128)S(1)}, f32[136,1024]{1,0:T(8,128)S(1)}, u32[]{:S(2)}, u32[]{:S(2)}) collective-permute-start(f32[136,1024]{1,0:T(8,128)S(1)} %pad_maximum_fusion.stat_m), channel_id=1, source_target_pairs={{0,1},{1,0},{2,3},{3,2},{4,5},{5,4},{6,7},{7,6},{8,9},{9,8},{10,11... | collective-permute-start | bytes 1671176 | tf_op jit(solution)/shard_map/ppermute | solution.py:342
  27.0 0.0 copy-start.6
  27.7 0.6 pad_add_fusion.where_ref
  28.3 0.0 copy-start.5
  28.3 0.1 pad_maximum_fusion.2
  28.4 0.0 copy-done.6
  28.4 0.6 copy-done.5
  29.0 0.1 select_reduce_fusion
  29.1 0.0 collective-permute-done.1.stat_o
  29.1 0.0 collective-permute-done.other_ref.other_hbm
  29.1 2.7 %shard_map.104 = f32[16,128]{1,0:T(8,128)S(1)} custom-call(s32[2]{0:T(128)} %pad_add_fusion.where_ref, f32[64,4096]{1,0:T(8,128)} %bitcast.16, f32[64,4096]{1,0:T(8,128)} %collective-permute-done.other_ref.other_hbm, f32[136,1024]{1,0:T(8,128)S(1)} %pad_maximum_fusion.stat_m, f32[136,1024]{1,0:T(8,128)S(1)} %collective-permute-done.1.stat_o), custom_call_target="tpu_custom_call" | custom-call | tf_op jit(solution)/shard_map/pallas_call | solution.py:31
  31.8 14.6 %psum.42 = f32[16,128]{1,0:T(8,128)S(1)} all-reduce(f32[16,128]{1,0:T(8,128)S(1)} %shard_map.104), channel_id=1, replica_groups={{0,9,16,25},{33,40,49,56},{64,73,80,89},{97,104,113,120},{128,137,144,1..., use_global_device_ids=true, to_apply=%region_0.1 | all-reduce | flops 2048 | bytes 16384 | tf_op jit(solution)/shard_map/psum | solution.py:357
  46.4 57.6 %psum.43.sums_ref = f32[16,128]{1,0:T(8,128)S(1)} all-reduce(f32[16,128]{1,0:T(8,128)S(1)} %psum.42), channel_id=1, replica_groups={{0,33,64,97,128,161,192,225},{9,40,73,104,137,168,201,232},{16,49,80,11..., use_global_device_ids=true, to_apply=%region_1.2 | all-reduce | flops 2048 | bytes 16384 | tf_op jit(solution)/shard_map/psum | solution.py:358
  104.0 0.0 copy-start.7
  104.0 2.1 collective-permute-start.2
  106.1 0.0 copy-done.7
  106.1 0.1 maximum_maximum_fusion.w_ref
  106.2 0.9 collective-permute-done.2.swapped_ref
  107.1 12.0 %shard_map.105 = (f32[32,2048]{1,0:T(8,128)S(1)}, f32[8,2176]{1,0:T(8,128)S(1)}, f32[8,2176]{1,0:T(8,128)S(1)}, f32[8,128]{1,0:T(8,128)S(1)}, f32[64,64]{1,0:T(8,128)S(1)}, /*index=5*/f32[32,2048]{1,0:T(8,128)}) custom-call(s32[2]{0:T(128)} %pad_add_fusion.where_ref, f32[16,128]{1,0:T(8,128)S(1)} %psum.43.sums_ref, ...), custom_call_target="tpu_custom_call" | custom-call | tf_op jit(solution)/shard_map/pallas_call | solution.py:31
  119.1 2.0 collective-permute-start.3
  121.0 2.0 collective-permute-start.4
  123.0 0.0 copy-done
  123.0 0.1 dynamic-slice_bitcast_fusion
  123.1 0.1 copy.15.en_ref
  123.2 3.4 %collective-permute-done.3.odd_ref = f32[8,2176]{1,0:T(8,128)S(1)} collective-permute-done((f32[8,2176]{1,0:T(8,128)S(1)}, f32[8,2176]{1,0:T(8,128)S(1)}, u32[]{:S(2)}, u32[]{:S(2)}) %collective-permute-start.3) | collective-permute-done | bytes 69664 | tf_op jit(solution)/shard_map/ppermute | solution.py:369
  126.5 0.6 collective-permute-done.4.even_ref
  127.1 0.9 shard_map.106
  128.0 5.5 %collective-permute-start.5 = (f32[8,2176]{1,0:T(8,128)S(1)}, f32[8,2176]{1,0:T(8,128)S(1)}, u32[]{:S(2)}, u32[]{:S(2)}) collective-permute-start(f32[8,2176]{1,0:T(8,128)S(1)} %get-tuple-element.29), channel_id=1, source_target_pairs={{9,16},{8,17},{16,9},{17,8},{25,33},{24,32},{33,25},{32,24},{40,49... | collective-permute-start | bytes 208904 | tf_op jit(solution)/shard_map/ppermute | solution.py:369
  133.5 2.0 collective-permute-start.6
  135.5 0.5 collective-permute-done.5.odd_ref
  136.0 3.9 %collective-permute-done.6.even_ref = f32[8,2176]{1,0:T(8,128)S(1)} collective-permute-done((f32[8,2176]{1,0:T(8,128)S(1)}, f32[8,2176]{1,0:T(8,128)S(1)}, u32[]{:S(2)}, u32[]{:S(2)}) %collective-permute-start.6) | collective-permute-done | bytes 69664 | tf_op jit(solution)/shard_map/ppermute | solution.py:369
  139.9 2.7 %shard_map.107 = (f32[32,2048]{1,0:T(8,128)S(1)}, f32[8,128]{1,0:T(8,128)S(1)}) custom-call(f32[32,2048]{1,0:T(8,128)S(1)} %get-tuple-element.27.v_ref.f_ref, f32[8,128]{1,0:T(8,128)S(1)} %get-tuple-element.28.pc_ref, f32[8,2176]{1,0:T(8,128)S(1)} %collective-permute-done.5.odd_ref, f32[8,2176]{1,0:T(8,128)S(1)} %collective-permute-done.6.even_ref, ...), custom_call_target="tpu_custom_call" | custom-call | tf_op jit(solution)/shard_map/pallas_call | solution.py:31
  142.6 7.6 %psum.44 = f32[8,128]{1,0:T(8,128)S(1)} all-reduce(f32[8,128]{1,0:T(8,128)S(1)} %get-tuple-element.31), channel_id=1, replica_groups={{0,9,16,25},{33,40,49,56},{64,73,80,89},{97,104,113,120},{128,137,144,1..., use_global_device_ids=true, to_apply=%region_3.4 | all-reduce | flops 1024 | bytes 8192 | tf_op jit(solution)/shard_map/psum | solution.py:357
  150.2 20.6 %psum.45.sums_ref = f32[8,128]{1,0:T(8,128)S(1)} all-reduce(f32[8,128]{1,0:T(8,128)S(1)} %psum.44), channel_id=1, replica_groups={{0,33,64,97,128,161,192,225},{9,40,73,104,137,168,201,232},{16,49,80,11..., use_global_device_ids=true, to_apply=%region_4.5 | all-reduce | flops 1024 | bytes 8192 | tf_op jit(solution)/shard_map/psum | solution.py:358
  170.8 3.1 %shard_map.108 = (f32[32,2048]{1,0:T(8,128)S(1)}, f32[8,2176]{1,0:T(8,128)S(1)}, f32[8,2176]{1,0:T(8,128)S(1)}, f32[8,128]{1,0:T(8,128)S(1)}) custom-call(f32[8,128]{1,0:T(8,128)S(1)} %psum.45.sums_ref, f32[64,64]{1,0:T(8,128)S(1)} %get-tuple-element.32.inv_ref, f32[32,2048]{1,0:T(8,128)S(1)} %get-tuple-element.23.v_ref.r_ref, ...), custom_call_target="tpu_custom_call" | custom-call | tf_op jit(solution)/shard_map/pallas_call | solution.py:31
  173.9 3.7 %collective-permute-start.7 = (f32[8,2176]{1,0:T(8,128)S(1)}, f32[8,2176]{1,0:T(8,128)S(1)}, u32[]{:S(2)}, u32[]{:S(2)}) collective-permute-start(f32[8,2176]{1,0:T(8,128)S(1)} %get-tuple-element.36), channel_id=1, source_target_pairs={{9,16},{8,17},{16,9},{17,8},{25,33},{24,32},{33,25},{32,24},{40,49... | collective-permute-start | bytes 208904 | tf_op jit(solution)/shard_map/ppermute | solution.py:369
  177.6 2.0 collective-permute-start.8
  179.6 1.8 collective-permute-done.7.odd_ref
  181.3 2.7 %collective-permute-done.8.even_ref = f32[8,2176]{1,0:T(8,128)S(1)} collective-permute-done((f32[8,2176]{1,0:T(8,128)S(1)}, f32[8,2176]{1,0:T(8,128)S(1)}, u32[]{:S(2)}, u32[]{:S(2)}) %collective-permute-start.8) | collective-permute-done | bytes 69664 | tf_op jit(solution)/shard_map/ppermute | solution.py:369
  184.0 0.5 shard_map.109
  184.5 8.8 %psum.46 = f32[1,128]{1,0:T(1,128)S(1)} all-reduce(f32[1,128]{1,0:T(1,128)S(1)} %get-tuple-element.38), channel_id=1, replica_groups={{0,9,16,25},{33,40,49,56},{64,73,80,89},{97,104,113,120},{128,137,144,1..., use_global_device_ids=true, to_apply=%region_5.6 | all-reduce | flops 128 | bytes 1024 | tf_op jit(solution)/shard_map/psum | solution.py:357
  193.3 21.1 %psum.47.lines_ref = f32[1,128]{1,0:T(1,128)S(1)} all-reduce(f32[1,128]{1,0:T(1,128)S(1)} %psum.46), channel_id=1, replica_groups={{0,33,64,97,128,161,192,225},{9,40,73,104,137,168,201,232},{16,49,80,11..., use_global_device_ids=true, to_apply=%region_6.7 | all-reduce | flops 128 | bytes 1024 | tf_op jit(solution)/shard_map/psum | solution.py:358
  214.4 1.4 shard_map.110
  215.8 2.1 collective-permute-start.9
  217.9 1.3 collective-permute-done.9
  219.3 0.6 broadcast_in_dim.8
  219.9 3.4 %all-to-all-start.1 = ((f32[4,4,1024]{2,1,0:T(4,128)}), f32[4,4,1024]{2,1,0:T(4,128)S(1)}, u32[]{:S(2)}, u32[]{:S(2)}) async-start(f32[4,4,1024]{2,1,0:T(4,128)} %broadcast_in_dim.8), calls=%async_computation.1 | async-start | bytes 131072 | tf_op jit(solution)/shard_map/all_to_all | solution.py:338
  223.4 0.9 reshape.79
  224.2 4.6 %all-to-all-done.1 = f32[4,4,1024]{2,1,0:T(4,128)S(1)} async-done(((f32[4,4,1024]{2,1,0:T(4,128)}), f32[4,4,1024]{2,1,0:T(4,128)S(1)}, u32[]{:S(2)}, u32[]{:S(2)}) %all-to-all-start.1) | async-done | bytes 65568 | tf_op jit(solution)/shard_map/all_to_all | solution.py:338
  228.9 0.6 mul.40
  (11 shorter events, 0.2 us)
Async XLA Ops:
  0.6 122.4 %copy-start = (f32[16]{0:T(128)S(1)}, f32[16]{0:T(128)}, u32[]{:S(2)}) copy-start(f32[16]{0:T(128)} %param.10) | copy-start | bytes 196
  1.8 21.7 %copy-start.3 = (f32[4,4,256]{2,1,0:T(4,128)S(1)}, f32[4,4,256]{2,1,0:T(4,128)}, u32[]{:S(2)}) copy-start(f32[4,4,256]{2,1,0:T(4,128)} %param.12) | copy-start | bytes 49156
  1.8 22.4 %copy-start.2 = (f32[128,4,256]{2,1,0:T(4,128)S(1)}, f32[128,4,256]{2,1,0:T(4,128)}, u32[]{:S(2)}) copy-start(f32[128,4,256]{2,1,0:T(4,128)} %param.14) | copy-start | bytes 1572868
  21.5 2.8 %copy-start.1 = (f32[4,16,4096]{2,1,0:T(8,128)}, f32[4,16,4096]{2,1,0:T(8,128)S(1)}, u32[]{:S(2)}) copy-start(f32[4,16,4096]{2,1,0:T(8,128)S(1)} %all_to_all.10) | copy-start | bytes 3145732
  21.5 7.5 %collective-permute-start = (f32[64,4096]{1,0:T(8,128)S(1)}, f32[64,4096]{1,0:T(8,128)}, u32[]{:S(2)}, u32[]{:S(2)}) collective-permute-start(f32[64,4096]{1,0:T(8,128)S(1)} %bitcast.15), channel_id=1, source_target_pairs={{0,1},{1,0},{2,3},{3,2},{4,5},{5,4},{6,7},{7,6},{8,9},{9,8},{10,11... | collective-permute-start | bytes 3145736 | tf_op jit(solution)/shard_map/ppermute | solution.py:342
  23.5 0.7 copy-start.4
  24.4 4.7 %collective-permute-start.1 = (f32[136,1024]{1,0:T(8,128)S(1)}, f32[136,1024]{1,0:T(8,128)S(1)}, u32[]{:S(2)}, u32[]{:S(2)}) collective-permute-start(f32[136,1024]{1,0:T(8,128)S(1)} %pad_maximum_fusion.stat_m), channel_id=1, source_target_pairs={{0,1},{1,0},{2,3},{3,2},{4,5},{5,4},{6,7},{7,6},{8,9},{9,8},{10,11... | collective-permute-start | bytes 1671176 | tf_op jit(solution)/shard_map/ppermute | solution.py:342
  27.0 1.4 copy-start.6
  28.3 0.7 copy-start.5
  104.0 2.1 copy-start.7
  104.0 3.1 %collective-permute-start.2 = (f32[16,128]{1,0:T(8,128)S(1)}, f32[16,128]{1,0:T(8,128)S(1)}, u32[]{:S(2)}, u32[]{:S(2)}) collective-permute-start(f32[16,128]{1,0:T(8,128)S(1)} %psum.43.sums_ref), channel_id=1, source_target_pairs={{0,1},{1,0},{2,3},{3,2},{4,5},{5,4},{6,7},{7,6},{8,9},{9,8},{10,11... | collective-permute-start | bytes 24584 | tf_op jit(solution)/shard_map/ppermute | solution.py:342
  119.1 7.4 %collective-permute-start.3 = (f32[8,2176]{1,0:T(8,128)S(1)}, f32[8,2176]{1,0:T(8,128)S(1)}, u32[]{:S(2)}, u32[]{:S(2)}) collective-permute-start(f32[8,2176]{1,0:T(8,128)S(1)} %get-tuple-element.25), channel_id=1, source_target_pairs={{9,16},{8,17},{16,9},{17,8},{25,33},{24,32},{33,25},{32,24},{40,49... | collective-permute-start | bytes 208904 | tf_op jit(solution)/shard_map/ppermute | solution.py:369
  121.0 6.1 %collective-permute-start.4 = (f32[8,2176]{1,0:T(8,128)S(1)}, f32[8,2176]{1,0:T(8,128)S(1)}, u32[]{:S(2)}, u32[]{:S(2)}) collective-permute-start(f32[8,2176]{1,0:T(8,128)S(1)} %get-tuple-element.26), channel_id=1, source_target_pairs={{0,9},{1,8},{9,0},{8,1},{16,25},{17,24},{25,16},{24,17},{33,40},{3... | collective-permute-start | bytes 208904 | tf_op jit(solution)/shard_map/ppermute | solution.py:369
  128.0 7.9 %collective-permute-start.5 = (f32[8,2176]{1,0:T(8,128)S(1)}, f32[8,2176]{1,0:T(8,128)S(1)}, u32[]{:S(2)}, u32[]{:S(2)}) collective-permute-start(f32[8,2176]{1,0:T(8,128)S(1)} %get-tuple-element.29), channel_id=1, source_target_pairs={{9,16},{8,17},{16,9},{17,8},{25,33},{24,32},{33,25},{32,24},{40,49... | collective-permute-start | bytes 208904 | tf_op jit(solution)/shard_map/ppermute | solution.py:369
  133.5 6.4 %collective-permute-start.6 = (f32[8,2176]{1,0:T(8,128)S(1)}, f32[8,2176]{1,0:T(8,128)S(1)}, u32[]{:S(2)}, u32[]{:S(2)}) collective-permute-start(f32[8,2176]{1,0:T(8,128)S(1)} %get-tuple-element.30), channel_id=1, source_target_pairs={{0,9},{1,8},{9,0},{8,1},{16,25},{17,24},{25,16},{24,17},{33,40},{3... | collective-permute-start | bytes 208904 | tf_op jit(solution)/shard_map/ppermute | solution.py:369
  173.9 7.4 %collective-permute-start.7 = (f32[8,2176]{1,0:T(8,128)S(1)}, f32[8,2176]{1,0:T(8,128)S(1)}, u32[]{:S(2)}, u32[]{:S(2)}) collective-permute-start(f32[8,2176]{1,0:T(8,128)S(1)} %get-tuple-element.36), channel_id=1, source_target_pairs={{9,16},{8,17},{16,9},{17,8},{25,33},{24,32},{33,25},{32,24},{40,49... | collective-permute-start | bytes 208904 | tf_op jit(solution)/shard_map/ppermute | solution.py:369
  177.6 6.4 %collective-permute-start.8 = (f32[8,2176]{1,0:T(8,128)S(1)}, f32[8,2176]{1,0:T(8,128)S(1)}, u32[]{:S(2)}, u32[]{:S(2)}) collective-permute-start(f32[8,2176]{1,0:T(8,128)S(1)} %get-tuple-element.37), channel_id=1, source_target_pairs={{0,9},{1,8},{9,0},{8,1},{16,25},{17,24},{25,16},{24,17},{33,40},{3... | collective-permute-start | bytes 208904 | tf_op jit(solution)/shard_map/ppermute | solution.py:369
  215.8 3.5 %collective-permute-start.9 = (f32[16,4096]{1,0:T(8,128)S(1)}, f32[16,4096]{1,0:T(8,128)S(1)}, u32[]{:S(2)}, u32[]{:S(2)}) collective-permute-start(f32[16,4096]{1,0:T(8,128)S(1)} %get-tuple-element.42), channel_id=1, source_target_pairs={{0,1},{1,0},{2,3},{3,2},{4,5},{5,4},{6,7},{7,6},{8,9},{9,8},{10,11... | collective-permute-start | bytes 786440 | tf_op jit(solution)/shard_map/ppermute | solution.py:342
  219.9 8.9 %all-to-all-start.1 = ((f32[4,4,1024]{2,1,0:T(4,128)}), f32[4,4,1024]{2,1,0:T(4,128)S(1)}, u32[]{:S(2)}, u32[]{:S(2)}) async-start(f32[4,4,1024]{2,1,0:T(4,128)} %broadcast_in_dim.8), calls=%async_computation.1 | async-start | bytes 131072 | tf_op jit(solution)/shard_map/all_to_all | solution.py:338
